TPU v7x, 32 devices: a whole 2x2x4 slice. The times are simulated.
32 devices in a mesh: tp: 4 (over z), fsdp: 8 (over y, x, core).
Axes of the slice: x: 2, y: 2, z: 4, core: 2. Of those that a mesh axis runs over, the one named last changes fastest.
Arguments:
- hidden: bfloat16 [32, 256, 3072], P('fsdp')
- positions: int32 [32, 256], P('fsdp')
- grad_layer: bfloat16 [32, 256, 3072], P('fsdp')
- ln_weight: bfloat16 [3072], P('fsdp')
- w_query: bfloat16 [3072, 3072], P('fsdp', 'tp')
- w_key: bfloat16 [3072, 1024], P('fsdp', 'tp')
- w_value: bfloat16 [3072, 1024], P('fsdp', 'tp')
- w_out: bfloat16 [3072, 3072], P('tp', 'fsdp')
- w_gate: bfloat16 [3072, 8192], P('fsdp', 'tp')
- w_up: bfloat16 [3072, 8192], P('fsdp', 'tp')
- w_down: bfloat16 [8192, 3072], P('tp', 'fsdp')
- q_norm: bfloat16 [24, 128], P('tp', 'fsdp')
- k_norm: bfloat16 [8, 128], P('tp', 'fsdp')
Outputs:
- output 1: bfloat16 [32, 256, 3072], P('fsdp')
- output 2: bfloat16 [32, 256, 3072], P('fsdp')
- output 3: float32 [3072], P('fsdp')
- output 4: bfloat16 [3072, 3072], P('fsdp', 'tp')
- output 5: bfloat16 [3072, 1024], P('fsdp', 'tp')
- output 6: bfloat16 [3072, 1024], P('fsdp', 'tp')
- output 7: bfloat16 [3072, 3072], P('tp', 'fsdp')
- output 8: bfloat16 [3072, 8192], P('fsdp', 'tp')
- output 9: bfloat16 [3072, 8192], P('fsdp', 'tp')
- output 10: bfloat16 [8192, 3072], P('tp', 'fsdp')
- output 11: float32 [24, 128], P('tp', 'fsdp')
- output 12: float32 [8, 128], P('tp', 'fsdp')
All inputs are finite; a program needn't handle non-finite values.
Results may differ from a plain program's by a relative error of at most 0.02.
Values are sent between devices in bfloat16 or wider.
A program may use at most 1 GiB of HBM per device.

v0:
```python
import jax
import jax.numpy as jnp
from jax import lax
from jax.sharding import PartitionSpec as P

LN_EPS = 1e-5
ROPE_BASE = 10000.0


def matmul_f32(form, left, right):
    return jnp.einsum(form, left, right, preferred_element_type=jnp.float32)


def norm_stats(tensor):
    centered = tensor - jnp.mean(tensor, axis=-1, keepdims=True)
    inv_std = lax.rsqrt(jnp.mean(centered * centered, axis=-1, keepdims=True) + LN_EPS)
    return centered * inv_std, inv_std


def norm_backward(grad_hat, x_hat, inv_std):
    mean_grad = jnp.mean(grad_hat, axis=-1, keepdims=True)
    mean_proj = jnp.mean(grad_hat * x_hat, axis=-1, keepdims=True)
    return inv_std * (grad_hat - mean_grad - x_hat * mean_proj)


def rotary(tensor, cosine, sine):
    pairs = tensor.reshape(tensor.shape[:-1] + (tensor.shape[-1] // 2, 2))
    first = pairs[..., 0]
    second = pairs[..., 1]
    turned = jnp.stack([first * cosine - second * sine, second * cosine + first * sine], axis=-1)
    return turned.reshape(tensor.shape)


def gather_first(weight):
    return lax.all_gather(weight, 'fsdp', axis=0, tiled=True)


def gather_second(weight):
    return lax.all_gather(weight, 'fsdp', axis=1, tiled=True)


def scatter_first(grad):
    return lax.psum_scatter(grad, 'fsdp', scatter_dimension=0, tiled=True)


def scatter_second(grad):
    return lax.psum_scatter(grad, 'fsdp', scatter_dimension=1, tiled=True)


def gather_weights(shards):
    ln_weight, w_query, w_key, w_value, w_out, w_gate, w_up, w_down, q_norm, k_norm = shards
    return (gather_first(ln_weight), gather_first(w_query), gather_first(w_key), gather_first(w_value), gather_second(w_out),
            gather_first(w_gate), gather_first(w_up), gather_second(w_down), gather_second(q_norm), gather_second(k_norm))


def layer_forward(hidden, positions, full):
    ln_full, wq_full, wk_full, wv_full, wo_full, wg_full, wu_full, wd_full, qn_full, kn_full = full
    batch, seq_len, _ = hidden.shape
    heads, head_dim = qn_full.shape
    kv_heads = kn_full.shape[0]
    group = heads // kv_heads
    x_hat, inv_std = norm_stats(hidden.astype(jnp.float32))
    normed = (x_hat * ln_full.astype(jnp.float32)).astype(jnp.bfloat16)
    query = matmul_f32('btd,de->bte', normed, wq_full).astype(jnp.bfloat16).reshape(batch, seq_len, heads, head_dim)
    key_proj = matmul_f32('btd,de->bte', normed, wk_full).astype(jnp.bfloat16).reshape(batch, seq_len, kv_heads, head_dim)
    value_heads = matmul_f32('btd,de->bte', normed, wv_full).astype(jnp.bfloat16).reshape(batch, seq_len, kv_heads, head_dim)
    inv_freq = ROPE_BASE ** (-jnp.arange(0, head_dim, 2, dtype=jnp.float32) / head_dim)
    angles = positions.astype(jnp.float32)[:, :, None, None] * inv_freq
    cosine = jnp.cos(angles)
    sine = jnp.sin(angles)
    q_hat, q_inv = norm_stats(query.astype(jnp.float32))
    k_hat, k_inv = norm_stats(key_proj.astype(jnp.float32))
    q_rot = rotary(q_hat * qn_full.astype(jnp.float32), cosine, sine).astype(jnp.bfloat16).reshape(batch, seq_len, kv_heads, group, head_dim)
    k_rot = rotary(k_hat * kn_full.astype(jnp.float32), cosine, sine).astype(jnp.bfloat16)
    scores = matmul_f32('bqkgd,bskd->bkgqs', q_rot, k_rot) * head_dim ** -0.5
    causal = lax.broadcasted_iota(jnp.int32, (seq_len, seq_len), 0) >= lax.broadcasted_iota(jnp.int32, (seq_len, seq_len), 1)
    attn_probs = jax.nn.softmax(jnp.where(causal, scores, -1e30), axis=-1)
    probs_bf = attn_probs.astype(jnp.bfloat16)
    attn_out = matmul_f32('bkgqs,bskd->bqkgd', probs_bf, value_heads).astype(jnp.bfloat16).reshape(batch, seq_len, heads * head_dim)
    attn_part = matmul_f32('bte,ed->btd', attn_out, wo_full)
    gate = matmul_f32('btd,df->btf', normed, wg_full).astype(jnp.bfloat16)
    up_proj = matmul_f32('btd,df->btf', normed, wu_full).astype(jnp.bfloat16)
    gated_act = (jax.nn.silu(gate.astype(jnp.float32)) * up_proj.astype(jnp.float32)).astype(jnp.bfloat16)
    mlp_part = matmul_f32('btf,fd->btd', gated_act, wd_full)
    saved = (x_hat, inv_std, normed, value_heads, cosine, sine, q_hat, q_inv, k_hat, k_inv, q_rot, k_rot, attn_probs, probs_bf, attn_out, gate, up_proj, gated_act)
    return attn_part, mlp_part, saved


def layer_backward(grad_layer, saved, full):
    _, wq_full, wk_full, wv_full, wo_full, wg_full, wu_full, wd_full, qn_full, kn_full = full
    x_hat, inv_std, normed, value_heads, cosine, sine, q_hat, q_inv, k_hat, k_inv, q_rot, k_rot, attn_probs, probs_bf, attn_out, gate, up_proj, gated_act = saved
    batch, seq_len, kv_heads, group, head_dim = q_rot.shape
    heads = kv_heads * group
    grad_act = matmul_f32('btd,fd->btf', grad_layer, wd_full)
    grad_wdown = matmul_f32('btf,btd->fd', gated_act, grad_layer)
    gate_f32 = gate.astype(jnp.float32)
    sigma = jax.nn.sigmoid(gate_f32)
    grad_gate = (grad_act * up_proj.astype(jnp.float32) * sigma * (1.0 + gate_f32 * (1.0 - sigma))).astype(jnp.bfloat16)
    grad_up = (grad_act * gate_f32 * sigma).astype(jnp.bfloat16)
    grad_wgate = matmul_f32('btd,btf->df', normed, grad_gate)
    grad_wup = matmul_f32('btd,btf->df', normed, grad_up)
    mlp_dh = matmul_f32('btf,df->btd', grad_gate, wg_full) + matmul_f32('btf,df->btd', grad_up, wu_full)
    grad_attn = matmul_f32('btd,ed->bte', grad_layer, wo_full).astype(jnp.bfloat16).reshape(batch, seq_len, kv_heads, group, head_dim)
    grad_wout = matmul_f32('bte,btd->ed', attn_out, grad_layer)
    grad_probs = matmul_f32('bqkgd,bskd->bkgqs', grad_attn, value_heads)
    grad_vheads = matmul_f32('bkgqs,bqkgd->bskd', probs_bf, grad_attn).astype(jnp.bfloat16)
    grad_scores = (attn_probs * (grad_probs - jnp.sum(grad_probs * attn_probs, axis=-1, keepdims=True)) * head_dim ** -0.5).astype(jnp.bfloat16)
    grad_qrot = matmul_f32('bkgqs,bskd->bqkgd', grad_scores, k_rot).reshape(batch, seq_len, heads, head_dim)
    grad_krot = matmul_f32('bkgqs,bqkgd->bskd', grad_scores, q_rot)
    grad_qscaled = rotary(grad_qrot, cosine, -sine)
    grad_kscaled = rotary(grad_krot, cosine, -sine)
    grad_qnorm = jnp.sum(grad_qscaled * q_hat, axis=(0, 1))
    grad_knorm = jnp.sum(grad_kscaled * k_hat, axis=(0, 1))
    grad_query = norm_backward(grad_qscaled * qn_full.astype(jnp.float32), q_hat, q_inv).astype(jnp.bfloat16).reshape(batch, seq_len, heads * head_dim)
    grad_key = norm_backward(grad_kscaled * kn_full.astype(jnp.float32), k_hat, k_inv).astype(jnp.bfloat16).reshape(batch, seq_len, kv_heads * head_dim)
    grad_value = grad_vheads.reshape(batch, seq_len, kv_heads * head_dim)
    grad_wquery = matmul_f32('btd,bte->de', normed, grad_query)
    grad_wkey = matmul_f32('btd,bte->de', normed, grad_key)
    grad_wvalue = matmul_f32('btd,bte->de', normed, grad_value)
    attn_dh = (matmul_f32('bte,de->btd', grad_query, wq_full) + matmul_f32('bte,de->btd', grad_key, wk_full)
               + matmul_f32('bte,de->btd', grad_value, wv_full))
    weight_grads = (grad_wquery, grad_wkey, grad_wvalue, grad_wout, grad_wgate, grad_wup, grad_wdown, grad_qnorm, grad_knorm)
    return attn_dh, mlp_dh, weight_grads


def solution(mesh):
    act_spec = P('fsdp', None, None)
    col_spec = P('fsdp', 'tp')
    row_spec = P('tp', 'fsdp')
    weight_specs = (P('fsdp'), col_spec, col_spec, col_spec, row_spec, col_spec, col_spec, row_spec, row_spec, row_spec)
    in_specs = (act_spec, P('fsdp', None), act_spec) + weight_specs
    out_specs = (act_spec, act_spec) + weight_specs

    def device_step(hidden, positions, grad_layer, ln_weight, w_query, w_key, w_value, w_out, w_gate, w_up, w_down, q_norm, k_norm):
        shards = (ln_weight, w_query, w_key, w_value, w_out, w_gate, w_up, w_down, q_norm, k_norm)
        full = gather_weights(shards)
        attn_part, mlp_part, saved = layer_forward(hidden, positions, full)
        attn_sum = lax.psum(attn_part.astype(jnp.bfloat16), 'tp')
        mlp_sum = lax.psum(mlp_part.astype(jnp.bfloat16), 'tp')
        layer_out = (hidden.astype(jnp.float32) + attn_sum.astype(jnp.float32) + mlp_sum.astype(jnp.float32)).astype(jnp.bfloat16)
        held = lax.optimization_barrier((shards, layer_out))
        full_again = gather_weights(held[0])
        attn_dh, mlp_dh, weight_grads = layer_backward(grad_layer, saved, full_again)
        attn_dh_sum = lax.psum(attn_dh.astype(jnp.bfloat16), 'tp')
        mlp_dh_sum = lax.psum(mlp_dh.astype(jnp.bfloat16), 'tp')
        x_hat = saved[0]
        inv_std = saved[1]
        grad_normed = (attn_dh_sum.astype(jnp.float32) + mlp_dh_sum.astype(jnp.float32)).astype(jnp.bfloat16).astype(jnp.float32)
        grad_ln = jnp.sum(grad_normed * x_hat, axis=(0, 1))
        grad_hidden = (grad_layer.astype(jnp.float32) + norm_backward(grad_normed * full_again[0].astype(jnp.float32), x_hat, inv_std)).astype(jnp.bfloat16)
        grad_wquery, grad_wkey, grad_wvalue, grad_wout, grad_wgate, grad_wup, grad_wdown, grad_qnorm, grad_knorm = weight_grads
        return (held[1], grad_hidden, scatter_first(grad_ln),
                scatter_first(grad_wquery.astype(jnp.bfloat16)), scatter_first(grad_wkey.astype(jnp.bfloat16)),
                scatter_first(grad_wvalue.astype(jnp.bfloat16)), scatter_second(grad_wout.astype(jnp.bfloat16)),
                scatter_first(grad_wgate.astype(jnp.bfloat16)), scatter_first(grad_wup.astype(jnp.bfloat16)),
                scatter_second(grad_wdown.astype(jnp.bfloat16)), scatter_second(grad_qnorm), scatter_second(grad_knorm))

    return jax.shard_map(device_step, mesh=mesh, in_specs=in_specs, out_specs=out_specs, check_vma=False)
```

profile of v0, /device:TPU:0, one launch (start us, length us, event | category | flops | bytes accessed | tf_op | source)
XLA Modules:
  0.0 2188.3 jit_solution(14057561812515531272)
XLA Ops:
  14.2 10.4 all-gather
  24.6 9.0 all-gather.2
  37.9 7.7 all-gather.1
  73.6 34.4 %all-gather.25.cloned.1.call-done = bf16[3072,768]{1,0:T(8,128)(2,1)} async-done(((bf16[384,768]{1,0:T(8,128)(2,1)}), bf16[3072,768]{1,0:T(8,128)(2,1)}) %all-gather.25.cloned.1.call-update) | async-done | bytes 4718608 | tf_op jit(solution)/shard_map/all_gather | solution.py:35
  108.0 8.8 fusion.78
  140.7 8.7 all-gather.27.cloned.1.call-done
  149.4 9.3 convolution_convert_fusion
  158.7 64.4 %all-gather.29.cloned.1.call-done = bf16[3072,2048]{1,0:T(8,128)(2,1)} async-done(((bf16[384,2048]{1,0:T(8,128)(2,1)}), bf16[3072,2048]{1,0:T(8,128)(2,1)}) %all-gather.29.cloned.1.call-update) | async-done | bytes 12582928 | tf_op jit(solution)/shard_map/all_gather | solution.py:35
  223.2 19.6 fusion.59
  242.7 54.2 %all-gather.31.cloned.1.call-done = bf16[3072,2048]{1,0:T(8,128)(2,1)} async-done(((bf16[384,2048]{1,0:T(8,128)(2,1)}), bf16[3072,2048]{1,0:T(8,128)(2,1)}) %all-gather.31.cloned.1.call-update) | async-done | bytes 12582928 | tf_op jit(solution)/shard_map/all_gather | solution.py:35
  296.9 19.4 fusion.62
  316.3 56.9 %all-gather.33.cloned.1.call-done = bf16[2048,3072]{1,0:T(8,128)(2,1)} async-done(((bf16[2048,384]{1,0:T(8,128)(2,1)}), bf16[2048,3072]{1,0:T(8,128)(2,1)}) %all-gather.33.cloned.1.call-update) | async-done | bytes 12582928 | tf_op jit(solution)/shard_map/all_gather | solution.py:39
  373.3 21.4 fusion.46
  394.7 426.2 %all-reduce.8.cloned.1.call-done = (bf16[4,256,3072]{2,1,0:T(8,128)(2,1)}, bf16[4,256,3072]{2,1,0:T(8,128)(2,1)}) async-done(((bf16[4,256,3072]{2,1,0:T(8,128)(2,1)}, bf16[4,256,3072]{2,1,0:T(8,128)(2,1)}), (bf16[4,256,3072]{2,1,0:T(8,128)(2,1)}, bf16[4,256,3072]{2,1,0:T(8,128)(2,1)})) %all-reduce.8.cloned.1.call-update) | async-done | bytes 12582928 | tf_op jit(solution)/shard_map/psum | solution.py:139
  820.9 13.6 fusion.18
  838.4 9.8 bitcast_convert_fusion.3
  854.8 23.8 %bitcast_convert_fusion = bf16[2048,3072]{1,0:T(8,128)(2,1)} fusion(bf16[4,256,3072]{2,1,0:T(8,128)(2,1)} %param.15, bf16[4,256,2048]{2,1,0:T(8,128)(2,1)} %fusion.62, bf16[4,256,2048]{2,1,0:T(8,128)(2,1)} %fusion.59), kind=kOutput, calls=%fused_computation.2 | convolution fusion | flops 12907970560 | bytes 27262976 | tf_op jit(solution)/shard_map/btf,btd->fd/dot_general | solution.py:11
  878.6 16.7 copy.325
  913.2 9.0 all-gather.4
  922.4 9.0 all-gather.3
  932.9 8.8 fusion.81
  946.7 11.0 fusion.97
  964.1 10.0 fusion.74
  995.2 9.5 multiply_reduce_fusion
  1010.3 8.0 fusion.85
  1018.3 10.8 fusion.50
  1029.1 12.6 add_convert_fusion.2
  1045.0 24.4 %fusion.34 = (bf16[4,256,2048]{2,1,0:T(8,128)(2,1)}, f32[2048,4,256]{0,2,1:T(8,128)}) fusion(bf16[4,256,2048]{2,1,0:T(8,128)(2,1)} %fusion.62, bf16[4,256,2048]{2,1,0:T(8,128)(2,1)} %fusion.59, bf16[4,256,3072]{2,1,0:T(8,128)(2,1)} %param.15, bf16[2048,3072]{1,0:T(8,128)(2,1)} %all-gather.43.cloned.1.call-done), kind=kOutput, calls=%fused_computation.53 | convolution fusion | flops 12910067712 | bytes 39845888 | tf_op jit(solution)/shard_map/btd,fd->btf/dot_general | solution.py:11
  1069.4 49.3 %all-gather.47.cloned.1.call-done = bf16[3072,2048]{1,0:T(8,128)(2,1)} async-done(((bf16[384,2048]{1,0:T(8,128)(2,1)}), bf16[3072,2048]{1,0:T(8,128)(2,1)}) %all-gather.47.cloned.1.call-update) | async-done | bytes 12582928 | tf_op jit(solution)/shard_map/all_gather | solution.py:35
  1118.8 22.2 %fusion.19 = f32[4,256,3072]{2,1,0:T(8,128)} fusion(bf16[3072,2048]{1,0:T(8,128)(2,1)} %all-gather.47.cloned.1.call-done, bf16[4,256,2048]{2,1,0:T(8,128)(2,1)} %fusion.59, f32[2048,4,256]{0,2,1:T(8,128)} %get-tuple-element.68), kind=kOutput, calls=%fused_computation.31 | convolution fusion | flops 12899581952 | bytes 37748736 | tf_op jit(solution)/shard_map/btf,df->btd/dot_general | solution.py:11
  1141.0 51.5 %all-gather.45.cloned.1.call-done = bf16[3072,2048]{1,0:T(8,128)(2,1)} async-done(((bf16[384,2048]{1,0:T(8,128)(2,1)}), bf16[3072,2048]{1,0:T(8,128)(2,1)}) %all-gather.45.cloned.1.call-update) | async-done | bytes 12582928 | tf_op jit(solution)/shard_map/all_gather | solution.py:35
  1192.5 20.9 add_convert_fusion.1
  1214.2 7.3 fusion.57
  1229.1 9.4 bitcast_convert_fusion.4
  1238.7 22.9 %bitcast_convert_fusion.1 = bf16[3072,2048]{1,0:T(8,128)(2,1)} fusion(bf16[4,256,2048]{2,1,0:T(8,128)(2,1)} %fusion.59, f32[2048,4,256]{0,2,1:T(8,128)} %get-tuple-element.68, bf16[4,256,3072]{2,1,0:T(8,128)(2,1)} %param.13, f32[3072]{0:T(1024)S(1)} %bitcast.321, f32[4,256]{1,0:T(4,128)S(1)} %copy-done.39, f32[4,256]{1,0:T(4,128)S(1)} %copy-done.37), kind=kOutput, calls=%fused_computation.3 | convolution fusion | flops 12921602048 | bytes 31477760 | tf_op jit(solution)/shard_map/btd,btf->df/dot_general | solution.py:11
  1261.8 22.3 %bitcast_convert_fusion.2 = bf16[3072,2048]{1,0:T(8,128)(2,1)} fusion(bf16[4,256,2048]{2,1,0:T(8,128)(2,1)} %get-tuple-element.67, bf16[4,256,3072]{2,1,0:T(8,128)(2,1)} %param.13, f32[3072]{0:T(1024)S(1)} %bitcast.322, f32[4,256]{1,0:T(4,128)S(1)} %copy-done.39, f32[4,256]{1,0:T(4,128)S(1)} %copy-done.37), kind=kOutput, calls=%fused_computation.4 | convolution fusion | flops 12906921984 | bytes 23089152 | tf_op jit(solution)/shard_map/btd,btf->df/dot_general | solution.py:11
  1288.2 9.4 all-gather.5
  1297.6 47.8 %reduce-scatter.30.cloned.1.call-done = bf16[384,2048]{1,0:T(8,128)(2,1)} async-done(((bf16[3072,2048]{1,0:T(8,128)(2,1)}), bf16[384,2048]{1,0:T(8,128)(2,1)}) %reduce-scatter.30.cloned.1.call-update) | async-done | bytes 1572880
  1348.0 33.8 %reduce-scatter.34.cloned.1.call-done = f32[16,2]{1,0:T(8,128)} async-done(((f32[128,2]{1,0:T(8,128)}), f32[16,2]{1,0:T(8,128)}) %reduce-scatter.34.cloned.1.call-update) | async-done | bytes 144
  1383.1 35.2 %reduce-scatter.32.cloned.1.call-done = f32[16,6]{1,0:T(8,128)} async-done(((f32[128,6]{1,0:T(8,128)}), f32[16,6]{1,0:T(8,128)}) %reduce-scatter.32.cloned.1.call-update) | async-done | bytes 400
  1419.7 427.8 %all-reduce.6.cloned.1.call-done = (bf16[4,256,3072]{2,1,0:T(8,128)(2,1)}, bf16[4,256,3072]{2,1,0:T(8,128)(2,1)}) async-done(((bf16[4,256,3072]{2,1,0:T(8,128)(2,1)}, bf16[4,256,3072]{2,1,0:T(8,128)(2,1)}), (bf16[4,256,3072]{2,1,0:T(8,128)(2,1)}, bf16[4,256,3072]{2,1,0:T(8,128)(2,1)})) %all-reduce.6.cloned.1.call-update) | async-done | bytes 12582928 | tf_op jit(solution)/shard_map/psum | solution.py:145
  1847.5 12.0 fusion.16
  1859.5 24.2 %all-reduce = f32[3072]{0:T(1024)S(1)} all-reduce(f32[3072]{0:T(1024)S(1)} %get-tuple-element.34), channel_id=2, replica_groups=mesh['tp'=4,'fsdp'=8] {'fsdp'}, use_global_device_ids=true, to_apply=%region_20.21.clone | all-reduce | flops 3072 | bytes 24576
  1884.3 12.0 fusion.13
  1896.4 34.7 %reduce-scatter.22.cloned.1.call-done = bf16[384,256]{1,0:T(8,128)(2,1)} async-done(((bf16[3072,256]{1,0:T(8,128)(2,1)}), bf16[384,256]{1,0:T(8,128)(2,1)}) %reduce-scatter.22.cloned.1.call-update) | async-done | bytes 196624 | tf_op jit(solution)/shard_map/reduce_scatter | solution.py:43
  1931.1 57.9 %reduce-scatter.18.cloned.1.call-done = bf16[384,768]{1,0:T(8,128)(2,1)} async-done(((bf16[3072,768]{1,0:T(8,128)(2,1)}), bf16[384,768]{1,0:T(8,128)(2,1)}) %reduce-scatter.18.cloned.1.call-update) | async-done | bytes 589840 | tf_op jit(solution)/shard_map/reduce_scatter | solution.py:43
  1988.9 96.2 %reduce-scatter.26.cloned.1.call-done = bf16[384,2048]{1,0:T(8,128)(2,1)} async-done(((bf16[3072,2048]{1,0:T(8,128)(2,1)}), bf16[384,2048]{1,0:T(8,128)(2,1)}) %reduce-scatter.26.cloned.1.call-update) | async-done | bytes 1572880 | tf_op jit(solution)/shard_map/reduce_scatter | solution.py:43
  2085.2 96.4 %reduce-scatter.24.cloned.1.call-done = bf16[384,2048]{1,0:T(8,128)(2,1)} async-done(((bf16[3072,2048]{1,0:T(8,128)(2,1)}), bf16[384,2048]{1,0:T(8,128)(2,1)}) %reduce-scatter.24.cloned.1.call-update) | async-done | bytes 1572880 | tf_op jit(solution)/shard_map/reduce_scatter | solution.py:43
  (258 shorter events, 151.7 us)
Async XLA Ops:
  7.2 7.0 copy-start.45
  7.2 17.4 copy-start.42
  7.2 27.9 %copy-start.44 = (s32[4,256]{1,0:T(4,128)S(1)}, s32[4,256]{1,0:T(4,128)}, u32[]{:S(2)}) copy-start(s32[4,256]{1,0:T(4,128)} %param.14) | copy-start | bytes 12292
  7.2 30.7 %copy-start.47 = (bf16[2,16]{1,0:T(2,128)(2,1)S(1)}, bf16[2,16]{1,0:T(2,128)(2,1)}, u32[]{:S(2)}) copy-start(bf16[2,16]{1,0:T(2,128)(2,1)} %param.25) | copy-start | bytes 196
  7.2 47.0 %all-gather.23.cloned.1.call-start = ((), (), s32[]{:S(2)}) async-start(), calls=%async_computation.10 | async-start | bytes 1769472 | tf_op jit(solution)/shard_map/all_gather | solution.py:35
  9.0 58.3 %all-gather.21.cloned.1.call-start = ((), (), s32[]{:S(2)}) async-start(), calls=%async_computation.9 | async-start | bytes 1769472 | tf_op jit(solution)/shard_map/all_gather | solution.py:35
  10.9 97.1 %all-gather.25.cloned.1.call-start = ((), (), s32[]{:S(2)}) async-start(), calls=%async_computation.11 | async-start | bytes 5308416 | tf_op jit(solution)/shard_map/all_gather | solution.py:35
  11.6 137.8 %all-gather.27.cloned.1.call-start = ((), (), s32[]{:S(2)}) async-start(), calls=%async_computation.12 | async-start | bytes 5308416 | tf_op jit(solution)/shard_map/all_gather | solution.py:39
  12.2 211.0 %all-gather.29.cloned.1.call-start = ((), (), s32[]{:S(2)}) async-start(), calls=%async_computation.13 | async-start | bytes 14155776 | tf_op jit(solution)/shard_map/all_gather | solution.py:35
  12.8 284.2 %all-gather.31.cloned.1.call-start = ((), (), s32[]{:S(2)}) async-start(), calls=%async_computation.14 | async-start | bytes 14155776 | tf_op jit(solution)/shard_map/all_gather | solution.py:35
  13.3 359.9 %all-gather.33.cloned.1.call-start = ((), (), s32[]{:S(2)}) async-start(), calls=%async_computation.15 | async-start | bytes 14155776 | tf_op jit(solution)/shard_map/all_gather | solution.py:39
  14.1 806.9 %all-reduce.8.cloned.1.call-start = ((), (), s32[]{:S(2)}) async-start(), calls=%async_computation.33 | async-start | bytes 25165824 | tf_op jit(solution)/shard_map/psum | solution.py:139
  24.6 272.3 %copy-start.40 = (f32[8,1,384]{2,1,0:T(1,128)}, f32[8,1,384]{2,1,0:T(1,128)S(1)}, u32[]{:S(2)}) copy-start(f32[8,1,384]{2,1,0:T(1,128)S(1)} %convert_element_type.256) | copy-start | bytes 36868
  36.9 25.2 %copy-start.7 = (f32[4,256,64]{1,2,0:T(8,128)}, f32[4,256,64]{1,2,0:T(8,128)S(1)}, u32[]{:S(2)}) copy-start(f32[4,256,64]{1,2,0:T(8,128)S(1)} %get-tuple-element.62) | copy-start | bytes 786436
  37.0 93.3 %copy-start.10 = (f32[4,256,64]{1,0,2:T(4,128)}, f32[4,256,64]{1,0,2:T(4,128)S(1)}, u32[]{:S(2)}) copy-start(f32[4,256,64]{1,0,2:T(4,128)S(1)} %copy.244) | copy-start | bytes 786436
  49.6 247.3 %copy-start.36 = (f32[4,256]{1,0:T(4,128)}, f32[4,256]{1,0:T(4,128)S(1)}, u32[]{:S(2)}) copy-start(f32[4,256]{1,0:T(4,128)S(1)} %broadcast_multiply_fusion.7) | copy-start | bytes 12292
  54.2 242.7 %copy-start.38 = (f32[4,256]{1,0:T(4,128)}, f32[4,256]{1,0:T(4,128)S(1)}, u32[]{:S(2)}) copy-start(f32[4,256]{1,0:T(4,128)S(1)} %add_rsqrt_fusion.2) | copy-start | bytes 12292
  59.5 14.1 copy-start.6
  60.2 13.5 copy-start.4
  116.8 5.7 copy-start
  122.5 5.4 copy-start.2
  124.8 5.5 copy-start.18
  394.7 538.3 %all-gather.35.cloned.1.call-start = ((), (), s32[]{:S(2)}) async-start(), calls=%async_computation.16 | async-start | bytes 5308416 | tf_op jit(solution)/shard_map/all_gather | solution.py:39
  834.5 175.7 %all-gather.39.cloned.1.call-start = ((), (), s32[]{:S(2)}) async-start(), calls=%async_computation.18 | async-start | bytes 1769472 | tf_op jit(solution)/shard_map/all_gather | solution.py:35
  835.1 183.1 %all-gather.37.cloned.1.call-start = ((), (), s32[]{:S(2)}) async-start(), calls=%async_computation.17 | async-start | bytes 5308416 | tf_op jit(solution)/shard_map/all_gather | solution.py:35
  835.9 193.2 %all-gather.41.cloned.1.call-start = ((), (), s32[]{:S(2)}) async-start(), calls=%async_computation.19 | async-start | bytes 1769472 | tf_op jit(solution)/shard_map/all_gather | solution.py:35
  836.4 208.6 %all-gather.43.cloned.1.call-start = ((), (), s32[]{:S(2)}) async-start(), calls=%async_computation.20 | async-start | bytes 14155776 | tf_op jit(solution)/shard_map/all_gather | solution.py:39
  837.2 281.6 %all-gather.47.cloned.1.call-start = ((), (), s32[]{:S(2)}) async-start(), calls=%async_computation.22 | async-start | bytes 14155776 | tf_op jit(solution)/shard_map/all_gather | solution.py:35
  837.8 354.8 %all-gather.45.cloned.1.call-start = ((), (), s32[]{:S(2)}) async-start(), calls=%async_computation.21 | async-start | bytes 14155776 | tf_op jit(solution)/shard_map/all_gather | solution.py:35
  838.3 447.7 %reduce-scatter.28.cloned.1.call-start = ((), (), s32[]{:S(2)}) async-start(), calls=%async_computation.28 | async-start | bytes 5308416
  854.8 490.6 %reduce-scatter.30.cloned.1.call-start = ((), (), s32[]{:S(2)}) async-start(), calls=%async_computation.29 | async-start | bytes 14155776
  895.4 5.8 copy-start.29
  895.4 486.4 %reduce-scatter.34.cloned.1.call-start = ((), (), s32[]{:S(2)}) async-start(), calls=%async_computation.31 | async-start | bytes 73728
  910.6 11.8 copy-start.43
  932.9 10.0 copy-start.24
  946.7 13.0 copy-start.8
  946.7 13.6 copy-start.5
  985.7 9.4 copy-start.1
  995.1 423.2 %reduce-scatter.32.cloned.1.call-start = ((), (), s32[]{:S(2)}) async-start(), calls=%async_computation.30 | async-start | bytes 73728
  995.2 9.5 copy-start.14
  1004.7 5.6 copy-start.12
  1010.2 837.3 %all-reduce.6.cloned.1.call-start = ((), (), s32[]{:S(2)}) async-start(), calls=%async_computation.32 | async-start | bytes 25165824 | tf_op jit(solution)/shard_map/psum | solution.py:145
  1010.3 8.0 copy-start.15
  1213.5 682.9 %reduce-scatter.20.cloned.1.call-start = ((), (), s32[]{:S(2)}) async-start(), calls=%async_computation.24 | async-start | bytes 1769472 | tf_op jit(solution)/shard_map/reduce_scatter | solution.py:43
  1221.5 709.6 %reduce-scatter.22.cloned.1.call-start = ((), (), s32[]{:S(2)}) async-start(), calls=%async_computation.25 | async-start | bytes 1769472 | tf_op jit(solution)/shard_map/reduce_scatter | solution.py:43
  1229.1 759.8 %reduce-scatter.18.cloned.1.call-start = ((), (), s32[]{:S(2)}) async-start(), calls=%async_computation.23 | async-start | bytes 5308416 | tf_op jit(solution)/shard_map/reduce_scatter | solution.py:43
  1238.6 846.6 %reduce-scatter.26.cloned.1.call-start = ((), (), s32[]{:S(2)}) async-start(), calls=%async_computation.27 | async-start | bytes 14155776 | tf_op jit(solution)/shard_map/reduce_scatter | solution.py:43
  1261.6 920.0 %reduce-scatter.24.cloned.1.call-start = ((), (), s32[]{:S(2)}) async-start(), calls=%async_computation.26 | async-start | bytes 14155776 | tf_op jit(solution)/shard_map/reduce_scatter | solution.py:43
  (29 other events, 71.3 us)
Sparse Core Ops, SparseCore 0:
  10.5 28.5 all-gather.22
  41.5 25.7 all-gather.20
  69.2 38.7 all-gather.24
  109.7 39.6 all-gather.26
  151.1 71.9 all-gather.28
  224.9 71.9 all-gather.30
  298.8 74.4 all-gather.32
  394.8 426.1 all-reduce.7
  834.6 38.5 all-gather.34
  875.0 25.5 all-gather.38
  902.5 38.8 all-gather.36
  943.1 25.5 all-gather.40
  970.5 74.4 all-gather.42
  1046.8 71.9 all-gather.46
  1120.5 71.9 all-gather.44
  1195.8 53.7 reduce-scatter.27
  1253.0 92.3 reduce-scatter.29
  1348.2 33.5 reduce-scatter.33
  1384.8 33.5 reduce-scatter.31
  1421.4 426.1 all-reduce.5
  1851.4 37.3 reduce-scatter.19
  1892.7 38.3 reduce-scatter.21
  1935.1 53.7 reduce-scatter.17
  1992.8 92.2 reduce-scatter.25
  2089.2 92.2 reduce-scatter.23
where the time goes:
time: 2190 us
  waiting for transfers between devices  1590 us (73%)
  matrix products  338 us (15%)
  local copies, waits for them, and re-layouts  85.9 us (4%)
  other arithmetic  79.2 us (4%)
  blocking collectives  78.7 us (4%)
    psum x1, waiting for transfers between devices, device_step(): mlp_dh_sum = lax.psum(mlp_dh.astype(jnp.bfloat16), 'tp')  428 us
    psum x1, waiting for transfers between devices, device_step(): mlp_sum = lax.psum(mlp_part.astype(jnp.bfloat16), 'tp')  426 us
    dot_general x26, matrix products, matmul_f32(): return jnp.einsum(form, left, right, preferred_element_type=jnp.float32)  333 us
    reduce_scatter x5, waiting for transfers between devices, scatter_first(): return lax.psum_scatter(grad, 'fsdp', scatter_dimension=0, tiled=True)  285 us
    all_gather x10, waiting for transfers between devices, gather_first(): return lax.all_gather(weight, 'fsdp', axis=0, tiled=True)  257 us
    unnamed x29, waiting for transfers between devices  124 us
    all_gather x4, waiting for transfers between devices, gather_second(): return lax.all_gather(weight, 'fsdp', axis=1, tiled=True)  69 us
  transfers between devices with their start and end apart: 25, of which 18 were waited for; matrix products, arithmetic and copies ran while one was open for 21% of the time, Pallas kernels for 0%

commit v1 on v0

v1 whole, which is shorter than its diff:
```python
import functools

import jax
import jax.numpy as jnp
from jax import lax
from jax.experimental import pallas as pl
from jax.experimental.pallas import tpu as pltpu
from jax.sharding import PartitionSpec as P


LN_EPS = 1e-5
ROPE_BASE = 10000.0
F32 = jnp.float32
BF16 = jnp.bfloat16

CORE_GROUPS = [[0, 2, 4, 6], [1, 3, 5, 7]]
SIBLING = [(i, i ^ 1) for i in range(8)]


def mm(form, left, right):
    return jnp.einsum(form, left, right, preferred_element_type=F32)


def norm_stats(tensor):
    centered = tensor - jnp.mean(tensor, axis=-1, keepdims=True)
    inv_std = lax.rsqrt(jnp.mean(centered * centered, axis=-1, keepdims=True) + LN_EPS)
    return centered * inv_std, inv_std


def norm_backward(grad_hat, x_hat, inv_std):
    mean_grad = jnp.mean(grad_hat, axis=-1, keepdims=True)
    mean_proj = jnp.mean(grad_hat * x_hat, axis=-1, keepdims=True)
    return inv_std * (grad_hat - mean_grad - x_hat * mean_proj)


def attention_kernel(heads, kv_heads, head_dim, qkv_ref, ga_ref, cos_ref, sin_ref, norm_ref, out_ref, gqkv_ref, gnorm_ref):
    seq_len = qkv_ref.shape[0]
    group = heads // kv_heads
    scale = head_dim ** -0.5
    cosine, sine = cos_ref[...], sin_ref[...]
    even = lax.rem(lax.broadcasted_iota(jnp.int32, (seq_len, head_dim), 1), 2) == 0
    causal = (lax.broadcasted_iota(jnp.int32, (seq_len, seq_len), 0)
              >= lax.broadcasted_iota(jnp.int32, (seq_len, seq_len), 1))

    def turn(tensor, signed_sine):
        swapped = jnp.where(even, pltpu.roll(tensor, head_dim - 1, 1), pltpu.roll(tensor, 1, 1))
        return tensor * cosine + swapped * signed_sine

    def dot(left, right, left_dim, right_dim):
        return lax.dot_general(left, right, (((left_dim,), (right_dim,)), ((), ())), preferred_element_type=F32)

    def columns(index):
        return pl.ds(index * head_dim, head_dim)

    @pl.when(pl.program_id(0) == 0)
    def _():
        gnorm_ref[...] = jnp.zeros_like(gnorm_ref)

    def finish(index, grad_rot, hat, inv, gain):
        scaled = turn(grad_rot, -sine)
        gnorm_ref[pl.ds(index, 1), :] += jnp.sum(scaled * hat, axis=0, keepdims=True)
        gqkv_ref[:, columns(index)] = norm_backward(scaled * gain, hat, inv).astype(BF16)

    for kv in range(kv_heads):
        k_index, v_index = heads + kv, heads + kv_heads + kv
        k_hat, k_inv = norm_stats(qkv_ref[:, columns(k_index)].astype(F32))
        k_gain = norm_ref[pl.ds(k_index, 1), :]
        k_rot = turn(k_hat * k_gain, sine).astype(BF16)
        value = qkv_ref[:, columns(v_index)]
        grad_k = jnp.zeros((seq_len, head_dim), F32)
        grad_v = jnp.zeros((seq_len, head_dim), F32)
        for head in range(kv * group, (kv + 1) * group):
            q_hat, q_inv = norm_stats(qkv_ref[:, columns(head)].astype(F32))
            q_gain = norm_ref[pl.ds(head, 1), :]
            q_rot = turn(q_hat * q_gain, sine).astype(BF16)
            scores = jnp.where(causal, dot(q_rot, k_rot, 1, 1) * scale, -1e30)
            weights = jnp.exp(scores - jnp.max(scores, axis=-1, keepdims=True))
            probs = weights / jnp.sum(weights, axis=-1, keepdims=True)
            probs_bf = probs.astype(BF16)
            out_ref[:, columns(head)] = dot(probs_bf, value, 1, 0).astype(BF16)
            grad_out = ga_ref[:, columns(head)]
            grad_probs = dot(grad_out, value, 1, 1)
            grad_v += dot(probs_bf, grad_out, 0, 0)
            centre = jnp.sum(grad_probs * probs, axis=-1, keepdims=True)
            grad_scores = (probs * (grad_probs - centre) * scale).astype(BF16)
            grad_k += dot(grad_scores, q_rot, 0, 0)
            finish(head, dot(grad_scores, k_rot, 1, 0), q_hat, q_inv, q_gain)
        finish(k_index, grad_k, k_hat, k_inv, k_gain)
        gqkv_ref[:, columns(v_index)] = grad_v.astype(BF16)


def attention(qkv, grad_attn, cosine, sine, norm_full, batch, seq_len, heads, kv_heads, head_dim):
    tokens, width = qkv.shape

    def rows(columns):
        return pl.BlockSpec((seq_len, columns), lambda b: (b, 0))

    whole = pl.BlockSpec(norm_full.shape, lambda b: (0, 0))
    return pl.pallas_call(
        functools.partial(attention_kernel, heads, kv_heads, head_dim),
        grid=(batch,),
        in_specs=[rows(width), rows(heads * head_dim), rows(head_dim), rows(head_dim), whole],
        out_specs=[rows(heads * head_dim), rows(width), whole],
        out_shape=[jax.ShapeDtypeStruct((tokens, heads * head_dim), BF16),
                   jax.ShapeDtypeStruct((tokens, width), BF16),
                   jax.ShapeDtypeStruct(norm_full.shape, F32)],
        compiler_params=pltpu.CompilerParams(dimension_semantics=("arbitrary",), vmem_limit_bytes=32 * 1024 * 1024),
        cost_estimate=pl.CostEstimate(flops=12 * batch * heads * seq_len * seq_len * head_dim, bytes_accessed=10 * tokens * width,
                                      transcendentals=batch * heads * seq_len * seq_len),
        name="attention",
    )(qkv, grad_attn, cosine, sine, norm_full)


def split_model_dim(tensor, core, width):
    pieces = [lax.slice_in_dim(tensor, j * width, (j + 1) * width, axis=tensor.ndim - 1) for j in range(8)]
    even = jnp.concatenate(pieces[0::2], axis=-1)
    odd = jnp.concatenate(pieces[1::2], axis=-1)
    first = core == 0
    return jnp.where(first, even, odd), jnp.where(first, odd, even)


def join_model_dim(mine, other, core, width):
    first = core == 0
    even = jnp.where(first, mine, other)
    odd = jnp.where(first, other, mine)
    pieces = []
    for j in range(4):
        pieces += [even[..., j * width:(j + 1) * width], odd[..., j * width:(j + 1) * width]]
    return jnp.concatenate(pieces, axis=-1)


def gather_mine(shard):
    return lax.all_gather(shard, 'fsdp', axis=0, tiled=True, axis_index_groups=CORE_GROUPS)


def with_sibling(mine):
    return mine, lax.ppermute(mine, 'fsdp', SIBLING)


def after(value, event):
    return lax.optimization_barrier((value, event))[0]


def chain_sum(parts, rank, n):
    def chunk(part, offset):
        return lax.dynamic_index_in_dim(part, rank[offset % n], 0, keepdims=False)

    halves = range(len(parts))
    from_left = [None for _ in halves]
    from_right = [None for _ in halves]
    sent = []
    for step in range(n - 1):
        right = [(i, i + 1) for i in range(step + 1)]
        left = [(n - 1 - i, n - 2 - i) for i in range(step + 1)]
        if step:
            from_left, from_right = after((from_left, from_right), sent[-len(parts):])
            from_left, from_right = list(from_left), list(from_right)
        for h in halves:
            go_right, go_left = chunk(parts[h], n - 1 - step), chunk(parts[h], step + 1)
            if step:
                go_right = (go_right.astype(F32) + from_left[h].astype(F32)).astype(BF16)
                go_left = (go_left.astype(F32) + from_right[h].astype(F32)).astype(BF16)
            sent.append((go_right, go_left))
            from_left[h] = lax.ppermute(go_right, 'tp', right)
            from_right[h] = lax.ppermute(go_left, 'tp', left)
    total = [chunk(parts[h], 0).astype(F32) + from_left[h].astype(F32) + from_right[h].astype(F32) for h in halves]
    return total, [sent[k * len(parts):(k + 1) * len(parts)] for k in range(n - 1)]


def chain_gather(block, rank, n):
    zero = jnp.uint32(0)
    from_left, from_right = [], []
    go_right = go_left = block
    for step in range(n - 1):
        go_right = lax.ppermute(go_right, 'tp', [(i, i + 1) for i in range(step, n - 1)])
        go_left = lax.ppermute(go_left, 'tp', [(i, i - 1) for i in range(n - 1 - step, 0, -1)])
        from_left.append(go_right)
        from_right.append(go_left)
    whole = jnp.zeros((n,) + block.shape, block.dtype)
    own = after(block, (from_left[0], from_right[0]))
    whole = lax.dynamic_update_slice(whole, own[None], (rank[0], zero, zero))
    for k in range(1, n):
        piece = jnp.where(rank[0] >= k, from_left[k - 1], from_right[n - k - 1])
        whole = lax.dynamic_update_slice(whole, piece[None], (rank[n - k], zero, zero))
    return whole


def solution(mesh):
    act_spec = P('fsdp', None, None)
    col_spec = P('fsdp', 'tp')
    row_spec = P('tp', 'fsdp')
    weight_specs = (P('fsdp'), col_spec, col_spec, col_spec, row_spec, col_spec, col_spec, row_spec, row_spec, row_spec)
    in_specs = (act_spec, P('fsdp', None), act_spec) + weight_specs
    out_specs = (act_spec, act_spec) + weight_specs
    n_tp = mesh.shape['tp']
    n_fsdp = mesh.shape['fsdp']

    def device_step(hidden, positions, grad_layer, ln_weight, w_query, w_key, w_value, w_out, w_gate, w_up, w_down, q_norm, k_norm):
        batch, seq_len, model_dim = hidden.shape
        tokens = batch * seq_len
        width = ln_weight.shape[0]
        heads, kv_heads = q_norm.shape[0], k_norm.shape[0]
        dims_part = q_norm.shape[1]
        head_dim = dims_part * n_fsdp
        q_width, kv_width = heads * head_dim, kv_heads * head_dim
        qkv_width = q_width + 2 * kv_width
        fsdp = lax.axis_index('fsdp')
        core = lax.rem(fsdp, 2)
        tp = [lax.rem(lax.axis_index('tp') + k, n_tp).astype(jnp.uint32) for k in range(n_tp)]

        attn_shard = jnp.concatenate([w_query, w_key, w_value, w_out.T], axis=1)
        attn_mine = gather_mine(attn_shard)
        gate_mine = gather_mine(w_gate)
        up_mine = gather_mine(w_up)
        down_mine = gather_mine(w_down.T)
        attn_w = with_sibling(attn_mine)

        small = jnp.concatenate([ln_weight, q_norm.reshape(-1), k_norm.reshape(-1)])
        small_all = lax.all_gather(small, 'fsdp', axis=0, tiled=False).astype(F32)
        ln_full = small_all[:, :width].reshape(-1)
        q_part = heads * dims_part
        qn_full = small_all[:, width:width + q_part].reshape(n_fsdp, heads, dims_part).transpose(1, 0, 2).reshape(heads, head_dim)
        kn_full = small_all[:, width + q_part:].reshape(n_fsdp, kv_heads, dims_part).transpose(1, 0, 2).reshape(kv_heads, head_dim)
        norm_full = jnp.concatenate([qn_full, kn_full], axis=0)

        x_hat, _ = norm_stats(hidden.astype(F32))
        normed = (x_hat * ln_full).astype(BF16).reshape(tokens, model_dim)
        h_m, h_o = split_model_dim(normed, core, width)
        g_m, g_o = split_model_dim(grad_layer.reshape(tokens, model_dim), core, width)

        def contract(left, right):
            return mm('td,de->te', left[0], right[0]) + mm('td,de->te', left[1], right[1])

        def expand(left, right):
            return [mm('te,de->td', left, part) for part in right]

        def weight_grad(rows, cols):
            other = mm('td,te->de', rows[1], cols).astype(BF16)
            arrived = lax.ppermute(other, 'fsdp', SIBLING)
            total = (mm('td,te->de', rows[0], cols) + arrived.astype(F32)).astype(BF16)
            return lax.psum_scatter(total, 'fsdp', scatter_dimension=0, tiled=True, axis_index_groups=CORE_GROUPS)

        h_pair, g_pair = (h_m, h_o), (g_m, g_o)
        qkv_w = tuple(part[:, :qkv_width] for part in attn_w)
        out_w = tuple(part[:, qkv_width:] for part in attn_w)

        qkv = contract(h_pair, qkv_w).astype(BF16)
        grad_attn = contract(g_pair, out_w).astype(BF16)
        lane = lax.broadcasted_iota(jnp.int32, (1, head_dim), 1)
        inv_freq = ROPE_BASE ** (-((lane // 2) * 2).astype(F32) / head_dim)
        angles = positions.reshape(tokens, 1).astype(F32) * inv_freq
        cosine = jnp.cos(angles)
        sine = jnp.where(lane % 2 == 0, -1.0, 1.0) * jnp.sin(angles)
        attn_out, grad_qkv, norm_part = attention(qkv, grad_attn, cosine, sine, norm_full, batch, seq_len, heads, kv_heads, head_dim)
        attn_part = expand(attn_out, out_w)
        attn_dh = expand(grad_qkv, qkv_w)


        gate_w = with_sibling(after(gate_mine, attn_part))
        gate = contract(h_pair, gate_w).astype(BF16)
        up_w = with_sibling(after(up_mine, gate))
        up_proj = contract(h_pair, up_w).astype(BF16)
        down_w = with_sibling(after(down_mine, up_proj))
        gate_f32, up_f32 = gate.astype(F32), up_proj.astype(F32)
        sigma = jax.nn.sigmoid(gate_f32)
        gated_act = (gate_f32 * sigma * up_f32).astype(BF16)
        mlp_part = expand(gated_act, down_w)
        forward_part = [(a + b).astype(BF16) for a, b in zip(attn_part, mlp_part)]

        def own_chunk(tensor):
            return lax.dynamic_index_in_dim(tensor.reshape(n_tp, tokens // n_tp, model_dim), tp[0], 0, keepdims=False).astype(F32)

        def chunks(parts):
            return [part.reshape(n_tp, tokens // n_tp, part.shape[-1]) for part in parts]

        fwd_sum, fwd_sent = chain_sum(chunks(forward_part), tp, n_tp)
        hidden_chunk = own_chunk(hidden)
        out_chunk = (hidden_chunk + join_model_dim(fwd_sum[0], fwd_sum[1], core, width)).astype(BF16)
        layer_out = chain_gather(out_chunk, tp, n_tp)

        grad_act = contract((after(g_m, forward_part[0]), after(g_o, forward_part[1])), down_w)
        grad_gate = (grad_act * up_f32 * sigma * (1.0 + gate_f32 * (1.0 - sigma))).astype(BF16)
        grad_up = (grad_act * gate_f32 * sigma).astype(BF16)
        early_gate, early_up = after(grad_gate, fwd_sent[1]), after(grad_up, fwd_sent[2])
        dh_part = [(a + b + c).astype(BF16)
                   for a, b, c in zip(attn_dh, expand(early_gate, gate_w), expand(early_up, up_w))]
        dh_sum, _ = chain_sum(chunks(dh_part), tp, n_tp)

        grad_wqkv = weight_grad(h_pair, after(grad_qkv, forward_part))
        grad_wout = weight_grad(g_pair, after(attn_out, forward_part))
        grad_wdown = weight_grad(g_pair, after(gated_act, dh_part))
        grad_wgate = weight_grad(h_pair, after(grad_gate, dh_part))
        grad_wup = weight_grad(h_pair, after(grad_up, dh_part))
        grad_wqkv, grad_wout = after((grad_wqkv, grad_wout), dh_part)

        dh_sum = after(dh_sum, out_chunk)
        grad_normed = join_model_dim(dh_sum[0], dh_sum[1], core, width).astype(BF16).astype(F32)
        late_hidden, late_grad = after((own_chunk(hidden), own_chunk(grad_layer)), (out_chunk, dh_part))
        xc_hat, xc_inv = norm_stats(late_hidden)
        grad_chunk = (late_grad + norm_backward(grad_normed * ln_full, xc_hat, xc_inv)).astype(BF16)
        grad_hidden = chain_gather(grad_chunk, tp, n_tp)

        ln_part = jnp.sum(grad_normed * xc_hat, axis=0).reshape(n_fsdp, width)
        all_heads = heads + kv_heads
        head_part = norm_part.reshape(all_heads, n_fsdp, dims_part).transpose(1, 0, 2).reshape(n_fsdp, all_heads * dims_part)
        small_parts = lax.all_gather(jnp.concatenate([ln_part, head_part], axis=1), ('fsdp', 'tp'), axis=0, tiled=False)
        small_own = lax.dynamic_index_in_dim(small_parts, fsdp, 1, keepdims=False)
        grad_ln = jnp.sum(small_own[:, :width], axis=0)
        head_own = small_own[:, width:].reshape(n_fsdp, n_tp, all_heads * dims_part)
        head_own = jnp.sum(lax.dynamic_index_in_dim(head_own, tp[0], 1, keepdims=False), axis=0)
        norm_own = head_own.reshape(all_heads, dims_part)

        return (layer_out.reshape(hidden.shape), grad_hidden.reshape(hidden.shape), grad_ln, grad_wqkv[:, :q_width], grad_wqkv[:, q_width:q_width + kv_width],
                grad_wqkv[:, q_width + kv_width:], grad_wout.T, grad_wgate, grad_wup, grad_wdown.T,
                norm_own[:heads], norm_own[heads:])

    return jax.shard_map(device_step, mesh=mesh, in_specs=in_specs, out_specs=out_specs, check_vma=False)
```

time: 2190 us -> 970 us (0.44)
  waiting for transfers between devices: 1590 us -> 300 us
  starting transfers between devices: 1.58 us -> 93 us
  matrix products: 338 us -> 271 us
  blocking collectives: 78.7 us -> 135 us
  local copies, waits for them, and re-layouts: 85.9 us -> 37 us
  Pallas kernels: 0 us -> 30.2 us
    psum x2 -> x0, waiting for transfers between devices: 854 us -> none  [the longest x1 428 us: device_step(): mlp_dh_sum = lax.psum(mlp_dh.astype(jnp.bfloat16), 'tp')]
    reduce_scatter x5, waiting for transfers between devices: 285 us -> 0.01 us  [weight_grad(): lax.psum_scatter(total, 'fsdp', scatter_dimension=0, tiled=True, axis_ind...]
    all_gather x14 -> x4, waiting for transfers between devices: 326 us -> 144 us  [gather_mine(): lax.all_gather(shard, 'fsdp', axis=0, tiled=True, axis_index_groups=CORE_...]
    ppermute x0 -> x45, waiting for transfers between devices: none -> 155 us  [the longest x6 80.4 us: chain_gather(): lax.ppermute(go_left, 'tp', [(i, i - 1) for i in range(n - 1 - step, 0, -...]
    unnamed x29 -> x9, waiting for transfers between devices: 124 us -> 1.49 us
    ppermute x0 -> x45, starting transfers between devices: none -> 92.6 us  [the longest x12 53.8 us: chain_sum(): from_left[h] = lax.ppermute(go_right, 'tp', right)]
    all_gather x6 -> x2, blocking collectives: 54.6 us -> 135 us  [the longest x1 125 us: device_step(): lax.all_gather(jnp.concatenate([ln_part, head_part], axis=1), ('fsdp', 't...]
    dot_general x26 -> x30, matrix products: 333 us -> 271 us  [mm(): return jnp.einsum(form, left, right, preferred_element_type=F32)]
  transfers between devices with their start and end apart: 25 -> 54, of which waited for: 18 -> 17; matrix products, arithmetic and copies ran while one was open for 21% -> 39% of each run, Pallas kernels for 0% -> 3%
where the time goes in v1:
time: 970 us; the launch traced here: 960 us
  waiting for transfers between devices  300 us (31%)
  matrix products  271 us (28%)
  blocking collectives  135 us (14%)
  starting transfers between devices  93 us (10%)
  other arithmetic  77.6 us (8%)
  local copies, waits for them, and re-layouts  37 us (4%)
  Pallas kernels  30.2 us (3%)
  between operations  15.6 us (2%)
    dot_general x30, matrix products, mm(): return jnp.einsum(form, left, right, preferred_element_type=F32)  271 us
    all_gather x4, waiting for transfers between devices, gather_mine(): lax.all_gather(shard, 'fsdp', axis=0, tiled=True, axis_index_groups=CORE_...  144 us
    all_gather x1, blocking collectives, device_step(): lax.all_gather(jnp.concatenate([ln_part, head_part], axis=1), ('fsdp', 't...  125 us
    ppermute x6, waiting for transfers between devices, chain_gather(): lax.ppermute(go_left, 'tp', [(i, i - 1) for i in range(n - 1 - step, 0, -...  80.4 us
    ppermute x12, waiting for transfers between devices, chain_sum(): from_left[h] = lax.ppermute(go_right, 'tp', right)  65.9 us
    ppermute x12, starting transfers between devices, chain_sum(): from_left[h] = lax.ppermute(go_right, 'tp', right)  53.8 us
    pallas_call x1, Pallas kernels, attention(): pl.pallas_call(functools.partial(attention_kernel, heads, kv_heads, head_...  30.2 us
  transfers between devices with their start and end apart: 54, of which 17 were waited for; matrix products, arithmetic and copies ran while one was open for 39% of the time, Pallas kernels for 3%

profile of v1, /device:TPU:0, one launch (start us, length us, event | category | flops | bytes accessed | tf_op | source)
XLA Modules:
  0.0 960.1 jit_solution(13762672223739135121)
XLA Ops:
  15.0 10.4 %all-gather.2 = bf16[8,1,512]{2,1,0:T(2,128)(2,1)S(1)} all-gather(bf16[1,1,512]{2,1,0:T(2,128)(2,1)S(1)} %reshape.249), channel_id=2, replica_groups=mesh['tp'=4,'fsdp'=8] {'fsdp'}, dimensions={0}, use_global_device_ids=true | all-gather | bytes 9216 | tf_op jit(solution)/shard_map/all_gather | solution.py:219
  29.8 56.1 %all-gather.8.cloned.1.call-done = bf16[1536,2048]{0,1:T(8,128)(2,1)} async-done(((bf16[384,2048]{0,1:T(8,128)(2,1)}), bf16[1536,2048]{0,1:T(8,128)(2,1)}) %all-gather.8.cloned.1.call-update) | async-done | bytes 6291472 | tf_op jit(solution)/shard_map/all_gather | solution.py:133
  92.5 6.9 fusion.4
  108.2 6.0 fusion.22
  114.1 7.4 add_convert_fusion.10.qkv_ref
  126.6 30.2 %attention.1 = (bf16[1024,768]{1,0:T(8,128)(2,1)S(1)}, bf16[1024,1280]{1,0:T(8,128)(2,1)S(1)}, f32[8,128]{1,0:T(8,128)S(1)}) custom-call(bf16[1024,1280]{1,0:T(8,128)(2,1)S(1)} %add_convert_fusion.10.qkv_ref, bf16[1024,768]{1,0:T(8,128)(2,1)S(1)} %add_convert_fusion.13.ga_ref, f32[1024,128]{1,0:T(8,128)S(1)} %get-tuple-element.198.cos_ref, ...), custom_call_target="tpu_custom_call" | custom-call | flops 2415919104 | bytes 13107200 | tf_op jit(solution)/shard_map/attention/pallas_call | solution.py:99
  156.8 6.7 fusion.30
  168.5 10.7 %fusion.63 = f32[1024,2048]{1,0:T(8,128)S(1)} fusion(bf16[1024,1536]{1,0:T(8,128)(2,1)} %copy-done.6, bf16[1536,2048]{1,0:T(8,128)(2,1)} %all-gather.10.cloned.1.call-done), kind=kOutput, calls=%fused_computation.182 | convolution fusion | flops 6442450944 | bytes 17825792 | tf_op jit(solution)/shard_map/td,de->te/dot_general | solution.py:21
  181.8 8.3 add_convert_fusion.4
  190.0 39.7 %all-gather.12.cloned.1.call-done = bf16[1536,2048]{1,0:T(8,128)(2,1)} async-done(((bf16[384,2048]{1,0:T(8,128)(2,1)}), bf16[1536,2048]{1,0:T(8,128)(2,1)}) %all-gather.12.cloned.1.call-update) | async-done | bytes 6291472 | tf_op jit(solution)/shard_map/all_gather | solution.py:133
  229.9 10.1 %fusion.64 = f32[1024,2048]{1,0:T(8,128)S(1)} fusion(bf16[1024,1536]{1,0:T(8,128)(2,1)} %copy-done.6, bf16[1536,2048]{1,0:T(8,128)(2,1)} %all-gather.12.cloned.1.call-done), kind=kOutput, calls=%fused_computation.183 | convolution fusion | flops 6442450944 | bytes 17825792 | tf_op jit(solution)/shard_map/td,de->te/dot_general | solution.py:21
  240.3 13.0 %fusion.5 = (bf16[1024,2048]{1,0:T(8,128)(2,1)}, bf16[1024,2048]{1,0:T(8,128)(2,1)}) fusion(bf16[1024,2048]{1,0:T(8,128)(2,1)S(1)} %copy-done.41, f32[1024,2048]{1,0:T(8,128)S(1)} %fusion.64, bf16[1024,1536]{1,0:T(8,128)(2,1)S(1)} %copy-done.12, bf16[1536,2048]{1,0:T(8,128)(2,1)} %collective-permute-done.2), kind=kOutput, calls=%fused_computation.16 | convolution fusion | flops 6463422464 | bytes 30408704 | tf_op jit(solution)/shard_map/td,de->te/dot_general | solution.py:21
  253.3 48.1 %all-gather.14.cloned.1.call-done = bf16[1536,2048]{0,1:T(8,128)(2,1)} async-done(((bf16[384,2048]{0,1:T(8,128)(2,1)}), bf16[1536,2048]{0,1:T(8,128)(2,1)}) %all-gather.14.cloned.1.call-update) | async-done | bytes 6291472 | tf_op jit(solution)/shard_map/all_gather | solution.py:133
  301.4 8.5 fusion.18
  309.8 8.7 add_convert_fusion.9
  325.8 9.4 fusion.65
  335.2 9.0 add_convert_fusion.8
  353.7 17.6 %fusion.8 = (bf16[1024,2048]{1,0:T(8,128)(2,1)}, bf16[1024,2048]{1,0:T(8,128)(2,1)}) fusion(bf16[1024,2048]{1,0:T(8,128)(2,1)} %get-tuple-element.200, bf16[1024,2048]{1,0:T(8,128)(2,1)} %add_convert_fusion.4, f32[1024,2048]{1,0:T(8,128)} %fusion.65, bf16[1024,1536]{1,0:T(8,128)(2,1)} %copy-done.20, bf16[1536,2048]{0,1:T(8,128)(2,1)} %collective-permute-done.4), kind=kOutput, calls=%fused_computation.19 | convolution fusion | flops 6476005376 | bytes 34603008 | tf_op jit(solution)/shard_map/td,de->te/dot_general | solution.py:21
  371.3 8.6 convolution_convert_fusion
  390.6 12.1 %fusion.66 = f32[1024,1536]{1,0:T(8,128)} fusion(bf16[1024,2048]{1,0:T(8,128)(2,1)} %get-tuple-element.87, bf16[1536,2048]{1,0:T(8,128)(2,1)} %all-gather.10.cloned.1.call-done), kind=kOutput, calls=%fused_computation.185 | convolution fusion | flops 6442450944 | bytes 16777216 | tf_op jit(solution)/shard_map/te,de->td/dot_general | solution.py:21
  402.7 10.4 %fusion.68 = f32[1024,1536]{1,0:T(8,128)} fusion(bf16[1024,2048]{1,0:T(8,128)(2,1)} %get-tuple-element.87, bf16[1536,2048]{1,0:T(8,128)(2,1)S(1)} %bitcast.186), kind=kOutput, calls=%fused_computation.187 | convolution fusion | flops 6442450944 | bytes 16777216 | tf_op jit(solution)/shard_map/te,de->td/dot_general | solution.py:21
  413.1 5.1 collective-permute-done.8
  425.9 12.5 %add_convert_fusion.6 = bf16[1024,1536]{1,0:T(8,128)(2,1)} fusion(f32[1024,1536]{1,0:T(8,128)S(1)} %bitcast.190, f32[1024,1536]{1,0:T(8,128)} %fusion.68, bf16[1024,2048]{1,0:T(8,128)(2,1)} %get-tuple-element.88, bf16[1536,2048]{1,0:T(8,128)(2,1)} %collective-permute-done.2), kind=kOutput, calls=%fused_computation.33 | convolution fusion | flops 6447169536 | bytes 26214400 | tf_op jit(solution)/shard_map/te,de->td/dot_general | solution.py:21
  438.4 5.2 add_convert_fusion.11
  443.7 10.5 %fusion.67 = f32[1024,1536]{1,0:T(8,128)S(1)} fusion(bf16[1024,2048]{1,0:T(8,128)(2,1)} %get-tuple-element.88, bf16[1536,2048]{1,0:T(8,128)(2,1)} %all-gather.12.cloned.1.call-done), kind=kOutput, calls=%fused_computation.186 | convolution fusion | flops 6442450944 | bytes 16777216 | tf_op jit(solution)/shard_map/te,de->td/dot_general | solution.py:21
  454.2 9.1 add_convert_fusion.7
  463.4 8.6 convolution_convert_fusion.1
  472.0 7.5 add_convert_fusion.5
  482.5 11.9 %add_convert_fusion = bf16[1536,2048]{1,0:T(8,128)(2,1)} fusion(bf16[1536,2048]{1,0:T(8,128)(2,1)} %collective-permute-done.44, bf16[1024,1536]{1,0:T(8,128)(2,1)S(1)} %copy-done.18, bf16[1024,2048]{1,0:T(8,128)(2,1)} %get-tuple-element.89), kind=kOutput, calls=%fused_computation.11 | convolution fusion | flops 6451888128 | bytes 19922944 | tf_op jit(solution)/shard_map/td,te->de/dot_general | solution.py:21
  496.3 10.9 %convolution_convert_fusion.2 = bf16[1536,2048]{1,0:T(8,128)(2,1)} fusion(bf16[1024,1536]{1,0:T(8,128)(2,1)S(1)} %copy-done.13, bf16[1024,2048]{1,0:T(8,128)(2,1)} %get-tuple-element.88), kind=kOutput, calls=%fused_computation.31 | convolution fusion | flops 6445596672 | bytes 13631488 | tf_op jit(solution)/shard_map/td,te->de/dot_general | solution.py:21
  513.1 5.5 collective-permute-start.14
  524.5 10.6 %add_convert_fusion.1 = bf16[1536,2048]{1,0:T(8,128)(2,1)} fusion(bf16[1536,2048]{1,0:T(8,128)(2,1)} %collective-permute-done.43, bf16[1024,1536]{1,0:T(8,128)(2,1)S(1)} %copy-done.8, bf16[1024,2048]{1,0:T(8,128)(2,1)S(1)} %copy-done.40), kind=kOutput, calls=%fused_computation.12 | convolution fusion | flops 6451888128 | bytes 19922944 | tf_op jit(solution)/shard_map/td,te->de/dot_general | solution.py:21
  539.1 11.1 %convolution_convert_fusion.3 = bf16[1536,2048]{1,0:T(8,128)(2,1)} fusion(bf16[1024,1536]{1,0:T(8,128)(2,1)S(1)} %copy-done.14, bf16[1024,2048]{1,0:T(8,128)(2,1)} %get-tuple-element.87), kind=kOutput, calls=%fused_computation.32 | convolution fusion | flops 6445596672 | bytes 13631488 | tf_op jit(solution)/shard_map/td,te->de/dot_general | solution.py:21
  554.1 5.1 collective-permute-start.12
  559.2 10.4 %collective-permute-done.22 = bf16[256,1536]{1,0:T(8,128)(2,1)S(1)} collective-permute-done((bf16[256,1536]{1,0:T(8,128)(2,1)S(1)}, bf16[256,1536]{1,0:T(8,128)(2,1)S(1)}, u32[]{:S(2)}, u32[]{:S(2)}) %collective-permute-start.22) | collective-permute-done | bytes 786464 | tf_op jit(solution)/shard_map/ppermute | solution.py:164
  576.6 6.0 collective-permute-start.27
  586.4 5.3 collective-permute-start.26
  603.4 5.5 collective-permute-start.16
  610.2 10.0 %collective-permute-done.26 = bf16[256,1536]{1,0:T(8,128)(2,1)} collective-permute-done((bf16[256,1536]{1,0:T(8,128)(2,1)}, bf16[256,1536]{1,0:T(8,128)(2,1)}, u32[]{:S(2)}, u32[]{:S(2)}) %collective-permute-start.26) | collective-permute-done | bytes 786464 | tf_op jit(solution)/shard_map/ppermute | solution.py:164
  621.8 9.9 %collective-permute-start.32 = (bf16[256,1536]{1,0:T(8,128)(2,1)S(1)}, bf16[256,1536]{1,0:T(8,128)(2,1)S(1)}, u32[]{:S(2)}, u32[]{:S(2)}) collective-permute-start(bf16[256,1536]{1,0:T(8,128)(2,1)S(1)} %add_convert_fusion.15), channel_id=1, source_target_pairs={{0,8},{8,16},{16,24},{1,9},{9,17},{17,25},{2,10},{10,18},{18,26},{... | collective-permute-start | bytes 2359304 | tf_op jit(solution)/shard_map/ppermute | solution.py:164
  639.4 30.6 %collective-permute-done.32 = bf16[256,1536]{1,0:T(8,128)(2,1)S(1)} collective-permute-done((bf16[256,1536]{1,0:T(8,128)(2,1)S(1)}, bf16[256,1536]{1,0:T(8,128)(2,1)S(1)}, u32[]{:S(2)}, u32[]{:S(2)}) %collective-permute-start.32) | collective-permute-done | bytes 786464 | tf_op jit(solution)/shard_map/ppermute | solution.py:164
  670.0 5.3 collective-permute-start.30
  679.0 10.9 %add_convert_fusion.2 = bf16[1536,2048]{1,0:T(8,128)(2,1)} fusion(bf16[1536,2048]{1,0:T(8,128)(2,1)} %collective-permute-done.42, bf16[1024,1536]{1,0:T(8,128)(2,1)S(1)} %copy-done.9, bf16[1024,2048]{1,0:T(8,128)(2,1)S(1)} %copy-done.39), kind=kOutput, calls=%fused_computation.13 | convolution fusion | flops 6451888128 | bytes 19922944 | tf_op jit(solution)/shard_map/td,te->de/dot_general | solution.py:21
  691.1 5.0 collective-permute-done.31
  712.7 124.9 %all-gather.1 = f32[256,512]{1,0:T(8,128)S(1)} all-gather(f32[8,512]{1,0:T(8,128)S(1)} %pad_maximum_fusion.5), channel_id=3, replica_groups=mesh['tp'=4,'fsdp'=8] {'fsdp','tp'}, dimensions={0}, use_global_device_ids=true | all-gather | bytes 540672 | tf_op jit(solution)/shard_map/all_gather | solution.py:306
  852.3 25.9 %collective-permute-done.36 = bf16[256,3072]{1,0:T(8,128)(2,1)S(1)} collective-permute-done((bf16[256,3072]{1,0:T(8,128)(2,1)S(1)}, bf16[256,3072]{1,0:T(8,128)(2,1)S(1)}, u32[]{:S(2)}, u32[]{:S(2)}) %collective-permute-start.36) | collective-permute-done | bytes 1572896 | tf_op jit(solution)/shard_map/ppermute | solution.py:176
  880.6 31.3 %collective-permute-done.19 = bf16[256,3072]{1,0:T(8,128)(2,1)S(1)} collective-permute-done((bf16[256,3072]{1,0:T(8,128)(2,1)}, bf16[256,3072]{1,0:T(8,128)(2,1)S(1)}, u32[]{:S(2)}, u32[]{:S(2)}) %collective-permute-start.19) | collective-permute-done | bytes 1572896 | tf_op jit(solution)/shard_map/ppermute | solution.py:176
  916.3 23.1 %collective-permute-done.37 = bf16[256,3072]{1,0:T(8,128)(2,1)S(1)} collective-permute-done((bf16[256,3072]{1,0:T(8,128)(2,1)S(1)}, bf16[256,3072]{1,0:T(8,128)(2,1)S(1)}, u32[]{:S(2)}, u32[]{:S(2)}) %collective-permute-start.37) | collective-permute-done | bytes 1572896 | tf_op jit(solution)/shard_map/ppermute | solution.py:176
  (323 shorter events, 189.1 us)
Async XLA Ops:
  7.2 78.8 %all-gather.8.cloned.1.call-start = ((), (), s32[]{:S(2)}) async-start(), calls=%async_computation.5 | async-start | bytes 7864320 | tf_op jit(solution)/shard_map/all_gather | solution.py:133
  13.2 154.8 %all-gather.10.cloned.1.call-start = ((), (), s32[]{:S(2)}) async-start(), calls=%async_computation.6 | async-start | bytes 7864320 | tf_op jit(solution)/shard_map/all_gather | solution.py:133
  13.9 215.8 %all-gather.12.cloned.1.call-start = ((), (), s32[]{:S(2)}) async-start(), calls=%async_computation.7 | async-start | bytes 7864320 | tf_op jit(solution)/shard_map/all_gather | solution.py:133
  14.7 286.7 %all-gather.14.cloned.1.call-start = ((), (), s32[]{:S(2)}) async-start(), calls=%async_computation.8 | async-start | bytes 7864320 | tf_op jit(solution)/shard_map/all_gather | solution.py:133
  86.0 28.2 %collective-permute-start = (bf16[1536,2048]{0,1:T(8,128)(2,1)}, bf16[1536,2048]{0,1:T(8,128)(2,1)}, u32[]{:S(2)}, u32[]{:S(2)}) collective-permute-start(bf16[1536,2048]{0,1:T(8,128)(2,1)} %all-gather.8.cloned.1.call-done), channel_id=1, source_target_pairs={{0,1},{1,0},{2,3},{3,2},{4,5},{5,4},{6,7},{7,6},{8,9},{9,8},{10,11... | collective-permute-start | bytes 18874376 | tf_op jit(solution)/shard_map/ppermute | solution.py:137
  229.8 714.9 %reduce-scatter.8.cloned.1.call-start = ((), (), s32[]{:S(2)}) async-start(), calls=%async_computation.10 | async-start | bytes 2949120 | tf_op jit(solution)/shard_map/reduce_scatter | solution.py:241
  301.4 33.8 %collective-permute-start.4 = (bf16[1536,2048]{0,1:T(8,128)(2,1)}, bf16[1536,2048]{0,1:T(8,128)(2,1)}, u32[]{:S(2)}, u32[]{:S(2)}) collective-permute-start(bf16[1536,2048]{0,1:T(8,128)(2,1)} %all-gather.14.cloned.1.call-done), channel_id=1, source_target_pairs={{0,1},{1,0},{2,3},{3,2},{4,5},{5,4},{6,7},{7,6},{8,9},{9,8},{10,11... | collective-permute-start | bytes 18874376 | tf_op jit(solution)/shard_map/ppermute | solution.py:137
  319.5 60.4 %collective-permute-start.3 = (bf16[256,1536]{1,0:T(8,128)(2,1)S(1)}, bf16[256,1536]{1,0:T(8,128)(2,1)}, u32[]{:S(2)}, u32[]{:S(2)}) collective-permute-start(bf16[256,1536]{1,0:T(8,128)(2,1)S(1)} %get-tuple-element.192), channel_id=1, source_target_pairs={{0,8},{1,9},{2,10},{3,11},{4,12},{5,13},{6,14},{7,15}} | collective-permute-start | bytes 2359304 | tf_op jit(solution)/shard_map/ppermute | solution.py:164
  324.0 55.9 %collective-permute-start.6 = (bf16[256,1536]{1,0:T(8,128)(2,1)}, bf16[256,1536]{1,0:T(8,128)(2,1)}, u32[]{:S(2)}, u32[]{:S(2)}) collective-permute-start(bf16[256,1536]{1,0:T(8,128)(2,1)} %get-tuple-element.191), channel_id=1, source_target_pairs={{24,16},{25,17},{26,18},{27,19},{28,20},{29,21},{30,22},{31,23}} | collective-permute-start | bytes 2359304 | tf_op jit(solution)/shard_map/ppermute | solution.py:165
  345.5 34.5 %collective-permute-start.5 = (bf16[256,1536]{1,0:T(8,128)(2,1)}, bf16[256,1536]{1,0:T(8,128)(2,1)}, u32[]{:S(2)}, u32[]{:S(2)}) collective-permute-start(bf16[256,1536]{1,0:T(8,128)(2,1)} %get-tuple-element.190), channel_id=1, source_target_pairs={{0,8},{1,9},{2,10},{3,11},{4,12},{5,13},{6,14},{7,15}} | collective-permute-start | bytes 2359304 | tf_op jit(solution)/shard_map/ppermute | solution.py:164
  347.8 32.2 %collective-permute-start.7 = (bf16[256,1536]{1,0:T(8,128)(2,1)}, bf16[256,1536]{1,0:T(8,128)(2,1)}, u32[]{:S(2)}, u32[]{:S(2)}) collective-permute-start(bf16[256,1536]{1,0:T(8,128)(2,1)} %get-tuple-element.189), channel_id=1, source_target_pairs={{24,16},{25,17},{26,18},{27,19},{28,20},{29,21},{30,22},{31,23}} | collective-permute-start | bytes 2359304 | tf_op jit(solution)/shard_map/ppermute | solution.py:165
  353.5 84.9 %collective-permute-start.41 = (bf16[1536,768]{1,0:T(8,128)(2,1)}, bf16[1536,768]{1,0:T(8,128)(2,1)}, u32[]{:S(2)}, u32[]{:S(2)}) collective-permute-start(bf16[1536,768]{1,0:T(8,128)(2,1)} %convolution_convert_fusion.4), channel_id=1, source_target_pairs={{0,1},{1,0},{2,3},{3,2},{4,5},{5,4},{6,7},{7,6},{8,9},{9,8},{10,11... | collective-permute-start | bytes 7077896 | tf_op jit(solution)/shard_map/ppermute | solution.py:239
  381.8 31.2 %collective-permute-start.11 = (bf16[256,1536]{1,0:T(8,128)(2,1)S(1)}, bf16[256,1536]{1,0:T(8,128)(2,1)S(1)}, u32[]{:S(2)}, u32[]{:S(2)}) collective-permute-start(bf16[256,1536]{1,0:T(8,128)(2,1)S(1)} %get-tuple-element.185), channel_id=1, source_target_pairs={{24,16},{16,8},{25,17},{17,9},{26,18},{18,10},{27,19},{19,11},{28,... | collective-permute-start | bytes 2359304 | tf_op jit(solution)/shard_map/ppermute | solution.py:165
  382.6 30.5 %collective-permute-start.9 = (bf16[256,1536]{1,0:T(8,128)(2,1)S(1)}, bf16[256,1536]{1,0:T(8,128)(2,1)S(1)}, u32[]{:S(2)}, u32[]{:S(2)}) collective-permute-start(bf16[256,1536]{1,0:T(8,128)(2,1)S(1)} %get-tuple-element.186), channel_id=1, source_target_pairs={{0,8},{8,16},{1,9},{9,17},{2,10},{10,18},{3,11},{11,19},{4,12},{12... | collective-permute-start | bytes 2359304 | tf_op jit(solution)/shard_map/ppermute | solution.py:164
  385.6 27.5 %collective-permute-start.10 = (bf16[256,1536]{1,0:T(8,128)(2,1)S(1)}, bf16[256,1536]{1,0:T(8,128)(2,1)S(1)}, u32[]{:S(2)}, u32[]{:S(2)}) collective-permute-start(bf16[256,1536]{1,0:T(8,128)(2,1)S(1)} %get-tuple-element.187), channel_id=1, source_target_pairs={{24,16},{16,8},{25,17},{17,9},{26,18},{18,10},{27,19},{19,11},{28,... | collective-permute-start | bytes 2359304 | tf_op jit(solution)/shard_map/ppermute | solution.py:165
  386.3 31.9 %collective-permute-start.8 = (bf16[256,1536]{1,0:T(8,128)(2,1)S(1)}, bf16[256,1536]{1,0:T(8,128)(2,1)S(1)}, u32[]{:S(2)}, u32[]{:S(2)}) collective-permute-start(bf16[256,1536]{1,0:T(8,128)(2,1)S(1)} %get-tuple-element.188), channel_id=1, source_target_pairs={{0,8},{8,16},{1,9},{9,17},{2,10},{10,18},{3,11},{11,19},{4,12},{12... | collective-permute-start | bytes 2359304 | tf_op jit(solution)/shard_map/ppermute | solution.py:164
  413.1 58.9 %collective-permute-start.40 = (bf16[1536,1280]{1,0:T(8,128)(2,1)}, bf16[1536,1280]{1,0:T(8,128)(2,1)}, u32[]{:S(2)}, u32[]{:S(2)}) collective-permute-start(bf16[1536,1280]{1,0:T(8,128)(2,1)} %convolution_convert_fusion), channel_id=1, source_target_pairs={{0,1},{1,0},{2,3},{3,2},{4,5},{5,4},{6,7},{7,6},{8,9},{9,8},{10,11... | collective-permute-start | bytes 11796488 | tf_op jit(solution)/shard_map/ppermute | solution.py:239
  443.7 501.0 %reduce-scatter.6.cloned.1.call-start = ((), (), s32[]{:S(2)}) async-start(), calls=%async_computation.9 | async-start | bytes 4915200 | tf_op jit(solution)/shard_map/reduce_scatter | solution.py:241
  479.5 471.0 %reduce-scatter.14.cloned.1.call-start = ((), (), s32[]{:S(2)}) async-start(), calls=%async_computation.13 | async-start | bytes 7864320 | tf_op jit(solution)/shard_map/reduce_scatter | solution.py:241
  494.5 458.6 %reduce-scatter.12.cloned.1.call-start = ((), (), s32[]{:S(2)}) async-start(), calls=%async_computation.12 | async-start | bytes 7864320 | tf_op jit(solution)/shard_map/reduce_scatter | solution.py:241
  513.1 63.5 %collective-permute-start.14 = (bf16[256,1536]{1,0:T(8,128)(2,1)}, bf16[256,1536]{1,0:T(8,128)(2,1)}, u32[]{:S(2)}, u32[]{:S(2)}) collective-permute-start(bf16[256,1536]{1,0:T(8,128)(2,1)} %add_convert_fusion.19), channel_id=1, source_target_pairs={{0,8},{8,16},{16,24},{1,9},{9,17},{17,25},{2,10},{10,18},{18,26},{... | collective-permute-start | bytes 2359304 | tf_op jit(solution)/shard_map/ppermute | solution.py:164
  519.9 32.9 %collective-permute-start.23 = (bf16[256,1536]{1,0:T(8,128)(2,1)}, bf16[256,1536]{1,0:T(8,128)(2,1)}, u32[]{:S(2)}, u32[]{:S(2)}) collective-permute-start(bf16[256,1536]{1,0:T(8,128)(2,1)} %get-tuple-element.182), channel_id=1, source_target_pairs={{0,8},{1,9},{2,10},{3,11},{4,12},{5,13},{6,14},{7,15}} | collective-permute-start | bytes 2359304 | tf_op jit(solution)/shard_map/ppermute | solution.py:164
  523.0 31.1 %collective-permute-start.25 = (bf16[256,1536]{1,0:T(8,128)(2,1)}, bf16[256,1536]{1,0:T(8,128)(2,1)}, u32[]{:S(2)}, u32[]{:S(2)}) collective-permute-start(bf16[256,1536]{1,0:T(8,128)(2,1)} %get-tuple-element.181), channel_id=1, source_target_pairs={{24,16},{25,17},{26,18},{27,19},{28,20},{29,21},{30,22},{31,23}} | collective-permute-start | bytes 2359304 | tf_op jit(solution)/shard_map/ppermute | solution.py:165
  535.1 418.0 %reduce-scatter.10.cloned.1.call-start = ((), (), s32[]{:S(2)}) async-start(), calls=%async_computation.11 | async-start | bytes 7864320 | tf_op jit(solution)/shard_map/reduce_scatter | solution.py:241
  536.8 32.7 %collective-permute-start.22 = (bf16[256,1536]{1,0:T(8,128)(2,1)S(1)}, bf16[256,1536]{1,0:T(8,128)(2,1)S(1)}, u32[]{:S(2)}, u32[]{:S(2)}) collective-permute-start(bf16[256,1536]{1,0:T(8,128)(2,1)S(1)} %get-tuple-element.184), channel_id=1, source_target_pairs={{0,8},{1,9},{2,10},{3,11},{4,12},{5,13},{6,14},{7,15}} | collective-permute-start | bytes 2359304 | tf_op jit(solution)/shard_map/ppermute | solution.py:164
  538.2 32.6 %collective-permute-start.24 = (bf16[256,1536]{1,0:T(8,128)(2,1)S(1)}, bf16[256,1536]{1,0:T(8,128)(2,1)S(1)}, u32[]{:S(2)}, u32[]{:S(2)}) collective-permute-start(bf16[256,1536]{1,0:T(8,128)(2,1)S(1)} %get-tuple-element.183), channel_id=1, source_target_pairs={{24,16},{25,17},{26,18},{27,19},{28,20},{29,21},{30,22},{31,23}} | collective-permute-start | bytes 2359304 | tf_op jit(solution)/shard_map/ppermute | solution.py:165
  552.8 29.8 %collective-permute-start.15 = (bf16[256,1536]{1,0:T(8,128)(2,1)S(1)}, bf16[256,1536]{1,0:T(8,128)(2,1)S(1)}, u32[]{:S(2)}, u32[]{:S(2)}) collective-permute-start(bf16[256,1536]{1,0:T(8,128)(2,1)S(1)} %copy-done.30), channel_id=1, source_target_pairs={{24,16},{16,8},{8,0},{25,17},{17,9},{9,1},{26,18},{18,10},{10,2},{... | collective-permute-start | bytes 2359304 | tf_op jit(solution)/shard_map/ppermute | solution.py:165
  554.1 32.3 %collective-permute-start.12 = (bf16[256,1536]{1,0:T(8,128)(2,1)S(1)}, bf16[256,1536]{1,0:T(8,128)(2,1)S(1)}, u32[]{:S(2)}, u32[]{:S(2)}) collective-permute-start(bf16[256,1536]{1,0:T(8,128)(2,1)S(1)} %copy-done.29), channel_id=1, source_target_pairs={{0,8},{8,16},{16,24},{1,9},{9,17},{17,25},{2,10},{10,18},{18,26},{... | collective-permute-start | bytes 2359304 | tf_op jit(solution)/shard_map/ppermute | solution.py:164
  569.5 22.1 %collective-permute-start.13 = (bf16[256,1536]{1,0:T(8,128)(2,1)S(1)}, bf16[256,1536]{1,0:T(8,128)(2,1)S(1)}, u32[]{:S(2)}, u32[]{:S(2)}) collective-permute-start(bf16[256,1536]{1,0:T(8,128)(2,1)S(1)} %copy-done.28), channel_id=1, source_target_pairs={{24,16},{16,8},{8,0},{25,17},{17,9},{9,1},{26,18},{18,10},{10,2},{... | collective-permute-start | bytes 2359304 | tf_op jit(solution)/shard_map/ppermute | solution.py:165
  570.8 108.1 %collective-permute-start.42 = (bf16[1536,2048]{1,0:T(8,128)(2,1)}, bf16[1536,2048]{1,0:T(8,128)(2,1)}, u32[]{:S(2)}, u32[]{:S(2)}) collective-permute-start(bf16[1536,2048]{1,0:T(8,128)(2,1)} %convolution_convert_fusion.3), channel_id=1, source_target_pairs={{0,1},{1,0},{2,3},{3,2},{4,5},{5,4},{6,7},{7,6},{8,9},{9,8},{10,11... | collective-permute-start | bytes 18874376 | tf_op jit(solution)/shard_map/ppermute | solution.py:239
  576.6 26.7 %collective-permute-start.27 = (bf16[256,1536]{1,0:T(8,128)(2,1)}, bf16[256,1536]{1,0:T(8,128)(2,1)}, u32[]{:S(2)}, u32[]{:S(2)}) collective-permute-start(bf16[256,1536]{1,0:T(8,128)(2,1)} %get-tuple-element.178), channel_id=1, source_target_pairs={{0,8},{8,16},{1,9},{9,17},{2,10},{10,18},{3,11},{11,19},{4,12},{12... | collective-permute-start | bytes 2359304 | tf_op jit(solution)/shard_map/ppermute | solution.py:164
  582.6 26.3 %collective-permute-start.29 = (bf16[256,1536]{1,0:T(8,128)(2,1)}, bf16[256,1536]{1,0:T(8,128)(2,1)}, u32[]{:S(2)}, u32[]{:S(2)}) collective-permute-start(bf16[256,1536]{1,0:T(8,128)(2,1)} %get-tuple-element.177), channel_id=1, source_target_pairs={{24,16},{16,8},{25,17},{17,9},{26,18},{18,10},{27,19},{19,11},{28,... | collective-permute-start | bytes 2359304 | tf_op jit(solution)/shard_map/ppermute | solution.py:165
  586.4 33.8 %collective-permute-start.26 = (bf16[256,1536]{1,0:T(8,128)(2,1)}, bf16[256,1536]{1,0:T(8,128)(2,1)}, u32[]{:S(2)}, u32[]{:S(2)}) collective-permute-start(bf16[256,1536]{1,0:T(8,128)(2,1)} %get-tuple-element.180), channel_id=1, source_target_pairs={{0,8},{8,16},{1,9},{9,17},{2,10},{10,18},{3,11},{11,19},{4,12},{12... | collective-permute-start | bytes 2359304 | tf_op jit(solution)/shard_map/ppermute | solution.py:164
  591.7 28.5 %collective-permute-start.28 = (bf16[256,1536]{1,0:T(8,128)(2,1)}, bf16[256,1536]{1,0:T(8,128)(2,1)}, u32[]{:S(2)}, u32[]{:S(2)}) collective-permute-start(bf16[256,1536]{1,0:T(8,128)(2,1)} %get-tuple-element.179), channel_id=1, source_target_pairs={{24,16},{16,8},{25,17},{17,9},{26,18},{18,10},{27,19},{19,11},{28,... | collective-permute-start | bytes 2359304 | tf_op jit(solution)/shard_map/ppermute | solution.py:165
  603.4 107.3 %collective-permute-start.16 = (bf16[256,3072]{1,0:T(8,128)(2,1)}, bf16[256,3072]{1,0:T(8,128)(2,1)}, u32[]{:S(2)}, u32[]{:S(2)}) collective-permute-start(bf16[256,3072]{1,0:T(8,128)(2,1)} %add_convert_fusion.12), channel_id=1, source_target_pairs={{0,8},{8,16},{16,24},{1,9},{9,17},{17,25},{2,10},{10,18},{18,26},{... | collective-permute-start | bytes 4718600 | tf_op jit(solution)/shard_map/ppermute | solution.py:175
  608.9 100.5 %collective-permute-start.17 = (bf16[256,3072]{1,0:T(8,128)(2,1)}, bf16[256,3072]{1,0:T(8,128)(2,1)}, u32[]{:S(2)}, u32[]{:S(2)}) collective-permute-start(bf16[256,3072]{1,0:T(8,128)(2,1)} %add_convert_fusion.12), channel_id=1, source_target_pairs={{24,16},{16,8},{8,0},{25,17},{17,9},{9,1},{26,18},{18,10},{10,2},{... | collective-permute-start | bytes 4718600 | tf_op jit(solution)/shard_map/ppermute | solution.py:176
  621.8 48.2 %collective-permute-start.32 = (bf16[256,1536]{1,0:T(8,128)(2,1)S(1)}, bf16[256,1536]{1,0:T(8,128)(2,1)S(1)}, u32[]{:S(2)}, u32[]{:S(2)}) collective-permute-start(bf16[256,1536]{1,0:T(8,128)(2,1)S(1)} %add_convert_fusion.15), channel_id=1, source_target_pairs={{0,8},{8,16},{16,24},{1,9},{9,17},{17,25},{2,10},{10,18},{18,26},{... | collective-permute-start | bytes 2359304 | tf_op jit(solution)/shard_map/ppermute | solution.py:164
  633.2 42.0 %collective-permute-start.33 = (bf16[256,1536]{1,0:T(8,128)(2,1)S(1)}, bf16[256,1536]{1,0:T(8,128)(2,1)S(1)}, u32[]{:S(2)}, u32[]{:S(2)}) collective-permute-start(bf16[256,1536]{1,0:T(8,128)(2,1)S(1)} %add_convert_fusion.14), channel_id=1, source_target_pairs={{24,16},{16,8},{8,0},{25,17},{17,9},{9,1},{26,18},{18,10},{10,2},{... | collective-permute-start | bytes 2359304 | tf_op jit(solution)/shard_map/ppermute | solution.py:165
  703.4 135.6 %collective-permute-start.35 = (bf16[256,3072]{1,0:T(8,128)(2,1)}, bf16[256,3072]{1,0:T(8,128)(2,1)S(1)}, u32[]{:S(2)}, u32[]{:S(2)}) collective-permute-start(bf16[256,3072]{1,0:T(8,128)(2,1)} %fusion.27), channel_id=1, source_target_pairs={{24,16},{16,8},{8,0},{25,17},{17,9},{9,1},{26,18},{18,10},{10,2},{... | collective-permute-start | bytes 4718600 | tf_op jit(solution)/shard_map/ppermute | solution.py:176
  704.7 135.7 %collective-permute-start.34 = (bf16[256,3072]{1,0:T(8,128)(2,1)}, bf16[256,3072]{1,0:T(8,128)(2,1)S(1)}, u32[]{:S(2)}, u32[]{:S(2)}) collective-permute-start(bf16[256,3072]{1,0:T(8,128)(2,1)} %fusion.27), channel_id=1, source_target_pairs={{0,8},{8,16},{16,24},{1,9},{9,17},{17,25},{2,10},{10,18},{18,26},{... | collective-permute-start | bytes 4718600 | tf_op jit(solution)/shard_map/ppermute | solution.py:175
  709.4 131.8 %collective-permute-start.18 = (bf16[256,3072]{1,0:T(8,128)(2,1)}, bf16[256,3072]{1,0:T(8,128)(2,1)}, u32[]{:S(2)}, u32[]{:S(2)}) collective-permute-start(bf16[256,3072]{1,0:T(8,128)(2,1)} %collective-permute-done.17), channel_id=1, source_target_pairs={{16,8},{8,0},{17,9},{9,1},{18,10},{10,2},{19,11},{11,3},{20,12},{1... | collective-permute-start | bytes 4718600 | tf_op jit(solution)/shard_map/ppermute | solution.py:176
  710.7 134.7 %collective-permute-start.20 = (bf16[256,3072]{1,0:T(8,128)(2,1)}, bf16[256,3072]{1,0:T(8,128)(2,1)}, u32[]{:S(2)}, u32[]{:S(2)}) collective-permute-start(bf16[256,3072]{1,0:T(8,128)(2,1)} %collective-permute-done.16), channel_id=1, source_target_pairs={{8,16},{16,24},{9,17},{17,25},{10,18},{18,26},{11,19},{19,27},{12,... | collective-permute-start | bytes 4718600 | tf_op jit(solution)/shard_map/ppermute | solution.py:175
  839.0 39.1 %collective-permute-start.36 = (bf16[256,3072]{1,0:T(8,128)(2,1)S(1)}, bf16[256,3072]{1,0:T(8,128)(2,1)S(1)}, u32[]{:S(2)}, u32[]{:S(2)}) collective-permute-start(bf16[256,3072]{1,0:T(8,128)(2,1)S(1)} %collective-permute-done.35), channel_id=1, source_target_pairs={{16,8},{8,0},{17,9},{9,1},{18,10},{10,2},{19,11},{11,3},{20,12},{1... | collective-permute-start | bytes 4718600 | tf_op jit(solution)/shard_map/ppermute | solution.py:176
  840.3 39.1 %collective-permute-start.38 = (bf16[256,3072]{1,0:T(8,128)(2,1)S(1)}, bf16[256,3072]{1,0:T(8,128)(2,1)S(1)}, u32[]{:S(2)}, u32[]{:S(2)}) collective-permute-start(bf16[256,3072]{1,0:T(8,128)(2,1)S(1)} %collective-permute-done.34), channel_id=1, source_target_pairs={{8,16},{16,24},{9,17},{17,25},{10,18},{18,26},{11,19},{19,27},{12,... | collective-permute-start | bytes 4718600 | tf_op jit(solution)/shard_map/ppermute | solution.py:175
  841.1 70.8 %collective-permute-start.19 = (bf16[256,3072]{1,0:T(8,128)(2,1)}, bf16[256,3072]{1,0:T(8,128)(2,1)S(1)}, u32[]{:S(2)}, u32[]{:S(2)}) collective-permute-start(bf16[256,3072]{1,0:T(8,128)(2,1)} %collective-permute-done.18), channel_id=1, source_target_pairs={{8,0},{9,1},{10,2},{11,3},{12,4},{13,5},{14,6},{15,7}} | collective-permute-start | bytes 4718600 | tf_op jit(solution)/shard_map/ppermute | solution.py:176
  845.4 69.0 %collective-permute-start.21 = (bf16[256,3072]{1,0:T(8,128)(2,1)}, bf16[256,3072]{1,0:T(8,128)(2,1)S(1)}, u32[]{:S(2)}, u32[]{:S(2)}) collective-permute-start(bf16[256,3072]{1,0:T(8,128)(2,1)} %collective-permute-done.20), channel_id=1, source_target_pairs={{16,24},{17,25},{18,26},{19,27},{20,28},{21,29},{22,30},{23,31}} | collective-permute-start | bytes 4718600 | tf_op jit(solution)/shard_map/ppermute | solution.py:175
  878.2 61.3 %collective-permute-start.37 = (bf16[256,3072]{1,0:T(8,128)(2,1)S(1)}, bf16[256,3072]{1,0:T(8,128)(2,1)S(1)}, u32[]{:S(2)}, u32[]{:S(2)}) collective-permute-start(bf16[256,3072]{1,0:T(8,128)(2,1)S(1)} %collective-permute-done.36), channel_id=1, source_target_pairs={{8,0},{9,1},{10,2},{11,3},{12,4},{13,5},{14,6},{15,7}} | collective-permute-start | bytes 4718600 | tf_op jit(solution)/shard_map/ppermute | solution.py:176
  879.5 63.4 %collective-permute-start.39 = (bf16[256,3072]{1,0:T(8,128)(2,1)S(1)}, bf16[256,3072]{1,0:T(8,128)(2,1)S(1)}, u32[]{:S(2)}, u32[]{:S(2)}) collective-permute-start(bf16[256,3072]{1,0:T(8,128)(2,1)S(1)} %collective-permute-done.38), channel_id=1, source_target_pairs={{16,24},{17,25},{18,26},{19,27},{20,28},{21,29},{22,30},{23,31}} | collective-permute-start | bytes 4718600 | tf_op jit(solution)/shard_map/ppermute | solution.py:175
  (60 other events, 906.9 us)
Sparse Core Ops, SparseCore 0:
  13.3 72.6 all-gather.7
  87.8 70.0 all-gather.9
  159.7 70.0 all-gather.11
  231.4 69.8 all-gather.13
  443.8 36.9 reduce-scatter.7
  483.7 50.3 reduce-scatter.5
  537.1 70.0 reduce-scatter.13
  610.7 70.0 reduce-scatter.11
  690.1 71.8 reduce-scatter.9

commit v2 on v1

--- a/solution.py
+++ b/solution.py
@@ -133,6 +133,18 @@
     return lax.all_gather(shard, 'fsdp', axis=0, tiled=True, axis_index_groups=CORE_GROUPS)
 
 
+def neighbours(bit):
+    return [(i, i ^ bit) for i in range(8)]
+
+
+def place(pieces, slots):
+    zero = jnp.uint32(0)
+    whole = jnp.zeros((len(pieces),) + pieces[0].shape, pieces[0].dtype)
+    for piece, slot in zip(pieces, slots):
+        whole = lax.dynamic_update_slice(whole, piece[None], (slot, zero, zero))
+    return whole.reshape((-1,) + pieces[0].shape[1:])
+
+
 def with_sibling(mine):
     return mine, lax.ppermute(mine, 'fsdp', SIBLING)
 
@@ -211,9 +223,13 @@
         attn_shard = jnp.concatenate([w_query, w_key, w_value, w_out.T], axis=1)
         attn_mine = gather_mine(attn_shard)
         gate_mine = gather_mine(w_gate)
-        up_mine = gather_mine(w_up)
-        down_mine = gather_mine(w_down.T)
-        attn_w = with_sibling(attn_mine)
+        up_y, up_x = lax.ppermute(w_up, 'fsdp', neighbours(4)), lax.ppermute(w_up, 'fsdp', neighbours(2))
+        up_far = lax.ppermute(up_y, 'fsdp', neighbours(2))
+        down_shard = after(w_down.T, up_y)
+        down_y, down_x = lax.ppermute(down_shard, 'fsdp', neighbours(4)), lax.ppermute(down_shard, 'fsdp', neighbours(2))
+        down_far = lax.ppermute(down_y, 'fsdp', neighbours(2))
+        chip = (fsdp // 2).astype(jnp.uint32)
+        slots = [chip ^ jnp.uint32(k) for k in range(4)]
 
         small = jnp.concatenate([ln_weight, q_norm.reshape(-1), k_norm.reshape(-1)])
         small_all = lax.all_gather(small, 'fsdp', axis=0, tiled=False).astype(F32)
@@ -241,26 +257,27 @@
             return lax.psum_scatter(total, 'fsdp', scatter_dimension=0, tiled=True, axis_index_groups=CORE_GROUPS)
 
         h_pair, g_pair = (h_m, h_o), (g_m, g_o)
-        qkv_w = tuple(part[:, :qkv_width] for part in attn_w)
-        out_w = tuple(part[:, qkv_width:] for part in attn_w)
-
-        qkv = contract(h_pair, qkv_w).astype(BF16)
-        grad_attn = contract(g_pair, out_w).astype(BF16)
         lane = lax.broadcasted_iota(jnp.int32, (1, head_dim), 1)
         inv_freq = ROPE_BASE ** (-((lane // 2) * 2).astype(F32) / head_dim)
         angles = positions.reshape(tokens, 1).astype(F32) * inv_freq
         cosine = jnp.cos(angles)
         sine = jnp.where(lane % 2 == 0, -1.0, 1.0) * jnp.sin(angles)
+        attn_w = with_sibling(after(attn_mine, (h_pair, g_pair, cosine, up_y)))
+        qkv_w = tuple(part[:, :qkv_width] for part in attn_w)
+        out_w = tuple(part[:, qkv_width:] for part in attn_w)
+
+        qkv = contract((after(h_m, up_y), h_o), qkv_w).astype(BF16)
+        grad_attn = contract(g_pair, out_w).astype(BF16)
         attn_out, grad_qkv, norm_part = attention(qkv, grad_attn, cosine, sine, norm_full, batch, seq_len, heads, kv_heads, head_dim)
-        attn_part = expand(attn_out, out_w)
+        attn_part = expand(after(attn_out, down_y), out_w)
         attn_dh = expand(grad_qkv, qkv_w)
 
 
-        gate_w = with_sibling(after(gate_mine, attn_part))
+        up_w = with_sibling(place(after((w_up, up_x, up_y, up_far), attn_out), slots))
+        up_proj = contract((after(h_m, attn_part), h_o), up_w).astype(BF16)
+        gate_w = with_sibling(after(gate_mine, up_proj))
         gate = contract(h_pair, gate_w).astype(BF16)
-        up_w = with_sibling(after(up_mine, gate))
-        up_proj = contract(h_pair, up_w).astype(BF16)
-        down_w = with_sibling(after(down_mine, up_proj))
+        down_w = with_sibling(place(after((down_shard, down_x, down_y, down_far), gate), slots))
         gate_f32, up_f32 = gate.astype(F32), up_proj.astype(F32)
         sigma = jax.nn.sigmoid(gate_f32)
         gated_act = (gate_f32 * sigma * up_f32).astype(BF16)
@@ -303,12 +320,10 @@
         ln_part = jnp.sum(grad_normed * xc_hat, axis=0).reshape(n_fsdp, width)
         all_heads = heads + kv_heads
         head_part = norm_part.reshape(all_heads, n_fsdp, dims_part).transpose(1, 0, 2).reshape(n_fsdp, all_heads * dims_part)
-        small_parts = lax.all_gather(jnp.concatenate([ln_part, head_part], axis=1), ('fsdp', 'tp'), axis=0, tiled=False)
-        small_own = lax.dynamic_index_in_dim(small_parts, fsdp, 1, keepdims=False)
-        grad_ln = jnp.sum(small_own[:, :width], axis=0)
-        head_own = small_own[:, width:].reshape(n_fsdp, n_tp, all_heads * dims_part)
-        head_own = jnp.sum(lax.dynamic_index_in_dim(head_own, tp[0], 1, keepdims=False), axis=0)
-        norm_own = head_own.reshape(all_heads, dims_part)
+        small_parts = lax.all_gather(jnp.concatenate([ln_part, head_part], axis=1), 'fsdp', axis=0, tiled=False)
+        small_own = jnp.sum(lax.dynamic_index_in_dim(small_parts, fsdp, 1, keepdims=False), axis=0)
+        norm_own = small_own[width:].reshape(all_heads, dims_part)
+        grad_ln = jnp.sum(lax.all_gather(small_own[:width], 'tp', axis=0, tiled=False), axis=0)
 
         return (layer_out.reshape(hidden.shape), grad_hidden.reshape(hidden.shape), grad_ln, grad_wqkv[:, :q_width], grad_wqkv[:, q_width:q_width + kv_width],
                 grad_wqkv[:, q_width + kv_width:], grad_wout.T, grad_wgate, grad_wup, grad_wdown.T,

time: 970 us -> 1030 us (1.062)
  the two profiles are of different devices: /device:TPU:0 before, /device:TPU:26 now
where the time goes in v2:
time: 1030 us; the launch traced here: 1020 us
  waiting for transfers between devices  308 us (30%)
  matrix products  276 us (27%)
  blocking collectives  152 us (15%)
  starting transfers between devices  105 us (10%)
  other arithmetic  76.7 us (7%)
  local copies, waits for them, and re-layouts  57.9 us (6%)
  Pallas kernels  30.2 us (3%)
  between operations  16 us (2%)
    dot_general x30, matrix products, mm(): return jnp.einsum(form, left, right, preferred_element_type=F32)  276 us
    all_gather x1, blocking collectives, device_step(): lax.all_gather(small_own[:width], 'tp', axis=0, tiled=False)  87.1 us
    ppermute x1, waiting for transfers between devices, device_step(): up_far = lax.ppermute(up_y, 'fsdp', neighbours(2))  60.7 us
    ppermute x12, starting transfers between devices, chain_sum(): from_right[h] = lax.ppermute(go_left, 'tp', left)  56.9 us
    all_gather x1, blocking collectives, device_step(): small_all = lax.all_gather(small, 'fsdp', axis=0, tiled=False).astype(F32)  56.1 us
    ppermute x6, waiting for transfers between devices, chain_gather(): lax.ppermute(go_right, 'tp', [(i, i + 1) for i in range(step, n - 1)])  54.7 us
    ppermute x12, waiting for transfers between devices, chain_sum(): from_right[h] = lax.ppermute(go_left, 'tp', left)  51.4 us
    ppermute x1, waiting for transfers between devices, device_step(): lax.ppermute(down_shard, 'fsdp', neighbours(4))  36.4 us
  transfers between devices with their start and end apart: 58, of which 19 were waited for; matrix products, arithmetic and copies ran while one was open for 38% of the time, Pallas kernels for 3%

profile of v2, /device:TPU:26, one launch (start us, length us, event | category | flops | bytes accessed | tf_op | source)
XLA Modules:
  0.0 1022.7 jit_solution(12443242986051494731)
XLA Ops:
  15.1 56.1 %all-gather.3 = bf16[8,1,512]{2,1,0:T(2,128)(2,1)S(1)} all-gather(bf16[1,1,512]{2,1,0:T(2,128)(2,1)S(1)} %reshape.256), channel_id=2, replica_groups=mesh['tp'=4,'fsdp'=8] {'fsdp'}, dimensions={0}, use_global_device_ids=true | all-gather | bytes 9216 | tf_op jit(solution)/shard_map/all_gather | solution.py:235
  92.1 9.1 all-gather.8.cloned.1.call-done
  104.0 7.7 collective-permute-done.1
  111.7 6.1 fusion.32
  117.8 6.5 fusion.20
  131.5 30.2 %attention.1 = (bf16[1024,768]{1,0:T(8,128)(2,1)S(1)}, bf16[1024,1280]{1,0:T(8,128)(2,1)S(1)}, f32[8,128]{1,0:T(8,128)S(1)}) custom-call(bf16[1024,1280]{1,0:T(8,128)(2,1)S(1)} %add_convert_fusion.10.qkv_ref, bf16[1024,768]{1,0:T(8,128)(2,1)S(1)} %add_convert_fusion.13.ga_ref, f32[1024,128]{1,0:T(8,128)S(1)} %get-tuple-element.220.cos_ref, ...), custom_call_target="tpu_custom_call" | custom-call | flops 2415919104 | bytes 13107200 | tf_op jit(solution)/shard_map/attention/pallas_call | solution.py:99
  161.8 60.7 %collective-permute-done.4 = bf16[384,2048]{1,0:T(8,128)(2,1)S(1)} collective-permute-done((bf16[384,2048]{1,0:T(8,128)(2,1)}, bf16[384,2048]{1,0:T(8,128)(2,1)S(1)}, u32[]{:S(2)}, u32[]{:S(2)}) %collective-permute-start.4) | collective-permute-done | bytes 1572896 | tf_op jit(solution)/shard_map/ppermute | solution.py:227
  238.9 36.4 %collective-permute-done.2 = bf16[384,2048]{1,0:T(8,128)(2,1)} collective-permute-done((bf16[384,2048]{1,0:T(8,128)(2,1)}, bf16[384,2048]{1,0:T(8,128)(2,1)}, u32[]{:S(2)}, u32[]{:S(2)}) %collective-permute-start.2) | collective-permute-done | bytes 1572896 | tf_op jit(solution)/shard_map/ppermute | solution.py:229
  275.2 6.1 fusion.34
  281.3 6.3 fusion.30
  287.6 9.1 fusion.63
  296.8 11.3 %add_convert_fusion.4 = bf16[1024,2048]{1,0:T(8,128)(2,1)} fusion(f32[1024,2048]{1,0:T(8,128)S(1)} %fusion.63, bf16[1024,1536]{1,0:T(8,128)(2,1)S(1)} %copy-done.16, bf16[1536,2048]{1,0:T(8,128)(2,1)} %collective-permute-done.5), kind=kOutput, calls=%fused_computation.27 | convolution fusion | flops 6446645248 | bytes 22020096 | tf_op jit(solution)/shard_map/td,de->te/dot_general | solution.py:21
  310.3 11.7 %fusion.64 = f32[1024,2048]{1,0:T(8,128)} fusion(bf16[1024,1536]{1,0:T(8,128)(2,1)} %get-tuple-element.67, bf16[1536,2048]{1,0:T(8,128)(2,1)} %all-gather.10.cloned.1.call-done), kind=kOutput, calls=%fused_computation.188 | convolution fusion | flops 6442450944 | bytes 17825792 | tf_op jit(solution)/shard_map/td,de->te/dot_general | solution.py:21
  322.0 14.6 %fusion.5 = (bf16[1024,2048]{1,0:T(8,128)(2,1)}, bf16[1024,2048]{1,0:T(8,128)(2,1)}) fusion(bf16[1024,2048]{1,0:T(8,128)(2,1)S(1)} %copy-done.47, f32[1024,2048]{1,0:T(8,128)} %fusion.64, bf16[1024,1536]{1,0:T(8,128)(2,1)S(1)} %copy-done.17, bf16[1536,2048]{1,0:T(8,128)(2,1)S(1)} %collective-permute-done.6), kind=kOutput, calls=%fused_computation.16 | convolution fusion | flops 6463422464 | bytes 30408704 | tf_op jit(solution)/shard_map/td,de->te/dot_general | solution.py:21
  336.6 8.9 collective-permute-done.7
  345.5 33.2 %collective-permute-done.8 = bf16[384,2048]{1,0:T(8,128)(2,1)S(1)} collective-permute-done((bf16[384,2048]{1,0:T(8,128)(2,1)}, bf16[384,2048]{1,0:T(8,128)(2,1)S(1)}, u32[]{:S(2)}, u32[]{:S(2)}) %collective-permute-start.8) | collective-permute-done | bytes 1572896 | tf_op jit(solution)/shard_map/ppermute | solution.py:230
  388.7 8.3 fusion.18
  397.0 11.1 %add_convert_fusion.9 = bf16[1024,1536]{1,0:T(8,128)(2,1)S(1)} fusion(f32[1024,1536]{1,0:T(8,128)} %fusion.34, bf16[1024,2048]{1,0:T(8,128)(2,1)S(1)} %copy-done.48, bf16[1536,2048]{1,0:T(8,128)(2,1)} %bitcast.16), kind=kOutput, calls=%fused_computation.36 | convolution fusion | flops 6445596672 | bytes 19922944 | tf_op jit(solution)/shard_map/te,de->td/dot_general | solution.py:21
  413.5 11.2 %fusion.65 = f32[1024,2048]{1,0:T(8,128)} fusion(bf16[1024,1536]{1,0:T(8,128)(2,1)S(1)} %copy-done.22, bf16[1536,2048]{1,0:T(8,128)(2,1)} %bitcast.16), kind=kOutput, calls=%fused_computation.189 | convolution fusion | flops 6442450944 | bytes 17825792 | tf_op jit(solution)/shard_map/td,de->te/dot_general | solution.py:21
  424.7 9.0 add_convert_fusion.8
  443.1 17.8 %fusion.8 = (bf16[1024,2048]{1,0:T(8,128)(2,1)}, bf16[1024,2048]{1,0:T(8,128)(2,1)}) fusion(bf16[1024,2048]{1,0:T(8,128)(2,1)} %add_convert_fusion.4, bf16[1024,2048]{1,0:T(8,128)(2,1)} %get-tuple-element.222, f32[1024,2048]{1,0:T(8,128)} %fusion.65, bf16[1024,1536]{1,0:T(8,128)(2,1)} %get-tuple-element.88, bf16[1536,2048]{1,0:T(8,128)(2,1)} %collective-permute-done.10), kind=kOutput, calls=%fused_computation.19 | convolution fusion | flops 6476005376 | bytes 34603008 | tf_op jit(solution)/shard_map/td,de->te/dot_general | solution.py:21
  460.9 5.9 convolution_convert_fusion
  477.9 10.9 %fusion.66 = f32[1024,1536]{1,0:T(8,128)} fusion(bf16[1024,2048]{1,0:T(8,128)(2,1)S(1)} %copy-done.43, bf16[1536,2048]{1,0:T(8,128)(2,1)} %all-gather.10.cloned.1.call-done), kind=kOutput, calls=%fused_computation.190 | convolution fusion | flops 6442450944 | bytes 16777216 | tf_op jit(solution)/shard_map/te,de->td/dot_general | solution.py:21
  488.8 8.6 fusion.68
  497.4 7.5 collective-permute-done.16
  511.0 13.1 %add_convert_fusion.6 = bf16[1024,1536]{1,0:T(8,128)(2,1)} fusion(f32[1024,1536]{1,0:T(8,128)} %fusion.18, f32[1024,1536]{1,0:T(8,128)} %fusion.68, bf16[1024,2048]{1,0:T(8,128)(2,1)S(1)} %copy-done.45, bf16[1536,2048]{1,0:T(8,128)(2,1)} %collective-permute-done.5), kind=kOutput, calls=%fused_computation.33 | convolution fusion | flops 6447169536 | bytes 26214400 | tf_op jit(solution)/shard_map/te,de->td/dot_general | solution.py:21
  529.4 10.5 %fusion.67 = f32[1024,1536]{1,0:T(8,128)S(1)} fusion(bf16[1024,2048]{1,0:T(8,128)(2,1)} %get-tuple-element.110, bf16[1536,2048]{1,0:T(8,128)(2,1)} %bitcast.11), kind=kOutput, calls=%fused_computation.191 | convolution fusion | flops 6442450944 | bytes 16777216 | tf_op jit(solution)/shard_map/te,de->td/dot_general | solution.py:21
  540.0 9.3 add_convert_fusion.7
  549.2 8.8 convolution_convert_fusion.1
  558.0 7.8 add_convert_fusion.5
  568.5 12.0 %add_convert_fusion = bf16[1536,2048]{1,0:T(8,128)(2,1)} fusion(bf16[1536,2048]{1,0:T(8,128)(2,1)} %collective-permute-done.50, bf16[1024,1536]{1,0:T(8,128)(2,1)S(1)} %copy-done.24, bf16[1024,2048]{1,0:T(8,128)(2,1)} %get-tuple-element.111), kind=kOutput, calls=%fused_computation.11 | convolution fusion | flops 6451888128 | bytes 19922944 | tf_op jit(solution)/shard_map/td,te->de/dot_general | solution.py:21
  582.4 11.1 %convolution_convert_fusion.2 = bf16[1536,2048]{1,0:T(8,128)(2,1)} fusion(bf16[1024,1536]{1,0:T(8,128)(2,1)S(1)} %copy-done.19, bf16[1024,2048]{1,0:T(8,128)(2,1)} %get-tuple-element.110), kind=kOutput, calls=%fused_computation.31 | convolution fusion | flops 6445596672 | bytes 13631488 | tf_op jit(solution)/shard_map/td,te->de/dot_general | solution.py:21
  603.5 6.2 collective-permute-start.31
  609.7 10.7 %add_convert_fusion.1 = bf16[1536,2048]{1,0:T(8,128)(2,1)} fusion(bf16[1536,2048]{1,0:T(8,128)(2,1)} %collective-permute-done.49, bf16[1024,1536]{1,0:T(8,128)(2,1)S(1)} %copy-done.13, bf16[1024,2048]{1,0:T(8,128)(2,1)S(1)} %copy-done.46), kind=kOutput, calls=%fused_computation.12 | convolution fusion | flops 6451888128 | bytes 19922944 | tf_op jit(solution)/shard_map/td,te->de/dot_general | solution.py:21
  624.5 11.1 %convolution_convert_fusion.3 = bf16[1536,2048]{1,0:T(8,128)(2,1)} fusion(bf16[1024,1536]{1,0:T(8,128)(2,1)S(1)} %copy-done.20, bf16[1024,2048]{1,0:T(8,128)(2,1)} %get-tuple-element.109), kind=kOutput, calls=%fused_computation.32 | convolution fusion | flops 6445596672 | bytes 13631488 | tf_op jit(solution)/shard_map/td,te->de/dot_general | solution.py:21
  638.3 10.2 collective-permute-start.19
  660.7 10.5 %collective-permute-start.35 = (bf16[256,1536]{1,0:T(8,128)(2,1)}, bf16[256,1536]{1,0:T(8,128)(2,1)}, u32[]{:S(2)}, u32[]{:S(2)}) collective-permute-start(bf16[256,1536]{1,0:T(8,128)(2,1)} %get-tuple-element.199), channel_id=1, source_target_pairs={{24,16},{16,8},{25,17},{17,9},{26,18},{18,10},{27,19},{19,11},{28,... | collective-permute-start | bytes 2359304 | tf_op jit(solution)/shard_map/ppermute | solution.py:177
  694.5 5.5 collective-permute-start.23
  700.0 11.3 %collective-permute-done.34 = bf16[256,1536]{1,0:T(8,128)(2,1)} collective-permute-done((bf16[256,1536]{1,0:T(8,128)(2,1)}, bf16[256,1536]{1,0:T(8,128)(2,1)}, u32[]{:S(2)}, u32[]{:S(2)}) %collective-permute-start.34) | collective-permute-done | bytes 786464 | tf_op jit(solution)/shard_map/ppermute | solution.py:177
  725.7 16.7 %collective-permute-done.38 = bf16[256,1536]{1,0:T(8,128)(2,1)S(1)} collective-permute-done((bf16[256,1536]{1,0:T(8,128)(2,1)S(1)}, bf16[256,1536]{1,0:T(8,128)(2,1)S(1)}, u32[]{:S(2)}, u32[]{:S(2)}) %collective-permute-start.38) | collective-permute-done | bytes 786464 | tf_op jit(solution)/shard_map/ppermute | solution.py:176
  743.7 17.0 %collective-permute-done.39 = bf16[256,1536]{1,0:T(8,128)(2,1)S(1)} collective-permute-done((bf16[256,1536]{1,0:T(8,128)(2,1)S(1)}, bf16[256,1536]{1,0:T(8,128)(2,1)S(1)}, u32[]{:S(2)}, u32[]{:S(2)}) %collective-permute-start.39) | collective-permute-done | bytes 786464 | tf_op jit(solution)/shard_map/ppermute | solution.py:177
  768.3 11.0 %add_convert_fusion.2 = bf16[1536,2048]{1,0:T(8,128)(2,1)} fusion(bf16[1536,2048]{1,0:T(8,128)(2,1)} %collective-permute-done.48, bf16[1024,1536]{1,0:T(8,128)(2,1)S(1)} %copy-done.14, bf16[1024,2048]{1,0:T(8,128)(2,1)S(1)} %copy-done.44), kind=kOutput, calls=%fused_computation.13 | convolution fusion | flops 6451888128 | bytes 19922944 | tf_op jit(solution)/shard_map/td,te->de/dot_general | solution.py:21
  798.4 26.8 %collective-permute-done.41 = bf16[256,3072]{1,0:T(8,128)(2,1)S(1)} collective-permute-done((bf16[256,3072]{1,0:T(8,128)(2,1)}, bf16[256,3072]{1,0:T(8,128)(2,1)S(1)}, u32[]{:S(2)}, u32[]{:S(2)}) %collective-permute-start.41) | collective-permute-done | bytes 1572896 | tf_op jit(solution)/shard_map/ppermute | solution.py:188
  827.0 6.2 collective-permute-done.40
  836.3 8.6 all-gather.1
  845.1 87.1 %all-gather.4 = f32[4,1,384]{2,1,0:T(1,128)S(1)} all-gather(f32[1,1,384]{2,1,0:T(1,128)S(1)} %reshape.258), channel_id=4, replica_groups=mesh['tp'=4,'fsdp'=8] {'tp'}, dimensions={0}, use_global_device_ids=true | all-gather | bytes 7680 | tf_op jit(solution)/shard_map/all_gather | solution.py:326
  950.3 25.6 %collective-permute-done.27 = bf16[256,3072]{1,0:T(8,128)(2,1)S(1)} collective-permute-done((bf16[256,3072]{1,0:T(8,128)(2,1)}, bf16[256,3072]{1,0:T(8,128)(2,1)S(1)}, u32[]{:S(2)}, u32[]{:S(2)}) %collective-permute-start.27) | collective-permute-done | bytes 1572896 | tf_op jit(solution)/shard_map/ppermute | solution.py:187
  982.2 23.0 %collective-permute-done.45 = bf16[256,3072]{1,0:T(8,128)(2,1)S(1)} collective-permute-done((bf16[256,3072]{1,0:T(8,128)(2,1)}, bf16[256,3072]{1,0:T(8,128)(2,1)S(1)}, u32[]{:S(2)}, u32[]{:S(2)}) %collective-permute-start.45) | collective-permute-done | bytes 1572896 | tf_op jit(solution)/shard_map/ppermute | solution.py:187
  (346 shorter events, 242.4 us)
Async XLA Ops:
  7.2 94.0 %all-gather.8.cloned.1.call-start = ((), (), s32[]{:S(2)}) async-start(), calls=%async_computation.5 | async-start | bytes 7864320 | tf_op jit(solution)/shard_map/all_gather | solution.py:133
  13.2 294.9 %all-gather.10.cloned.1.call-start = ((), (), s32[]{:S(2)}) async-start(), calls=%async_computation.6 | async-start | bytes 7864320 | tf_op jit(solution)/shard_map/all_gather | solution.py:133
  13.3 78.8 %collective-permute-start = (bf16[384,2048]{1,0:T(8,128)(2,1)}, bf16[384,2048]{1,0:T(8,128)(2,1)}, u32[]{:S(2)}, u32[]{:S(2)}) collective-permute-start(bf16[384,2048]{1,0:T(8,128)(2,1)} %param.22), channel_id=1, source_target_pairs={{0,4},{1,5},{2,6},{3,7},{4,0},{5,1},{6,2},{7,3},{8,12},{9,13},{10,... | collective-permute-start | bytes 4718600 | tf_op jit(solution)/shard_map/ppermute | solution.py:226
  101.2 60.5 %collective-permute-start.3 = (bf16[384,2048]{1,0:T(8,128)(2,1)}, bf16[384,2048]{1,0:T(8,128)(2,1)}, u32[]{:S(2)}, u32[]{:S(2)}) collective-permute-start(bf16[384,2048]{1,0:T(8,128)(2,1)} %param.22), channel_id=1, source_target_pairs={{0,2},{1,3},{2,0},{3,1},{4,6},{5,7},{6,4},{7,5},{8,10},{9,11},{10,... | collective-permute-start | bytes 4718600 | tf_op jit(solution)/shard_map/ppermute | solution.py:226
  101.8 905.1 %reduce-scatter.8.cloned.1.call-start = ((), (), s32[]{:S(2)}) async-start(), calls=%async_computation.8 | async-start | bytes 2949120 | tf_op jit(solution)/shard_map/reduce_scatter | solution.py:257
  102.5 120.1 %collective-permute-start.4 = (bf16[384,2048]{1,0:T(8,128)(2,1)}, bf16[384,2048]{1,0:T(8,128)(2,1)S(1)}, u32[]{:S(2)}, u32[]{:S(2)}) collective-permute-start(bf16[384,2048]{1,0:T(8,128)(2,1)} %collective-permute-done), channel_id=1, source_target_pairs={{0,2},{1,3},{2,0},{3,1},{4,6},{5,7},{6,4},{7,5},{8,10},{9,11},{10,... | collective-permute-start | bytes 4718600 | tf_op jit(solution)/shard_map/ppermute | solution.py:227
  235.5 61.3 %collective-permute-start.5 = (bf16[1536,2048]{1,0:T(8,128)(2,1)}, bf16[1536,2048]{1,0:T(8,128)(2,1)}, u32[]{:S(2)}, u32[]{:S(2)}) collective-permute-start(bf16[1536,2048]{1,0:T(8,128)(2,1)} %bitcast.11), channel_id=1, source_target_pairs={{0,1},{1,0},{2,3},{3,2},{4,5},{5,4},{6,7},{7,6},{8,9},{9,8},{10,11... | collective-permute-start | bytes 18874376 | tf_op jit(solution)/shard_map/ppermute | solution.py:149
  238.1 37.1 %collective-permute-start.2 = (bf16[384,2048]{1,0:T(8,128)(2,1)}, bf16[384,2048]{1,0:T(8,128)(2,1)}, u32[]{:S(2)}, u32[]{:S(2)}) collective-permute-start(bf16[384,2048]{1,0:T(8,128)(2,1)} %bitcast.167), channel_id=1, source_target_pairs={{0,4},{1,5},{2,6},{3,7},{4,0},{5,1},{6,2},{7,3},{8,12},{9,13},{10,... | collective-permute-start | bytes 4718600 | tf_op jit(solution)/shard_map/ppermute | solution.py:229
  308.2 37.3 %collective-permute-start.7 = (bf16[384,2048]{1,0:T(8,128)(2,1)S(1)}, bf16[384,2048]{1,0:T(8,128)(2,1)S(1)}, u32[]{:S(2)}, u32[]{:S(2)}) collective-permute-start(bf16[384,2048]{1,0:T(8,128)(2,1)S(1)} %bitcast.168), channel_id=1, source_target_pairs={{0,2},{1,3},{2,0},{3,1},{4,6},{5,7},{6,4},{7,5},{8,10},{9,11},{10,... | collective-permute-start | bytes 4718600 | tf_op jit(solution)/shard_map/ppermute | solution.py:229
  308.4 70.2 %collective-permute-start.8 = (bf16[384,2048]{1,0:T(8,128)(2,1)}, bf16[384,2048]{1,0:T(8,128)(2,1)S(1)}, u32[]{:S(2)}, u32[]{:S(2)}) collective-permute-start(bf16[384,2048]{1,0:T(8,128)(2,1)} %collective-permute-done.2), channel_id=1, source_target_pairs={{0,2},{1,3},{2,0},{3,1},{4,6},{5,7},{6,4},{7,5},{8,10},{9,11},{10,... | collective-permute-start | bytes 4718600 | tf_op jit(solution)/shard_map/ppermute | solution.py:230
  388.7 36.0 %collective-permute-start.10 = (bf16[1536,2048]{1,0:T(8,128)(2,1)}, bf16[1536,2048]{1,0:T(8,128)(2,1)}, u32[]{:S(2)}, u32[]{:S(2)}) collective-permute-start(bf16[1536,2048]{1,0:T(8,128)(2,1)} %bitcast.16), channel_id=1, source_target_pairs={{0,1},{1,0},{2,3},{3,2},{4,5},{5,4},{6,7},{7,6},{8,9},{9,8},{10,11... | collective-permute-start | bytes 18874376 | tf_op jit(solution)/shard_map/ppermute | solution.py:149
  408.2 58.6 %collective-permute-start.12 = (bf16[256,1536]{1,0:T(8,128)(2,1)S(1)}, bf16[256,1536]{1,0:T(8,128)(2,1)}, u32[]{:S(2)}, u32[]{:S(2)}) collective-permute-start(bf16[256,1536]{1,0:T(8,128)(2,1)S(1)} %get-tuple-element.213), channel_id=1, source_target_pairs={{24,16},{25,17},{26,18},{27,19},{28,20},{29,21},{30,22},{31,23}} | collective-permute-start | bytes 2359304 | tf_op jit(solution)/shard_map/ppermute | solution.py:177
  411.8 55.0 %collective-permute-start.9 = (bf16[256,1536]{1,0:T(8,128)(2,1)S(1)}, bf16[256,1536]{1,0:T(8,128)(2,1)}, u32[]{:S(2)}, u32[]{:S(2)}) collective-permute-start(bf16[256,1536]{1,0:T(8,128)(2,1)S(1)} %get-tuple-element.214), channel_id=1, source_target_pairs={{0,8},{1,9},{2,10},{3,11},{4,12},{5,13},{6,14},{7,15}} | collective-permute-start | bytes 2359304 | tf_op jit(solution)/shard_map/ppermute | solution.py:176
  434.7 32.1 %collective-permute-start.11 = (bf16[256,1536]{1,0:T(8,128)(2,1)S(1)}, bf16[256,1536]{1,0:T(8,128)(2,1)}, u32[]{:S(2)}, u32[]{:S(2)}) collective-permute-start(bf16[256,1536]{1,0:T(8,128)(2,1)S(1)} %get-tuple-element.212), channel_id=1, source_target_pairs={{0,8},{1,9},{2,10},{3,11},{4,12},{5,13},{6,14},{7,15}} | collective-permute-start | bytes 2359304 | tf_op jit(solution)/shard_map/ppermute | solution.py:176
  436.5 30.4 %collective-permute-start.13 = (bf16[256,1536]{1,0:T(8,128)(2,1)}, bf16[256,1536]{1,0:T(8,128)(2,1)}, u32[]{:S(2)}, u32[]{:S(2)}) collective-permute-start(bf16[256,1536]{1,0:T(8,128)(2,1)} %get-tuple-element.211), channel_id=1, source_target_pairs={{24,16},{25,17},{26,18},{27,19},{28,20},{29,21},{30,22},{31,23}} | collective-permute-start | bytes 2359304 | tf_op jit(solution)/shard_map/ppermute | solution.py:177
  442.8 81.4 %collective-permute-start.47 = (bf16[1536,768]{1,0:T(8,128)(2,1)}, bf16[1536,768]{1,0:T(8,128)(2,1)}, u32[]{:S(2)}, u32[]{:S(2)}) collective-permute-start(bf16[1536,768]{1,0:T(8,128)(2,1)} %convolution_convert_fusion.4), channel_id=1, source_target_pairs={{0,1},{1,0},{2,3},{3,2},{4,5},{5,4},{6,7},{7,6},{8,9},{9,8},{10,11... | collective-permute-start | bytes 7077896 | tf_op jit(solution)/shard_map/ppermute | solution.py:255
  468.7 28.7 %collective-permute-start.15 = (bf16[256,1536]{1,0:T(8,128)(2,1)S(1)}, bf16[256,1536]{1,0:T(8,128)(2,1)S(1)}, u32[]{:S(2)}, u32[]{:S(2)}) collective-permute-start(bf16[256,1536]{1,0:T(8,128)(2,1)S(1)} %get-tuple-element.208), channel_id=1, source_target_pairs={{0,8},{8,16},{1,9},{9,17},{2,10},{10,18},{3,11},{11,19},{4,12},{12... | collective-permute-start | bytes 2359304 | tf_op jit(solution)/shard_map/ppermute | solution.py:176
  473.3 31.6 %collective-permute-start.16 = (bf16[256,1536]{1,0:T(8,128)(2,1)S(1)}, bf16[256,1536]{1,0:T(8,128)(2,1)S(1)}, u32[]{:S(2)}, u32[]{:S(2)}) collective-permute-start(bf16[256,1536]{1,0:T(8,128)(2,1)S(1)} %get-tuple-element.209), channel_id=1, source_target_pairs={{24,16},{16,8},{25,17},{17,9},{26,18},{18,10},{27,19},{19,11},{28,... | collective-permute-start | bytes 2359304 | tf_op jit(solution)/shard_map/ppermute | solution.py:177
  497.4 60.6 %collective-permute-start.46 = (bf16[1536,1280]{1,0:T(8,128)(2,1)}, bf16[1536,1280]{1,0:T(8,128)(2,1)}, u32[]{:S(2)}, u32[]{:S(2)}) collective-permute-start(bf16[1536,1280]{1,0:T(8,128)(2,1)} %convolution_convert_fusion), channel_id=1, source_target_pairs={{0,1},{1,0},{2,3},{3,2},{4,5},{5,4},{6,7},{7,6},{8,9},{9,8},{10,11... | collective-permute-start | bytes 11796488 | tf_op jit(solution)/shard_map/ppermute | solution.py:255
  529.4 477.5 %reduce-scatter.6.cloned.1.call-start = ((), (), s32[]{:S(2)}) async-start(), calls=%async_computation.7 | async-start | bytes 4915200 | tf_op jit(solution)/shard_map/reduce_scatter | solution.py:257
  565.9 446.9 %reduce-scatter.14.cloned.1.call-start = ((), (), s32[]{:S(2)}) async-start(), calls=%async_computation.11 | async-start | bytes 7864320 | tf_op jit(solution)/shard_map/reduce_scatter | solution.py:257
  580.5 434.8 %reduce-scatter.12.cloned.1.call-start = ((), (), s32[]{:S(2)}) async-start(), calls=%async_computation.10 | async-start | bytes 7864320 | tf_op jit(solution)/shard_map/reduce_scatter | solution.py:257
  599.1 55.2 %collective-permute-start.20 = (bf16[256,1536]{1,0:T(8,128)(2,1)}, bf16[256,1536]{1,0:T(8,128)(2,1)}, u32[]{:S(2)}, u32[]{:S(2)}) collective-permute-start(bf16[256,1536]{1,0:T(8,128)(2,1)} %add_convert_fusion.19), channel_id=1, source_target_pairs={{0,8},{8,16},{16,24},{1,9},{9,17},{17,25},{2,10},{10,18},{18,26},{... | collective-permute-start | bytes 2359304 | tf_op jit(solution)/shard_map/ppermute | solution.py:176
  602.0 33.6 %collective-permute-start.29 = (bf16[256,1536]{1,0:T(8,128)(2,1)}, bf16[256,1536]{1,0:T(8,128)(2,1)}, u32[]{:S(2)}, u32[]{:S(2)}) collective-permute-start(bf16[256,1536]{1,0:T(8,128)(2,1)} %get-tuple-element.204), channel_id=1, source_target_pairs={{0,8},{1,9},{2,10},{3,11},{4,12},{5,13},{6,14},{7,15}} | collective-permute-start | bytes 2359304 | tf_op jit(solution)/shard_map/ppermute | solution.py:176
  603.5 33.4 %collective-permute-start.31 = (bf16[256,1536]{1,0:T(8,128)(2,1)}, bf16[256,1536]{1,0:T(8,128)(2,1)}, u32[]{:S(2)}, u32[]{:S(2)}) collective-permute-start(bf16[256,1536]{1,0:T(8,128)(2,1)} %get-tuple-element.203), channel_id=1, source_target_pairs={{24,16},{25,17},{26,18},{27,19},{28,20},{29,21},{30,22},{31,23}} | collective-permute-start | bytes 2359304 | tf_op jit(solution)/shard_map/ppermute | solution.py:177
  620.5 394.8 %reduce-scatter.10.cloned.1.call-start = ((), (), s32[]{:S(2)}) async-start(), calls=%async_computation.9 | async-start | bytes 7864320 | tf_op jit(solution)/shard_map/reduce_scatter | solution.py:257
  637.0 34.2 %collective-permute-start.18 = (bf16[256,1536]{1,0:T(8,128)(2,1)S(1)}, bf16[256,1536]{1,0:T(8,128)(2,1)S(1)}, u32[]{:S(2)}, u32[]{:S(2)}) collective-permute-start(bf16[256,1536]{1,0:T(8,128)(2,1)S(1)} %copy-done.34), channel_id=1, source_target_pairs={{0,8},{8,16},{16,24},{1,9},{9,17},{17,25},{2,10},{10,18},{18,26},{... | collective-permute-start | bytes 2359304 | tf_op jit(solution)/shard_map/ppermute | solution.py:176
  638.3 39.2 %collective-permute-start.19 = (bf16[256,1536]{1,0:T(8,128)(2,1)S(1)}, bf16[256,1536]{1,0:T(8,128)(2,1)S(1)}, u32[]{:S(2)}, u32[]{:S(2)}) collective-permute-start(bf16[256,1536]{1,0:T(8,128)(2,1)S(1)} %copy-done.33), channel_id=1, source_target_pairs={{24,16},{16,8},{8,0},{25,17},{17,9},{9,1},{26,18},{18,10},{10,2},{... | collective-permute-start | bytes 2359304 | tf_op jit(solution)/shard_map/ppermute | solution.py:177
  648.5 119.8 %collective-permute-start.48 = (bf16[1536,2048]{1,0:T(8,128)(2,1)}, bf16[1536,2048]{1,0:T(8,128)(2,1)}, u32[]{:S(2)}, u32[]{:S(2)}) collective-permute-start(bf16[1536,2048]{1,0:T(8,128)(2,1)} %convolution_convert_fusion.3), channel_id=1, source_target_pairs={{0,1},{1,0},{2,3},{3,2},{4,5},{5,4},{6,7},{7,6},{8,9},{9,8},{10,11... | collective-permute-start | bytes 18874376 | tf_op jit(solution)/shard_map/ppermute | solution.py:255
  654.3 34.9 %collective-permute-start.33 = (bf16[256,1536]{1,0:T(8,128)(2,1)}, bf16[256,1536]{1,0:T(8,128)(2,1)}, u32[]{:S(2)}, u32[]{:S(2)}) collective-permute-start(bf16[256,1536]{1,0:T(8,128)(2,1)} %get-tuple-element.200), channel_id=1, source_target_pairs={{0,8},{8,16},{1,9},{9,17},{2,10},{10,18},{3,11},{11,19},{4,12},{12... | collective-permute-start | bytes 2359304 | tf_op jit(solution)/shard_map/ppermute | solution.py:176
  660.7 33.8 %collective-permute-start.35 = (bf16[256,1536]{1,0:T(8,128)(2,1)}, bf16[256,1536]{1,0:T(8,128)(2,1)}, u32[]{:S(2)}, u32[]{:S(2)}) collective-permute-start(bf16[256,1536]{1,0:T(8,128)(2,1)} %get-tuple-element.199), channel_id=1, source_target_pairs={{24,16},{16,8},{25,17},{17,9},{26,18},{18,10},{27,19},{19,11},{28,... | collective-permute-start | bytes 2359304 | tf_op jit(solution)/shard_map/ppermute | solution.py:177
  671.2 28.8 %collective-permute-start.32 = (bf16[256,1536]{1,0:T(8,128)(2,1)}, bf16[256,1536]{1,0:T(8,128)(2,1)}, u32[]{:S(2)}, u32[]{:S(2)}) collective-permute-start(bf16[256,1536]{1,0:T(8,128)(2,1)} %get-tuple-element.202), channel_id=1, source_target_pairs={{0,8},{8,16},{1,9},{9,17},{2,10},{10,18},{3,11},{11,19},{4,12},{12... | collective-permute-start | bytes 2359304 | tf_op jit(solution)/shard_map/ppermute | solution.py:176
  677.5 33.8 %collective-permute-start.34 = (bf16[256,1536]{1,0:T(8,128)(2,1)}, bf16[256,1536]{1,0:T(8,128)(2,1)}, u32[]{:S(2)}, u32[]{:S(2)}) collective-permute-start(bf16[256,1536]{1,0:T(8,128)(2,1)} %get-tuple-element.201), channel_id=1, source_target_pairs={{24,16},{16,8},{25,17},{17,9},{26,18},{18,10},{27,19},{19,11},{28,... | collective-permute-start | bytes 2359304 | tf_op jit(solution)/shard_map/ppermute | solution.py:177
  689.2 107.8 %collective-permute-start.22 = (bf16[256,3072]{1,0:T(8,128)(2,1)}, bf16[256,3072]{1,0:T(8,128)(2,1)}, u32[]{:S(2)}, u32[]{:S(2)}) collective-permute-start(bf16[256,3072]{1,0:T(8,128)(2,1)} %add_convert_fusion.12), channel_id=1, source_target_pairs={{0,8},{8,16},{16,24},{1,9},{9,17},{17,25},{2,10},{10,18},{18,26},{... | collective-permute-start | bytes 4718600 | tf_op jit(solution)/shard_map/ppermute | solution.py:187
  694.5 100.7 %collective-permute-start.23 = (bf16[256,3072]{1,0:T(8,128)(2,1)}, bf16[256,3072]{1,0:T(8,128)(2,1)}, u32[]{:S(2)}, u32[]{:S(2)}) collective-permute-start(bf16[256,3072]{1,0:T(8,128)(2,1)} %add_convert_fusion.12), channel_id=1, source_target_pairs={{24,16},{16,8},{8,0},{25,17},{17,9},{9,1},{26,18},{18,10},{10,2},{... | collective-permute-start | bytes 4718600 | tf_op jit(solution)/shard_map/ppermute | solution.py:188
  713.0 29.4 %collective-permute-start.38 = (bf16[256,1536]{1,0:T(8,128)(2,1)S(1)}, bf16[256,1536]{1,0:T(8,128)(2,1)S(1)}, u32[]{:S(2)}, u32[]{:S(2)}) collective-permute-start(bf16[256,1536]{1,0:T(8,128)(2,1)S(1)} %add_convert_fusion.15), channel_id=1, source_target_pairs={{0,8},{8,16},{16,24},{1,9},{9,17},{17,25},{2,10},{10,18},{18,26},{... | collective-permute-start | bytes 2359304 | tf_op jit(solution)/shard_map/ppermute | solution.py:176
  715.8 44.9 %collective-permute-start.39 = (bf16[256,1536]{1,0:T(8,128)(2,1)S(1)}, bf16[256,1536]{1,0:T(8,128)(2,1)S(1)}, u32[]{:S(2)}, u32[]{:S(2)}) collective-permute-start(bf16[256,1536]{1,0:T(8,128)(2,1)S(1)} %add_convert_fusion.14), channel_id=1, source_target_pairs={{24,16},{16,8},{8,0},{25,17},{17,9},{9,1},{26,18},{18,10},{10,2},{... | collective-permute-start | bytes 2359304 | tf_op jit(solution)/shard_map/ppermute | solution.py:177
  742.4 37.0 %collective-permute-start.36 = (bf16[256,1536]{1,0:T(8,128)(2,1)}, bf16[256,1536]{1,0:T(8,128)(2,1)}, u32[]{:S(2)}, u32[]{:S(2)}) collective-permute-start(bf16[256,1536]{1,0:T(8,128)(2,1)} %add_convert_fusion.17), channel_id=1, source_target_pairs={{0,8},{8,16},{16,24},{1,9},{9,17},{17,25},{2,10},{10,18},{18,26},{... | collective-permute-start | bytes 2359304 | tf_op jit(solution)/shard_map/ppermute | solution.py:176
  788.4 36.8 %collective-permute-start.41 = (bf16[256,3072]{1,0:T(8,128)(2,1)}, bf16[256,3072]{1,0:T(8,128)(2,1)S(1)}, u32[]{:S(2)}, u32[]{:S(2)}) collective-permute-start(bf16[256,3072]{1,0:T(8,128)(2,1)} %fusion.27), channel_id=1, source_target_pairs={{24,16},{16,8},{8,0},{25,17},{17,9},{9,1},{26,18},{18,10},{10,2},{... | collective-permute-start | bytes 4718600 | tf_op jit(solution)/shard_map/ppermute | solution.py:188
  793.8 39.4 %collective-permute-start.40 = (bf16[256,3072]{1,0:T(8,128)(2,1)}, bf16[256,3072]{1,0:T(8,128)(2,1)S(1)}, u32[]{:S(2)}, u32[]{:S(2)}) collective-permute-start(bf16[256,3072]{1,0:T(8,128)(2,1)} %fusion.27), channel_id=1, source_target_pairs={{0,8},{8,16},{16,24},{1,9},{9,17},{17,25},{2,10},{10,18},{18,26},{... | collective-permute-start | bytes 4718600 | tf_op jit(solution)/shard_map/ppermute | solution.py:187
  795.1 39.4 %collective-permute-start.24 = (bf16[256,3072]{1,0:T(8,128)(2,1)}, bf16[256,3072]{1,0:T(8,128)(2,1)}, u32[]{:S(2)}, u32[]{:S(2)}) collective-permute-start(bf16[256,3072]{1,0:T(8,128)(2,1)} %collective-permute-done.23), channel_id=1, source_target_pairs={{16,8},{8,0},{17,9},{9,1},{18,10},{10,2},{19,11},{11,3},{20,12},{1... | collective-permute-start | bytes 4718600 | tf_op jit(solution)/shard_map/ppermute | solution.py:188
  797.0 139.5 %collective-permute-start.26 = (bf16[256,3072]{1,0:T(8,128)(2,1)}, bf16[256,3072]{1,0:T(8,128)(2,1)}, u32[]{:S(2)}, u32[]{:S(2)}) collective-permute-start(bf16[256,3072]{1,0:T(8,128)(2,1)} %collective-permute-done.22), channel_id=1, source_target_pairs={{8,16},{16,24},{9,17},{17,25},{10,18},{18,26},{11,19},{19,27},{12,... | collective-permute-start | bytes 4718600 | tf_op jit(solution)/shard_map/ppermute | solution.py:187
  825.2 118.7 %collective-permute-start.42 = (bf16[256,3072]{1,0:T(8,128)(2,1)S(1)}, bf16[256,3072]{1,0:T(8,128)(2,1)}, u32[]{:S(2)}, u32[]{:S(2)}) collective-permute-start(bf16[256,3072]{1,0:T(8,128)(2,1)S(1)} %collective-permute-done.41), channel_id=1, source_target_pairs={{16,8},{8,0},{17,9},{9,1},{18,10},{10,2},{19,11},{11,3},{20,12},{1... | collective-permute-start | bytes 4718600 | tf_op jit(solution)/shard_map/ppermute | solution.py:188
  833.2 111.5 %collective-permute-start.44 = (bf16[256,3072]{1,0:T(8,128)(2,1)S(1)}, bf16[256,3072]{1,0:T(8,128)(2,1)}, u32[]{:S(2)}, u32[]{:S(2)}) collective-permute-start(bf16[256,3072]{1,0:T(8,128)(2,1)S(1)} %collective-permute-done.40), channel_id=1, source_target_pairs={{8,16},{16,24},{9,17},{17,25},{10,18},{18,26},{11,19},{19,27},{12,... | collective-permute-start | bytes 4718600 | tf_op jit(solution)/shard_map/ppermute | solution.py:187
  834.5 111.8 %collective-permute-start.25 = (bf16[256,3072]{1,0:T(8,128)(2,1)}, bf16[256,3072]{1,0:T(8,128)(2,1)}, u32[]{:S(2)}, u32[]{:S(2)}) collective-permute-start(bf16[256,3072]{1,0:T(8,128)(2,1)} %collective-permute-done.24), channel_id=1, source_target_pairs={{8,0},{9,1},{10,2},{11,3},{12,4},{13,5},{14,6},{15,7}} | collective-permute-start | bytes 4718600 | tf_op jit(solution)/shard_map/ppermute | solution.py:188
  936.5 39.4 %collective-permute-start.27 = (bf16[256,3072]{1,0:T(8,128)(2,1)}, bf16[256,3072]{1,0:T(8,128)(2,1)S(1)}, u32[]{:S(2)}, u32[]{:S(2)}) collective-permute-start(bf16[256,3072]{1,0:T(8,128)(2,1)} %collective-permute-done.26), channel_id=1, source_target_pairs={{16,24},{17,25},{18,26},{19,27},{20,28},{21,29},{22,30},{23,31}} | collective-permute-start | bytes 4718600 | tf_op jit(solution)/shard_map/ppermute | solution.py:187
  943.9 32.5 %collective-permute-start.43 = (bf16[256,3072]{1,0:T(8,128)(2,1)}, bf16[256,3072]{1,0:T(8,128)(2,1)S(1)}, u32[]{:S(2)}, u32[]{:S(2)}) collective-permute-start(bf16[256,3072]{1,0:T(8,128)(2,1)} %collective-permute-done.42), channel_id=1, source_target_pairs={{8,0},{9,1},{10,2},{11,3},{12,4},{13,5},{14,6},{15,7}} | collective-permute-start | bytes 4718600 | tf_op jit(solution)/shard_map/ppermute | solution.py:188
  944.7 60.5 %collective-permute-start.45 = (bf16[256,3072]{1,0:T(8,128)(2,1)}, bf16[256,3072]{1,0:T(8,128)(2,1)S(1)}, u32[]{:S(2)}, u32[]{:S(2)}) collective-permute-start(bf16[256,3072]{1,0:T(8,128)(2,1)} %collective-permute-done.44), channel_id=1, source_target_pairs={{16,24},{17,25},{18,26},{19,27},{20,28},{21,29},{22,30},{23,31}} | collective-permute-start | bytes 4718600 | tf_op jit(solution)/shard_map/ppermute | solution.py:187
  (68 other events, 1137.3 us)
Sparse Core Ops, SparseCore 0:
  13.3 87.8 all-gather.7
  103.1 119.4 all-gather.9
  529.5 38.5 reduce-scatter.7
  571.0 50.4 reduce-scatter.5
  624.3 70.0 reduce-scatter.13
  697.8 70.0 reduce-scatter.11
  779.5 70.7 reduce-scatter.9

commit v3 on v1

--- a/solution.py
+++ b/solution.py
@@ -234,10 +234,12 @@
         def expand(left, right):
             return [mm('te,de->td', left, part) for part in right]
 
-        def weight_grad(rows, cols):
+        def weight_total(rows, cols):
             other = mm('td,te->de', rows[1], cols).astype(BF16)
             arrived = lax.ppermute(other, 'fsdp', SIBLING)
-            total = (mm('td,te->de', rows[0], cols) + arrived.astype(F32)).astype(BF16)
+            return (mm('td,te->de', rows[0], cols) + arrived.astype(F32)).astype(BF16)
+
+        def scatter(total):
             return lax.psum_scatter(total, 'fsdp', scatter_dimension=0, tiled=True, axis_index_groups=CORE_GROUPS)
 
         h_pair, g_pair = (h_m, h_o), (g_m, g_o)
@@ -256,11 +258,13 @@
         attn_dh = expand(grad_qkv, qkv_w)
 
 
+        out_total = weight_total(g_pair, after(attn_out, gate_mine))
+        qkv_total = weight_total(h_pair, after(grad_qkv, gate_mine))
         gate_w = with_sibling(after(gate_mine, attn_part))
         gate = contract(h_pair, gate_w).astype(BF16)
-        up_w = with_sibling(after(up_mine, gate))
+        up_w = with_sibling(after(up_mine, (gate, out_total)))
         up_proj = contract(h_pair, up_w).astype(BF16)
-        down_w = with_sibling(after(down_mine, up_proj))
+        down_w = with_sibling(after(down_mine, (up_proj, qkv_total, attn_dh)))
         gate_f32, up_f32 = gate.astype(F32), up_proj.astype(F32)
         sigma = jax.nn.sigmoid(gate_f32)
         gated_act = (gate_f32 * sigma * up_f32).astype(BF16)
@@ -282,16 +286,15 @@
         grad_gate = (grad_act * up_f32 * sigma * (1.0 + gate_f32 * (1.0 - sigma))).astype(BF16)
         grad_up = (grad_act * gate_f32 * sigma).astype(BF16)
         early_gate, early_up = after(grad_gate, fwd_sent[1]), after(grad_up, fwd_sent[2])
-        dh_part = [(a + b + c).astype(BF16)
-                   for a, b, c in zip(attn_dh, expand(early_gate, gate_w), expand(early_up, up_w))]
+        dh_early = [a + b for a, b in zip(attn_dh, expand(early_gate, gate_w))]
+        dh_part = [(a + b).astype(BF16) for a, b in zip(dh_early, expand(early_up, up_w))]
         dh_sum, _ = chain_sum(chunks(dh_part), tp, n_tp)
 
-        grad_wqkv = weight_grad(h_pair, after(grad_qkv, forward_part))
-        grad_wout = weight_grad(g_pair, after(attn_out, forward_part))
-        grad_wdown = weight_grad(g_pair, after(gated_act, dh_part))
-        grad_wgate = weight_grad(h_pair, after(grad_gate, dh_part))
-        grad_wup = weight_grad(h_pair, after(grad_up, dh_part))
-        grad_wqkv, grad_wout = after((grad_wqkv, grad_wout), dh_part)
+        grad_wout, grad_wqkv = scatter(after(out_total, down_mine)), scatter(after(qkv_total, down_mine))
+        grad_wdown = scatter(weight_total(g_pair, after(gated_act, dh_part)))
+        grad_wgate = scatter(weight_total(h_pair, after(grad_gate, dh_part)))
+        grad_wup = scatter(weight_total(h_pair, after(grad_up, dh_part)))
+        grad_wqkv, grad_wout = after((grad_wqkv, grad_wout), dh_sum)
 
         dh_sum = after(dh_sum, out_chunk)
         grad_normed = join_model_dim(dh_sum[0], dh_sum[1], core, width).astype(BF16).astype(F32)
@@ -303,12 +306,14 @@
         ln_part = jnp.sum(grad_normed * xc_hat, axis=0).reshape(n_fsdp, width)
         all_heads = heads + kv_heads
         head_part = norm_part.reshape(all_heads, n_fsdp, dims_part).transpose(1, 0, 2).reshape(n_fsdp, all_heads * dims_part)
-        small_parts = lax.all_gather(jnp.concatenate([ln_part, head_part], axis=1), ('fsdp', 'tp'), axis=0, tiled=False)
-        small_own = lax.dynamic_index_in_dim(small_parts, fsdp, 1, keepdims=False)
-        grad_ln = jnp.sum(small_own[:, :width], axis=0)
-        head_own = small_own[:, width:].reshape(n_fsdp, n_tp, all_heads * dims_part)
-        head_own = jnp.sum(lax.dynamic_index_in_dim(head_own, tp[0], 1, keepdims=False), axis=0)
-        norm_own = head_own.reshape(all_heads, dims_part)
+        small_block = jnp.concatenate([ln_part, head_part], axis=1)
+        small_parts = lax.all_gather(small_block, 'fsdp', axis=0, tiled=False)
+        small_own = jnp.sum(lax.dynamic_index_in_dim(small_parts, fsdp, 1, keepdims=False), axis=0)
+        norm_own = small_own[width:].reshape(all_heads, dims_part)
+        ln_own = small_own[:width]
+        grad_ln = ln_own
+        for shift in range(1, n_tp):
+            grad_ln += lax.ppermute(ln_own, 'tp', [(i, (i + shift) % n_tp) for i in range(n_tp)])
 
         return (layer_out.reshape(hidden.shape), grad_hidden.reshape(hidden.shape), grad_ln, grad_wqkv[:, :q_width], grad_wqkv[:, q_width:q_width + kv_width],
                 grad_wqkv[:, q_width + kv_width:], grad_wout.T, grad_wgate, grad_wup, grad_wdown.T,

time: 970 us -> 897 us (0.925)
  blocking collectives: 135 us -> 20.5 us
  starting transfers between devices: 93 us -> 139 us
  waiting for transfers between devices: 300 us -> 277 us
  matrix products: 271 us -> 287 us
    all_gather x1, blocking collectives: 125 us -> 10.1 us  [device_step(): small_parts = lax.all_gather(small_block, 'fsdp', axis=0, tiled=False)]
    ppermute x5 -> x8, waiting for transfers between devices: 2.96 us -> 72.1 us  [the longest x3 61.7 us: device_step(): lax.ppermute(ln_own, 'tp', [(i, (i + shift) % n_tp) for i in range(n_tp)])]
    ppermute x6, waiting for transfers between devices: 80.4 us -> 22.6 us  [chain_gather(): lax.ppermute(go_left, 'tp', [(i, i - 1) for i in range(n - 1 - step, 0, -...]
    ppermute x5 -> x8, starting transfers between devices: 0.58 us -> 45.2 us  [the longest x3 44.4 us: device_step(): lax.ppermute(ln_own, 'tp', [(i, (i + shift) % n_tp) for i in range(n_tp)])]
    all_gather x4, waiting for transfers between devices: 144 us -> 108 us  [gather_mine(): lax.all_gather(shard, 'fsdp', axis=0, tiled=True, axis_index_groups=CORE_...]
    dot_general x30, matrix products: 271 us -> 287 us  [mm(): return jnp.einsum(form, left, right, preferred_element_type=F32)]
  transfers between devices with their start and end apart: 54 -> 57, of which waited for: 17 -> 16; matrix products, arithmetic and copies ran while one was open for 39% -> 45% of each run, Pallas kernels for 3% -> 3%
where the time goes in v3:
time: 897 us; the launch traced here: 887 us
  matrix products  287 us (32%)
  waiting for transfers between devices  277 us (31%)
  starting transfers between devices  139 us (15%)
  other arithmetic  83.4 us (9%)
  local copies, waits for them, and re-layouts  35 us (4%)
  Pallas kernels  30.4 us (3%)
  blocking collectives  20.5 us (2%)
  between operations  15.5 us (2%)
    dot_general x30, matrix products, mm(): return jnp.einsum(form, left, right, preferred_element_type=F32)  287 us
    all_gather x4, waiting for transfers between devices, gather_mine(): lax.all_gather(shard, 'fsdp', axis=0, tiled=True, axis_index_groups=CORE_...  108 us
    ppermute x12, waiting for transfers between devices, chain_sum(): from_left[h] = lax.ppermute(go_right, 'tp', right)  67.7 us
    ppermute x3, waiting for transfers between devices, device_step(): lax.ppermute(ln_own, 'tp', [(i, (i + shift) % n_tp) for i in range(n_tp)])  61.7 us
    ppermute x12, starting transfers between devices, chain_sum(): from_left[h] = lax.ppermute(go_right, 'tp', right)  54 us
    ppermute x3, starting transfers between devices, device_step(): lax.ppermute(ln_own, 'tp', [(i, (i + shift) % n_tp) for i in range(n_tp)])  44.4 us
    pallas_call x1, Pallas kernels, attention(): pl.pallas_call(functools.partial(attention_kernel, heads, kv_heads, head_...  30.4 us
    ppermute x6, waiting for transfers between devices, chain_gather(): lax.ppermute(go_left, 'tp', [(i, i - 1) for i in range(n - 1 - step, 0, -...  22.6 us
  transfers between devices with their start and end apart: 57, of which 16 were waited for; matrix products, arithmetic and copies ran while one was open for 45% of the time, Pallas kernels for 3%

profile of v3, /device:TPU:0, one launch (start us, length us, event | category | flops | bytes accessed | tf_op | source)
XLA Modules:
  0.0 887.4 jit_solution(1471340096565645928)
XLA Ops:
  15.0 10.4 %all-gather.2 = bf16[8,1,512]{2,1,0:T(2,128)(2,1)S(1)} all-gather(bf16[1,1,512]{2,1,0:T(2,128)(2,1)S(1)} %reshape.247), channel_id=2, replica_groups=mesh['tp'=4,'fsdp'=8] {'fsdp'}, dimensions={0}, use_global_device_ids=true | all-gather | bytes 9216 | tf_op jit(solution)/shard_map/all_gather | solution.py:219
  29.8 56.1 %all-gather.8.cloned.1.call-done = bf16[1536,2048]{0,1:T(8,128)(2,1)} async-done(((bf16[384,2048]{0,1:T(8,128)(2,1)}), bf16[1536,2048]{0,1:T(8,128)(2,1)}) %all-gather.8.cloned.1.call-update) | async-done | bytes 6291472 | tf_op jit(solution)/shard_map/all_gather | solution.py:133
  92.5 6.9 fusion.4
  103.9 7.0 fusion.37
  115.2 6.6 add_convert_fusion.10.qkv_ref
  126.8 30.4 %attention.1 = (bf16[1024,768]{1,0:T(8,128)(2,1)S(1)}, bf16[1024,1280]{1,0:T(8,128)(2,1)S(1)}, f32[8,128]{1,0:T(8,128)S(1)}) custom-call(bf16[1024,1280]{1,0:T(8,128)(2,1)S(1)} %add_convert_fusion.10.qkv_ref, bf16[1024,768]{1,0:T(8,128)(2,1)S(1)} %add_convert_fusion.13.ga_ref, f32[1024,128]{1,0:T(8,128)S(1)} %get-tuple-element.204.cos_ref, ...), custom_call_target="tpu_custom_call" | custom-call | flops 2415919104 | bytes 13107200 | tf_op jit(solution)/shard_map/attention/pallas_call | solution.py:99
  157.2 6.7 fusion.31
  163.9 6.1 fusion.35
  175.9 9.0 %fusion.64 = f32[1024,2048]{1,0:T(8,128)} fusion(bf16[1024,1536]{1,0:T(8,128)(2,1)S(1)} %copy-done.6, bf16[1536,2048]{1,0:T(8,128)(2,1)S(1)} %copy-done.34), kind=kOutput, calls=%fused_computation.180 | convolution fusion | flops 6442450944 | bytes 17825792 | tf_op jit(solution)/shard_map/td,de->te/dot_general | solution.py:21
  188.9 12.3 %add_convert_fusion.4 = bf16[1024,2048]{1,0:T(8,128)(2,1)} fusion(f32[1024,2048]{1,0:T(8,128)} %fusion.64, bf16[1024,1536]{1,0:T(8,128)(2,1)} %copy-done.11, bf16[1536,2048]{1,0:T(8,128)(2,1)} %collective-permute-done.1), kind=kOutput, calls=%fused_computation.27 | convolution fusion | flops 6446645248 | bytes 22020096 | tf_op jit(solution)/shard_map/td,de->te/dot_general | solution.py:21
  201.2 28.6 %all-gather.12.cloned.1.call-done = bf16[1536,2048]{1,0:T(8,128)(2,1)} async-done(((bf16[384,2048]{1,0:T(8,128)(2,1)}), bf16[1536,2048]{1,0:T(8,128)(2,1)}) %all-gather.12.cloned.1.call-update) | async-done | bytes 6291472 | tf_op jit(solution)/shard_map/all_gather | solution.py:133
  229.8 8.6 convolution_convert_fusion
  238.9 8.5 fusion.18
  247.5 8.6 fusion.21
  256.1 7.5 add_convert_fusion.5
  263.6 9.9 %fusion.65 = f32[1024,2048]{1,0:T(8,128)S(1)} fusion(bf16[1024,1536]{1,0:T(8,128)(2,1)} %copy-done.11, bf16[1536,2048]{1,0:T(8,128)(2,1)} %collective-permute-done.3), kind=kOutput, calls=%fused_computation.181 | convolution fusion | flops 6442450944 | bytes 17825792 | tf_op jit(solution)/shard_map/td,de->te/dot_general | solution.py:21
  273.5 12.0 %fusion.5 = (bf16[1024,2048]{1,0:T(8,128)(2,1)}, bf16[1024,2048]{1,0:T(8,128)(2,1)}) fusion(bf16[1024,2048]{1,0:T(8,128)(2,1)} %add_convert_fusion.4, f32[1024,2048]{1,0:T(8,128)S(1)} %fusion.65, bf16[1024,1536]{1,0:T(8,128)(2,1)S(1)} %copy-done.8, bf16[1536,2048]{1,0:T(8,128)(2,1)S(1)} %bitcast.177), kind=kOutput, calls=%fused_computation.16 | convolution fusion | flops 6463422464 | bytes 30408704 | tf_op jit(solution)/shard_map/td,de->te/dot_general | solution.py:21
  285.5 23.4 %all-gather.14.cloned.1.call-done = bf16[1536,2048]{0,1:T(8,128)(2,1)} async-done(((bf16[384,2048]{0,1:T(8,128)(2,1)}), bf16[1536,2048]{0,1:T(8,128)(2,1)}) %all-gather.14.cloned.1.call-update) | async-done | bytes 6291472 | tf_op jit(solution)/shard_map/all_gather | solution.py:133
  309.0 12.9 %add_convert_fusion.9 = bf16[1024,1536]{1,0:T(8,128)(2,1)S(1)} fusion(f32[1024,1536]{1,0:T(8,128)} %fusion.35, bf16[1024,2048]{1,0:T(8,128)(2,1)} %get-tuple-element.93, bf16[1536,2048]{0,1:T(8,128)(2,1)} %all-gather.14.cloned.1.call-done), kind=kOutput, calls=%fused_computation.36 | convolution fusion | flops 6445596672 | bytes 19922944 | tf_op jit(solution)/shard_map/te,de->td/dot_general | solution.py:21
  327.9 10.8 %add_convert_fusion.8 = bf16[1024,1536]{1,0:T(8,128)(2,1)S(1)} fusion(f32[1024,1536]{1,0:T(8,128)} %fusion.31, bf16[1024,2048]{1,0:T(8,128)(2,1)S(1)} %copy-done.38, bf16[1536,2048]{0,1:T(8,128)(2,1)} %collective-permute-done.6), kind=kOutput, calls=%fused_computation.35 | convolution fusion | flops 6445596672 | bytes 19922944 | tf_op jit(solution)/shard_map/te,de->td/dot_general | solution.py:21
  344.1 10.8 %fusion.66 = f32[1024,2048]{1,0:T(8,128)} fusion(bf16[1024,1536]{1,0:T(8,128)(2,1)S(1)} %copy-done.18, bf16[1536,2048]{0,1:T(8,128)(2,1)} %collective-permute-done.6), kind=kOutput, calls=%fused_computation.182 | convolution fusion | flops 6442450944 | bytes 17825792 | tf_op jit(solution)/shard_map/td,de->te/dot_general | solution.py:21
  354.9 18.1 %fusion.14 = (bf16[1024,2048]{1,0:T(8,128)(2,1)}, bf16[1024,2048]{1,0:T(8,128)(2,1)}) fusion(bf16[1024,2048]{1,0:T(8,128)(2,1)} %add_convert_fusion.4, f32[1024,2048]{1,0:T(8,128)} %fusion.66, bf16[1024,2048]{1,0:T(8,128)(2,1)} %get-tuple-element.158, bf16[1024,1536]{1,0:T(8,128)(2,1)S(1)} %copy-done.16, bf16[1536,2048]{0,1:T(8,128)(2,1)} %all-gather.14.cloned.1.call-done), kind=kOutput, calls=%fused_computation.25 | convolution fusion | flops 6476005376 | bytes 34603008 | tf_op jit(solution)/shard_map/td,de->te/dot_general | solution.py:21
  382.1 10.6 %fusion.67 = f32[1024,1536]{1,0:T(8,128)} fusion(bf16[1024,2048]{1,0:T(8,128)(2,1)S(1)} %copy-done.36, bf16[1536,2048]{1,0:T(8,128)(2,1)} %all-gather.10.cloned.1.call-done), kind=kOutput, calls=%fused_computation.183 | convolution fusion | flops 6442450944 | bytes 16777216 | tf_op jit(solution)/shard_map/te,de->td/dot_general | solution.py:21
  392.7 10.6 %fusion.68 = f32[1024,1536]{1,0:T(8,128)} fusion(bf16[1024,2048]{1,0:T(8,128)(2,1)S(1)} %copy-done.36, bf16[1536,2048]{1,0:T(8,128)(2,1)} %collective-permute-done.1), kind=kOutput, calls=%fused_computation.184 | convolution fusion | flops 6442450944 | bytes 16777216 | tf_op jit(solution)/shard_map/te,de->td/dot_general | solution.py:21
  403.3 7.1 collective-permute-done.10
  417.1 12.4 %add_convert_fusion.7 = bf16[1024,1536]{1,0:T(8,128)(2,1)} fusion(f32[1024,1536]{1,0:T(8,128)} %fusion.21, f32[1024,1536]{1,0:T(8,128)} %fusion.67, bf16[1024,2048]{1,0:T(8,128)(2,1)} %get-tuple-element.92, bf16[1536,2048]{1,0:T(8,128)(2,1)S(1)} %bitcast.179), kind=kOutput, calls=%fused_computation.34 | convolution fusion | flops 6447169536 | bytes 26214400 | tf_op jit(solution)/shard_map/te,de->td/dot_general | solution.py:21
  429.6 12.5 %add_convert_fusion.6 = bf16[1024,1536]{1,0:T(8,128)(2,1)} fusion(f32[1024,1536]{1,0:T(8,128)S(1)} %bitcast.183, f32[1024,1536]{1,0:T(8,128)} %fusion.68, bf16[1024,2048]{1,0:T(8,128)(2,1)} %get-tuple-element.92, bf16[1536,2048]{1,0:T(8,128)(2,1)} %collective-permute-done.3), kind=kOutput, calls=%fused_computation.33 | convolution fusion | flops 6447169536 | bytes 26214400 | tf_op jit(solution)/shard_map/te,de->td/dot_general | solution.py:21
  442.1 11.3 %convolution_convert_fusion.1 = bf16[1536,2048]{1,0:T(8,128)(2,1)} fusion(bf16[1024,1536]{1,0:T(8,128)(2,1)S(1)} %copy-done.19, bf16[1024,2048]{1,0:T(8,128)(2,1)} %get-tuple-element.93), kind=kOutput, calls=%fused_computation.30 | convolution fusion | flops 6445596672 | bytes 13631488 | tf_op jit(solution)/shard_map/td,te->de/dot_general | solution.py:21
  453.4 10.4 %collective-permute-done.47 = bf16[1536,2048]{1,0:T(8,128)(2,1)} collective-permute-done((bf16[1536,2048]{1,0:T(8,128)(2,1)}, bf16[1536,2048]{1,0:T(8,128)(2,1)}, u32[]{:S(2)}, u32[]{:S(2)}) %collective-permute-start.47) | collective-permute-done | bytes 6291488 | tf_op jit(solution)/shard_map/ppermute | solution.py:239
  463.9 11.8 %add_convert_fusion = bf16[1536,2048]{1,0:T(8,128)(2,1)} fusion(bf16[1536,2048]{1,0:T(8,128)(2,1)} %collective-permute-done.47, bf16[1024,1536]{1,0:T(8,128)(2,1)S(1)} %copy-done.16, bf16[1024,2048]{1,0:T(8,128)(2,1)} %get-tuple-element.93), kind=kOutput, calls=%fused_computation.11 | convolution fusion | flops 6451888128 | bytes 19922944 | tf_op jit(solution)/shard_map/td,te->de/dot_general | solution.py:21
  477.5 10.9 %convolution_convert_fusion.2 = bf16[1536,2048]{1,0:T(8,128)(2,1)} fusion(bf16[1024,1536]{1,0:T(8,128)(2,1)S(1)} %copy-done.12, bf16[1024,2048]{1,0:T(8,128)(2,1)} %get-tuple-element.92), kind=kOutput, calls=%fused_computation.31 | convolution fusion | flops 6445596672 | bytes 13631488 | tf_op jit(solution)/shard_map/td,te->de/dot_general | solution.py:21
  494.1 7.4 collective-permute-start.16
  507.5 10.8 %add_convert_fusion.1 = bf16[1536,2048]{1,0:T(8,128)(2,1)} fusion(bf16[1536,2048]{1,0:T(8,128)(2,1)} %collective-permute-done.46, bf16[1024,1536]{1,0:T(8,128)(2,1)S(1)} %copy-done.9, bf16[1024,2048]{1,0:T(8,128)(2,1)S(1)} %copy-done.39), kind=kOutput, calls=%fused_computation.12 | convolution fusion | flops 6451888128 | bytes 19922944 | tf_op jit(solution)/shard_map/td,te->de/dot_general | solution.py:21
  522.2 11.2 %convolution_convert_fusion.3 = bf16[1536,2048]{1,0:T(8,128)(2,1)} fusion(bf16[1024,1536]{1,0:T(8,128)(2,1)S(1)} %copy-done.13, bf16[1024,2048]{1,0:T(8,128)(2,1)} %get-tuple-element.91), kind=kOutput, calls=%fused_computation.32 | convolution fusion | flops 6445596672 | bytes 13631488 | tf_op jit(solution)/shard_map/td,te->de/dot_general | solution.py:21
  542.1 10.4 %collective-permute-done.24 = bf16[256,1536]{1,0:T(8,128)(2,1)S(1)} collective-permute-done((bf16[256,1536]{1,0:T(8,128)(2,1)S(1)}, bf16[256,1536]{1,0:T(8,128)(2,1)S(1)}, u32[]{:S(2)}, u32[]{:S(2)}) %collective-permute-start.24) | collective-permute-done | bytes 786464 | tf_op jit(solution)/shard_map/ppermute | solution.py:164
  559.7 5.7 collective-permute-start.29
  586.2 5.5 collective-permute-start.18
  593.1 10.0 %collective-permute-done.28 = bf16[256,1536]{1,0:T(8,128)(2,1)} collective-permute-done((bf16[256,1536]{1,0:T(8,128)(2,1)}, bf16[256,1536]{1,0:T(8,128)(2,1)}, u32[]{:S(2)}, u32[]{:S(2)}) %collective-permute-start.28) | collective-permute-done | bytes 786464 | tf_op jit(solution)/shard_map/ppermute | solution.py:164
  604.7 9.9 %collective-permute-start.34 = (bf16[256,1536]{1,0:T(8,128)(2,1)S(1)}, bf16[256,1536]{1,0:T(8,128)(2,1)S(1)}, u32[]{:S(2)}, u32[]{:S(2)}) collective-permute-start(bf16[256,1536]{1,0:T(8,128)(2,1)S(1)} %add_convert_fusion.15), channel_id=1, source_target_pairs={{0,8},{8,16},{16,24},{1,9},{9,17},{17,25},{2,10},{10,18},{18,26},{... | collective-permute-start | bytes 2359304 | tf_op jit(solution)/shard_map/ppermute | solution.py:164
  622.2 30.7 %collective-permute-done.34 = bf16[256,1536]{1,0:T(8,128)(2,1)S(1)} collective-permute-done((bf16[256,1536]{1,0:T(8,128)(2,1)S(1)}, bf16[256,1536]{1,0:T(8,128)(2,1)S(1)}, u32[]{:S(2)}, u32[]{:S(2)}) %collective-permute-start.34) | collective-permute-done | bytes 786464 | tf_op jit(solution)/shard_map/ppermute | solution.py:164
  652.9 5.5 collective-permute-start.32
  662.1 10.6 %add_convert_fusion.2 = bf16[1536,2048]{1,0:T(8,128)(2,1)} fusion(bf16[1536,2048]{1,0:T(8,128)(2,1)} %collective-permute-done.45, bf16[1024,1536]{1,0:T(8,128)(2,1)S(1)} %copy-done.10, bf16[1024,2048]{1,0:T(8,128)(2,1)S(1)} %copy-done.37), kind=kOutput, calls=%fused_computation.13 | convolution fusion | flops 6451888128 | bytes 19922944 | tf_op jit(solution)/shard_map/td,te->de/dot_general | solution.py:21
  695.5 10.1 %all-gather.1 = f32[64,512]{1,0:T(8,128)S(1)} all-gather(f32[8,512]{1,0:T(8,128)S(1)} %pad_maximum_fusion.5), channel_id=3, replica_groups=mesh['tp'=4,'fsdp'=8] {'fsdp'}, dimensions={0}, use_global_device_ids=true | all-gather | bytes 147456 | tf_op jit(solution)/shard_map/all_gather | solution.py:310
  705.7 6.4 collective-permute-start.42
  712.1 12.7 %collective-permute-done.42 = f32[384]{0:T(512)S(1)} collective-permute-done((f32[384]{0:T(512)S(1)}, f32[384]{0:T(512)S(1)}, u32[]{:S(2)}, u32[]{:S(2)}) %collective-permute-start.42) | collective-permute-done | bytes 1568 | tf_op jit(solution)/shard_map/ppermute | solution.py:316
  724.8 36.2 %collective-permute-start.43 = (f32[384]{0:T(512)S(1)}, f32[384]{0:T(512)S(1)}, u32[]{:S(2)}, u32[]{:S(2)}) collective-permute-start(f32[384]{0:T(512)S(1)} %bitcast.174), channel_id=1, source_target_pairs={{0,16},{8,24},{16,0},{24,8},{1,17},{9,25},{17,1},{25,9},{2,18},{10... | collective-permute-start | bytes 4616 | tf_op jit(solution)/shard_map/ppermute | solution.py:316
  780.6 49.0 %collective-permute-done.44 = f32[384]{0:T(512)S(1)} collective-permute-done((f32[384]{0:T(512)S(1)}, f32[384]{0:T(512)S(1)}, u32[]{:S(2)}, u32[]{:S(2)}) %collective-permute-start.44) | collective-permute-done | bytes 1568 | tf_op jit(solution)/shard_map/ppermute | solution.py:316
  848.6 22.6 %collective-permute-done.39 = bf16[256,3072]{1,0:T(8,128)(2,1)S(1)} collective-permute-done((bf16[256,3072]{1,0:T(8,128)(2,1)}, bf16[256,3072]{1,0:T(8,128)(2,1)S(1)}, u32[]{:S(2)}, u32[]{:S(2)}) %collective-permute-start.39) | collective-permute-done | bytes 1572896 | tf_op jit(solution)/shard_map/ppermute | solution.py:176
  (318 shorter events, 208.5 us)
Async XLA Ops:
  7.2 78.8 %all-gather.8.cloned.1.call-start = ((), (), s32[]{:S(2)}) async-start(), calls=%async_computation.5 | async-start | bytes 7864320 | tf_op jit(solution)/shard_map/all_gather | solution.py:133
  13.2 156.8 %all-gather.10.cloned.1.call-start = ((), (), s32[]{:S(2)}) async-start(), calls=%async_computation.6 | async-start | bytes 7864320 | tf_op jit(solution)/shard_map/all_gather | solution.py:133
  13.9 215.8 %all-gather.12.cloned.1.call-start = ((), (), s32[]{:S(2)}) async-start(), calls=%async_computation.7 | async-start | bytes 7864320 | tf_op jit(solution)/shard_map/all_gather | solution.py:133
  14.7 294.3 %all-gather.14.cloned.1.call-start = ((), (), s32[]{:S(2)}) async-start(), calls=%async_computation.8 | async-start | bytes 7864320 | tf_op jit(solution)/shard_map/all_gather | solution.py:133
  86.0 29.2 %collective-permute-start = (bf16[1536,2048]{0,1:T(8,128)(2,1)}, bf16[1536,2048]{0,1:T(8,128)(2,1)}, u32[]{:S(2)}, u32[]{:S(2)}) collective-permute-start(bf16[1536,2048]{0,1:T(8,128)(2,1)} %all-gather.8.cloned.1.call-done), channel_id=1, source_target_pairs={{0,1},{1,0},{2,3},{3,2},{4,5},{5,4},{6,7},{7,6},{8,9},{9,8},{10,11... | collective-permute-start | bytes 18874376 | tf_op jit(solution)/shard_map/ppermute | solution.py:137
  229.8 33.9 %collective-permute-start.3 = (bf16[1536,2048]{1,0:T(8,128)(2,1)}, bf16[1536,2048]{1,0:T(8,128)(2,1)}, u32[]{:S(2)}, u32[]{:S(2)}) collective-permute-start(bf16[1536,2048]{1,0:T(8,128)(2,1)} %all-gather.12.cloned.1.call-done), channel_id=1, source_target_pairs={{0,1},{1,0},{2,3},{3,2},{4,5},{5,4},{6,7},{7,6},{8,9},{9,8},{10,11... | collective-permute-start | bytes 18874376 | tf_op jit(solution)/shard_map/ppermute | solution.py:137
  238.9 532.6 %reduce-scatter.8.cloned.1.call-start = ((), (), s32[]{:S(2)}) async-start(), calls=%async_computation.10 | async-start | bytes 2949120 | tf_op jit(solution)/shard_map/reduce_scatter | solution.py:243
  309.0 462.5 %reduce-scatter.6.cloned.1.call-start = ((), (), s32[]{:S(2)}) async-start(), calls=%async_computation.9 | async-start | bytes 4915200 | tf_op jit(solution)/shard_map/reduce_scatter | solution.py:243
  322.0 50.9 %collective-permute-start.5 = (bf16[256,1536]{1,0:T(8,128)(2,1)S(1)}, bf16[256,1536]{1,0:T(8,128)(2,1)}, u32[]{:S(2)}, u32[]{:S(2)}) collective-permute-start(bf16[256,1536]{1,0:T(8,128)(2,1)S(1)} %get-tuple-element.198), channel_id=1, source_target_pairs={{0,8},{1,9},{2,10},{3,11},{4,12},{5,13},{6,14},{7,15}} | collective-permute-start | bytes 2359304 | tf_op jit(solution)/shard_map/ppermute | solution.py:164
  326.3 46.7 %collective-permute-start.8 = (bf16[256,1536]{1,0:T(8,128)(2,1)S(1)}, bf16[256,1536]{1,0:T(8,128)(2,1)}, u32[]{:S(2)}, u32[]{:S(2)}) collective-permute-start(bf16[256,1536]{1,0:T(8,128)(2,1)S(1)} %get-tuple-element.197), channel_id=1, source_target_pairs={{24,16},{25,17},{26,18},{27,19},{28,20},{29,21},{30,22},{31,23}} | collective-permute-start | bytes 2359304 | tf_op jit(solution)/shard_map/ppermute | solution.py:165
  339.9 33.0 %collective-permute-start.7 = (bf16[256,1536]{1,0:T(8,128)(2,1)}, bf16[256,1536]{1,0:T(8,128)(2,1)}, u32[]{:S(2)}, u32[]{:S(2)}) collective-permute-start(bf16[256,1536]{1,0:T(8,128)(2,1)} %get-tuple-element.196), channel_id=1, source_target_pairs={{0,8},{1,9},{2,10},{3,11},{4,12},{5,13},{6,14},{7,15}} | collective-permute-start | bytes 2359304 | tf_op jit(solution)/shard_map/ppermute | solution.py:164
  342.4 30.6 %collective-permute-start.9 = (bf16[256,1536]{1,0:T(8,128)(2,1)}, bf16[256,1536]{1,0:T(8,128)(2,1)}, u32[]{:S(2)}, u32[]{:S(2)}) collective-permute-start(bf16[256,1536]{1,0:T(8,128)(2,1)} %get-tuple-element.195), channel_id=1, source_target_pairs={{24,16},{25,17},{26,18},{27,19},{28,20},{29,21},{30,22},{31,23}} | collective-permute-start | bytes 2359304 | tf_op jit(solution)/shard_map/ppermute | solution.py:165
  374.8 28.5 %collective-permute-start.11 = (bf16[256,1536]{1,0:T(8,128)(2,1)S(1)}, bf16[256,1536]{1,0:T(8,128)(2,1)S(1)}, u32[]{:S(2)}, u32[]{:S(2)}) collective-permute-start(bf16[256,1536]{1,0:T(8,128)(2,1)S(1)} %get-tuple-element.192), channel_id=1, source_target_pairs={{0,8},{8,16},{1,9},{9,17},{2,10},{10,18},{3,11},{11,19},{4,12},{12... | collective-permute-start | bytes 2359304 | tf_op jit(solution)/shard_map/ppermute | solution.py:164
  376.2 27.2 %collective-permute-start.13 = (bf16[256,1536]{1,0:T(8,128)(2,1)S(1)}, bf16[256,1536]{1,0:T(8,128)(2,1)S(1)}, u32[]{:S(2)}, u32[]{:S(2)}) collective-permute-start(bf16[256,1536]{1,0:T(8,128)(2,1)S(1)} %get-tuple-element.191), channel_id=1, source_target_pairs={{24,16},{16,8},{25,17},{17,9},{26,18},{18,10},{27,19},{19,11},{28,... | collective-permute-start | bytes 2359304 | tf_op jit(solution)/shard_map/ppermute | solution.py:165
  378.6 31.8 %collective-permute-start.10 = (bf16[256,1536]{1,0:T(8,128)(2,1)S(1)}, bf16[256,1536]{1,0:T(8,128)(2,1)S(1)}, u32[]{:S(2)}, u32[]{:S(2)}) collective-permute-start(bf16[256,1536]{1,0:T(8,128)(2,1)S(1)} %get-tuple-element.194), channel_id=1, source_target_pairs={{0,8},{8,16},{1,9},{9,17},{2,10},{10,18},{3,11},{11,19},{4,12},{12... | collective-permute-start | bytes 2359304 | tf_op jit(solution)/shard_map/ppermute | solution.py:164
  381.1 29.3 %collective-permute-start.12 = (bf16[256,1536]{1,0:T(8,128)(2,1)S(1)}, bf16[256,1536]{1,0:T(8,128)(2,1)S(1)}, u32[]{:S(2)}, u32[]{:S(2)}) collective-permute-start(bf16[256,1536]{1,0:T(8,128)(2,1)S(1)} %get-tuple-element.193), channel_id=1, source_target_pairs={{24,16},{16,8},{25,17},{17,9},{26,18},{18,10},{27,19},{19,11},{28,... | collective-permute-start | bytes 2359304 | tf_op jit(solution)/shard_map/ppermute | solution.py:165
  453.4 424.4 %reduce-scatter.14.cloned.1.call-start = ((), (), s32[]{:S(2)}) async-start(), calls=%async_computation.13 | async-start | bytes 7864320 | tf_op jit(solution)/shard_map/reduce_scatter | solution.py:243
  475.7 404.7 %reduce-scatter.12.cloned.1.call-start = ((), (), s32[]{:S(2)}) async-start(), calls=%async_computation.12 | async-start | bytes 7864320 | tf_op jit(solution)/shard_map/reduce_scatter | solution.py:243
  494.1 65.6 %collective-permute-start.16 = (bf16[256,1536]{1,0:T(8,128)(2,1)}, bf16[256,1536]{1,0:T(8,128)(2,1)}, u32[]{:S(2)}, u32[]{:S(2)}) collective-permute-start(bf16[256,1536]{1,0:T(8,128)(2,1)} %add_convert_fusion.19), channel_id=1, source_target_pairs={{0,8},{8,16},{16,24},{1,9},{9,17},{17,25},{2,10},{10,18},{18,26},{... | collective-permute-start | bytes 2359304 | tf_op jit(solution)/shard_map/ppermute | solution.py:164
  502.7 33.0 %collective-permute-start.25 = (bf16[256,1536]{1,0:T(8,128)(2,1)}, bf16[256,1536]{1,0:T(8,128)(2,1)}, u32[]{:S(2)}, u32[]{:S(2)}) collective-permute-start(bf16[256,1536]{1,0:T(8,128)(2,1)} %get-tuple-element.188), channel_id=1, source_target_pairs={{0,8},{1,9},{2,10},{3,11},{4,12},{5,13},{6,14},{7,15}} | collective-permute-start | bytes 2359304 | tf_op jit(solution)/shard_map/ppermute | solution.py:164
  505.9 31.1 %collective-permute-start.27 = (bf16[256,1536]{1,0:T(8,128)(2,1)}, bf16[256,1536]{1,0:T(8,128)(2,1)}, u32[]{:S(2)}, u32[]{:S(2)}) collective-permute-start(bf16[256,1536]{1,0:T(8,128)(2,1)} %get-tuple-element.187), channel_id=1, source_target_pairs={{24,16},{25,17},{26,18},{27,19},{28,20},{29,21},{30,22},{31,23}} | collective-permute-start | bytes 2359304 | tf_op jit(solution)/shard_map/ppermute | solution.py:165
  518.3 362.1 %reduce-scatter.10.cloned.1.call-start = ((), (), s32[]{:S(2)}) async-start(), calls=%async_computation.11 | async-start | bytes 7864320 | tf_op jit(solution)/shard_map/reduce_scatter | solution.py:243
  520.0 32.4 %collective-permute-start.24 = (bf16[256,1536]{1,0:T(8,128)(2,1)S(1)}, bf16[256,1536]{1,0:T(8,128)(2,1)S(1)}, u32[]{:S(2)}, u32[]{:S(2)}) collective-permute-start(bf16[256,1536]{1,0:T(8,128)(2,1)S(1)} %get-tuple-element.190), channel_id=1, source_target_pairs={{0,8},{1,9},{2,10},{3,11},{4,12},{5,13},{6,14},{7,15}} | collective-permute-start | bytes 2359304 | tf_op jit(solution)/shard_map/ppermute | solution.py:164
  521.4 32.3 %collective-permute-start.26 = (bf16[256,1536]{1,0:T(8,128)(2,1)S(1)}, bf16[256,1536]{1,0:T(8,128)(2,1)S(1)}, u32[]{:S(2)}, u32[]{:S(2)}) collective-permute-start(bf16[256,1536]{1,0:T(8,128)(2,1)S(1)} %get-tuple-element.189), channel_id=1, source_target_pairs={{24,16},{25,17},{26,18},{27,19},{28,20},{29,21},{30,22},{31,23}} | collective-permute-start | bytes 2359304 | tf_op jit(solution)/shard_map/ppermute | solution.py:165
  535.7 29.8 %collective-permute-start.17 = (bf16[256,1536]{1,0:T(8,128)(2,1)S(1)}, bf16[256,1536]{1,0:T(8,128)(2,1)S(1)}, u32[]{:S(2)}, u32[]{:S(2)}) collective-permute-start(bf16[256,1536]{1,0:T(8,128)(2,1)S(1)} %copy-done.28), channel_id=1, source_target_pairs={{24,16},{16,8},{8,0},{25,17},{17,9},{9,1},{26,18},{18,10},{10,2},{... | collective-permute-start | bytes 2359304 | tf_op jit(solution)/shard_map/ppermute | solution.py:165
  537.0 32.3 %collective-permute-start.14 = (bf16[256,1536]{1,0:T(8,128)(2,1)S(1)}, bf16[256,1536]{1,0:T(8,128)(2,1)S(1)}, u32[]{:S(2)}, u32[]{:S(2)}) collective-permute-start(bf16[256,1536]{1,0:T(8,128)(2,1)S(1)} %copy-done.27), channel_id=1, source_target_pairs={{0,8},{8,16},{16,24},{1,9},{9,17},{17,25},{2,10},{10,18},{18,26},{... | collective-permute-start | bytes 2359304 | tf_op jit(solution)/shard_map/ppermute | solution.py:164
  552.4 22.2 %collective-permute-start.15 = (bf16[256,1536]{1,0:T(8,128)(2,1)S(1)}, bf16[256,1536]{1,0:T(8,128)(2,1)S(1)}, u32[]{:S(2)}, u32[]{:S(2)}) collective-permute-start(bf16[256,1536]{1,0:T(8,128)(2,1)S(1)} %copy-done.26), channel_id=1, source_target_pairs={{24,16},{16,8},{8,0},{25,17},{17,9},{9,1},{26,18},{18,10},{10,2},{... | collective-permute-start | bytes 2359304 | tf_op jit(solution)/shard_map/ppermute | solution.py:165
  553.7 108.3 %collective-permute-start.45 = (bf16[1536,2048]{1,0:T(8,128)(2,1)}, bf16[1536,2048]{1,0:T(8,128)(2,1)}, u32[]{:S(2)}, u32[]{:S(2)}) collective-permute-start(bf16[1536,2048]{1,0:T(8,128)(2,1)} %convolution_convert_fusion.3), channel_id=1, source_target_pairs={{0,1},{1,0},{2,3},{3,2},{4,5},{5,4},{6,7},{7,6},{8,9},{9,8},{10,11... | collective-permute-start | bytes 18874376 | tf_op jit(solution)/shard_map/ppermute | solution.py:239
  559.7 26.5 %collective-permute-start.29 = (bf16[256,1536]{1,0:T(8,128)(2,1)}, bf16[256,1536]{1,0:T(8,128)(2,1)}, u32[]{:S(2)}, u32[]{:S(2)}) collective-permute-start(bf16[256,1536]{1,0:T(8,128)(2,1)} %get-tuple-element.184), channel_id=1, source_target_pairs={{0,8},{8,16},{1,9},{9,17},{2,10},{10,18},{3,11},{11,19},{4,12},{12... | collective-permute-start | bytes 2359304 | tf_op jit(solution)/shard_map/ppermute | solution.py:164
  565.5 26.3 %collective-permute-start.31 = (bf16[256,1536]{1,0:T(8,128)(2,1)}, bf16[256,1536]{1,0:T(8,128)(2,1)}, u32[]{:S(2)}, u32[]{:S(2)}) collective-permute-start(bf16[256,1536]{1,0:T(8,128)(2,1)} %get-tuple-element.183), channel_id=1, source_target_pairs={{24,16},{16,8},{25,17},{17,9},{26,18},{18,10},{27,19},{19,11},{28,... | collective-permute-start | bytes 2359304 | tf_op jit(solution)/shard_map/ppermute | solution.py:165
  569.3 33.8 %collective-permute-start.28 = (bf16[256,1536]{1,0:T(8,128)(2,1)}, bf16[256,1536]{1,0:T(8,128)(2,1)}, u32[]{:S(2)}, u32[]{:S(2)}) collective-permute-start(bf16[256,1536]{1,0:T(8,128)(2,1)} %get-tuple-element.186), channel_id=1, source_target_pairs={{0,8},{8,16},{1,9},{9,17},{2,10},{10,18},{3,11},{11,19},{4,12},{12... | collective-permute-start | bytes 2359304 | tf_op jit(solution)/shard_map/ppermute | solution.py:164
  574.6 28.5 %collective-permute-start.30 = (bf16[256,1536]{1,0:T(8,128)(2,1)}, bf16[256,1536]{1,0:T(8,128)(2,1)}, u32[]{:S(2)}, u32[]{:S(2)}) collective-permute-start(bf16[256,1536]{1,0:T(8,128)(2,1)} %get-tuple-element.185), channel_id=1, source_target_pairs={{24,16},{16,8},{25,17},{17,9},{26,18},{18,10},{27,19},{19,11},{28,... | collective-permute-start | bytes 2359304 | tf_op jit(solution)/shard_map/ppermute | solution.py:165
  586.2 107.3 %collective-permute-start.18 = (bf16[256,3072]{1,0:T(8,128)(2,1)}, bf16[256,3072]{1,0:T(8,128)(2,1)}, u32[]{:S(2)}, u32[]{:S(2)}) collective-permute-start(bf16[256,3072]{1,0:T(8,128)(2,1)} %add_convert_fusion.12), channel_id=1, source_target_pairs={{0,8},{8,16},{16,24},{1,9},{9,17},{17,25},{2,10},{10,18},{18,26},{... | collective-permute-start | bytes 4718600 | tf_op jit(solution)/shard_map/ppermute | solution.py:175
  591.8 100.4 %collective-permute-start.19 = (bf16[256,3072]{1,0:T(8,128)(2,1)}, bf16[256,3072]{1,0:T(8,128)(2,1)}, u32[]{:S(2)}, u32[]{:S(2)}) collective-permute-start(bf16[256,3072]{1,0:T(8,128)(2,1)} %add_convert_fusion.12), channel_id=1, source_target_pairs={{24,16},{16,8},{8,0},{25,17},{17,9},{9,1},{26,18},{18,10},{10,2},{... | collective-permute-start | bytes 4718600 | tf_op jit(solution)/shard_map/ppermute | solution.py:176
  604.7 48.2 %collective-permute-start.34 = (bf16[256,1536]{1,0:T(8,128)(2,1)S(1)}, bf16[256,1536]{1,0:T(8,128)(2,1)S(1)}, u32[]{:S(2)}, u32[]{:S(2)}) collective-permute-start(bf16[256,1536]{1,0:T(8,128)(2,1)S(1)} %add_convert_fusion.15), channel_id=1, source_target_pairs={{0,8},{8,16},{16,24},{1,9},{9,17},{17,25},{2,10},{10,18},{18,26},{... | collective-permute-start | bytes 2359304 | tf_op jit(solution)/shard_map/ppermute | solution.py:164
  616.1 42.3 %collective-permute-start.35 = (bf16[256,1536]{1,0:T(8,128)(2,1)S(1)}, bf16[256,1536]{1,0:T(8,128)(2,1)S(1)}, u32[]{:S(2)}, u32[]{:S(2)}) collective-permute-start(bf16[256,1536]{1,0:T(8,128)(2,1)S(1)} %add_convert_fusion.14), channel_id=1, source_target_pairs={{24,16},{16,8},{8,0},{25,17},{17,9},{9,1},{26,18},{18,10},{10,2},{... | collective-permute-start | bytes 2359304 | tf_op jit(solution)/shard_map/ppermute | solution.py:165
  652.9 21.1 %collective-permute-start.32 = (bf16[256,1536]{1,0:T(8,128)(2,1)}, bf16[256,1536]{1,0:T(8,128)(2,1)}, u32[]{:S(2)}, u32[]{:S(2)}) collective-permute-start(bf16[256,1536]{1,0:T(8,128)(2,1)} %add_convert_fusion.17), channel_id=1, source_target_pairs={{0,8},{8,16},{16,24},{1,9},{9,17},{17,25},{2,10},{10,18},{18,26},{... | collective-permute-start | bytes 2359304 | tf_op jit(solution)/shard_map/ppermute | solution.py:164
  686.3 74.7 %collective-permute-start.37 = (bf16[256,3072]{1,0:T(8,128)(2,1)}, bf16[256,3072]{1,0:T(8,128)(2,1)S(1)}, u32[]{:S(2)}, u32[]{:S(2)}) collective-permute-start(bf16[256,3072]{1,0:T(8,128)(2,1)} %fusion.28), channel_id=1, source_target_pairs={{24,16},{16,8},{8,0},{25,17},{17,9},{9,1},{26,18},{18,10},{10,2},{... | collective-permute-start | bytes 4718600 | tf_op jit(solution)/shard_map/ppermute | solution.py:176
  687.6 74.7 %collective-permute-start.36 = (bf16[256,3072]{1,0:T(8,128)(2,1)}, bf16[256,3072]{1,0:T(8,128)(2,1)S(1)}, u32[]{:S(2)}, u32[]{:S(2)}) collective-permute-start(bf16[256,3072]{1,0:T(8,128)(2,1)} %fusion.28), channel_id=1, source_target_pairs={{0,8},{8,16},{16,24},{1,9},{9,17},{17,25},{2,10},{10,18},{18,26},{... | collective-permute-start | bytes 4718600 | tf_op jit(solution)/shard_map/ppermute | solution.py:175
  692.2 71.9 %collective-permute-start.20 = (bf16[256,3072]{1,0:T(8,128)(2,1)}, bf16[256,3072]{1,0:T(8,128)(2,1)}, u32[]{:S(2)}, u32[]{:S(2)}) collective-permute-start(bf16[256,3072]{1,0:T(8,128)(2,1)} %collective-permute-done.19), channel_id=1, source_target_pairs={{16,8},{8,0},{17,9},{9,1},{18,10},{10,2},{19,11},{11,3},{20,12},{1... | collective-permute-start | bytes 4718600 | tf_op jit(solution)/shard_map/ppermute | solution.py:176
  693.5 136.6 %collective-permute-start.22 = (bf16[256,3072]{1,0:T(8,128)(2,1)}, bf16[256,3072]{1,0:T(8,128)(2,1)}, u32[]{:S(2)}, u32[]{:S(2)}) collective-permute-start(bf16[256,3072]{1,0:T(8,128)(2,1)} %collective-permute-done.18), channel_id=1, source_target_pairs={{8,16},{16,24},{9,17},{17,25},{10,18},{18,26},{11,19},{19,27},{12,... | collective-permute-start | bytes 4718600 | tf_op jit(solution)/shard_map/ppermute | solution.py:175
  724.8 46.7 %collective-permute-start.43 = (f32[384]{0:T(512)S(1)}, f32[384]{0:T(512)S(1)}, u32[]{:S(2)}, u32[]{:S(2)}) collective-permute-start(f32[384]{0:T(512)S(1)} %bitcast.174), channel_id=1, source_target_pairs={{0,16},{8,24},{16,0},{24,8},{1,17},{9,25},{17,1},{25,9},{2,18},{10... | collective-permute-start | bytes 4616 | tf_op jit(solution)/shard_map/ppermute | solution.py:316
  761.0 76.1 %collective-permute-start.38 = (bf16[256,3072]{1,0:T(8,128)(2,1)S(1)}, bf16[256,3072]{1,0:T(8,128)(2,1)}, u32[]{:S(2)}, u32[]{:S(2)}) collective-permute-start(bf16[256,3072]{1,0:T(8,128)(2,1)S(1)} %collective-permute-done.37), channel_id=1, source_target_pairs={{16,8},{8,0},{17,9},{9,1},{18,10},{10,2},{19,11},{11,3},{20,12},{1... | collective-permute-start | bytes 4718600 | tf_op jit(solution)/shard_map/ppermute | solution.py:176
  762.3 76.1 %collective-permute-start.40 = (bf16[256,3072]{1,0:T(8,128)(2,1)S(1)}, bf16[256,3072]{1,0:T(8,128)(2,1)}, u32[]{:S(2)}, u32[]{:S(2)}) collective-permute-start(bf16[256,3072]{1,0:T(8,128)(2,1)S(1)} %collective-permute-done.36), channel_id=1, source_target_pairs={{8,16},{16,24},{9,17},{17,25},{10,18},{18,26},{11,19},{19,27},{12,... | collective-permute-start | bytes 4718600 | tf_op jit(solution)/shard_map/ppermute | solution.py:175
  764.1 75.3 %collective-permute-start.21 = (bf16[256,3072]{1,0:T(8,128)(2,1)}, bf16[256,3072]{1,0:T(8,128)(2,1)}, u32[]{:S(2)}, u32[]{:S(2)}) collective-permute-start(bf16[256,3072]{1,0:T(8,128)(2,1)} %collective-permute-done.20), channel_id=1, source_target_pairs={{8,0},{9,1},{10,2},{11,3},{12,4},{13,5},{14,6},{15,7}} | collective-permute-start | bytes 4718600 | tf_op jit(solution)/shard_map/ppermute | solution.py:176
  771.5 58.0 %collective-permute-start.44 = (f32[384]{0:T(512)S(1)}, f32[384]{0:T(512)S(1)}, u32[]{:S(2)}, u32[]{:S(2)}) collective-permute-start(f32[384]{0:T(512)S(1)} %bitcast.175), channel_id=1, source_target_pairs={{0,24},{8,0},{16,8},{24,16},{1,25},{9,1},{17,9},{25,17},{2,26},{10... | collective-permute-start | bytes 4616 | tf_op jit(solution)/shard_map/ppermute | solution.py:316
  837.0 34.1 %collective-permute-start.39 = (bf16[256,3072]{1,0:T(8,128)(2,1)}, bf16[256,3072]{1,0:T(8,128)(2,1)S(1)}, u32[]{:S(2)}, u32[]{:S(2)}) collective-permute-start(bf16[256,3072]{1,0:T(8,128)(2,1)} %collective-permute-done.38), channel_id=1, source_target_pairs={{8,0},{9,1},{10,2},{11,3},{12,4},{13,5},{14,6},{15,7}} | collective-permute-start | bytes 4718600 | tf_op jit(solution)/shard_map/ppermute | solution.py:176
  838.3 37.7 %collective-permute-start.41 = (bf16[256,3072]{1,0:T(8,128)(2,1)}, bf16[256,3072]{1,0:T(8,128)(2,1)S(1)}, u32[]{:S(2)}, u32[]{:S(2)}) collective-permute-start(bf16[256,3072]{1,0:T(8,128)(2,1)} %collective-permute-done.40), channel_id=1, source_target_pairs={{16,24},{17,25},{18,26},{19,27},{20,28},{21,29},{22,30},{23,31}} | collective-permute-start | bytes 4718600 | tf_op jit(solution)/shard_map/ppermute | solution.py:175
  (59 other events, 923.9 us)
Sparse Core Ops, SparseCore 0:
  13.3 72.6 all-gather.7
  87.8 70.0 all-gather.9
  159.7 70.0 all-gather.11
  239.0 69.8 all-gather.13
  311.8 37.3 reduce-scatter.7
  453.5 51.6 reduce-scatter.5
  508.1 70.0 reduce-scatter.13
  581.7 70.0 reduce-scatter.11
  672.8 72.4 reduce-scatter.9
